TPU v7x, 128 devices: a whole 4x4x4 slice. The times are simulated.
128 devices in a mesh: dp: 1, ep: 128 (over z, y, x, core).
Axes of the slice: x: 4, y: 4, z: 4, core: 2. Of those that a mesh axis runs over, the one named last changes fastest.
Arguments:
- x_in: bfloat16 [12288, 512], P(('dp', 'ep'))
- idx_a: int32 [12288, 8], P(('dp', 'ep'))
- idx_b: int32 [12288, 8], P(('dp', 'ep'))
- gate_a: float32 [12288, 8], P(('dp', 'ep'))
- gate_b: float32 [12288, 8], P(('dp', 'ep'))
- dy_out: bfloat16 [12288, 512], P(('dp', 'ep'))
- w1_a: bfloat16 [384, 512, 128], P('ep')
- w3_a: bfloat16 [384, 512, 128], P('ep')
- w2_a: bfloat16 [384, 128, 512], P('ep')
- w1_b: bfloat16 [384, 512, 128], P('ep')
- w3_b: bfloat16 [384, 512, 128], P('ep')
- w2_b: bfloat16 [384, 128, 512], P('ep')
Outputs:
- output 1: bfloat16 [12288, 512], P(('dp', 'ep'))
- output 2: bfloat16 [12288, 512], P(('dp', 'ep'))
- output 3: float32 [384, 512, 128], P(('dp', 'ep'))
- output 4: float32 [384, 512, 128], P(('dp', 'ep'))
- output 5: float32 [384, 128, 512], P(('dp', 'ep'))
- output 6: float32 [384, 512, 128], P(('dp', 'ep'))
- output 7: float32 [384, 512, 128], P(('dp', 'ep'))
- output 8: float32 [384, 128, 512], P(('dp', 'ep'))
- output 9: float32 [12288, 8], P(('dp', 'ep'))
- output 10: float32 [12288, 8], P(('dp', 'ep'))
All inputs are finite; a program needn't handle non-finite values.
Results may differ from a plain program's by a relative error of at most 0.00686.
Values are sent between devices in bfloat16 or wider.
A program may use at most 1 GiB of HBM per device.

v0:
```python
import jax
import jax.numpy as jnp
from jax import lax
from jax.sharding import PartitionSpec as P

CAP_FACTOR = 4


def slot_maps(dev_ids, experts, capacity):
    pair_total = dev_ids.shape[0] * dev_ids.shape[1]
    flat_ids = dev_ids.reshape(-1)
    onehot = (flat_ids[:, None] == jnp.arange(experts, dtype=jnp.int32)[None, :]).astype(jnp.int32)
    pair_slot = jnp.sum(jnp.cumsum(onehot, axis=0) * onehot, axis=1) - 1
    pair_row = flat_ids * capacity + pair_slot
    pair_ids = jnp.arange(pair_total, dtype=jnp.int32)
    row_pair = jnp.full((experts * capacity,), pair_total, jnp.int32).at[pair_row].set(pair_ids)
    return pair_row, row_pair


def send_rows(rows, index, capacity):
    send_buf = jnp.take(rows, index, axis=0, mode="fill", fill_value=0)
    send_buf = send_buf.reshape((index.shape[0] // capacity, capacity) + send_buf.shape[1:])
    return lax.all_to_all(send_buf, "ep", 0, 1, tiled=True)


def send_back(rows):
    back_rows = lax.all_to_all(rows, "ep", 1, 0, tiled=True)
    return back_rows.reshape((back_rows.shape[0] * back_rows.shape[1],) + back_rows.shape[2:])


def expert_forward(u_rows, w_gate, w_up, w_down):
    pre_gate = jnp.einsum("erd,edf->erf", u_rows, w_gate, preferred_element_type=jnp.float32)
    pre_up = jnp.einsum("erd,edf->erf", u_rows, w_up, preferred_element_type=jnp.float32)
    hidden = (jax.nn.silu(pre_gate) * pre_up).astype(jnp.bfloat16)
    out_rows = jnp.einsum("erf,efd->erd", hidden, w_down, preferred_element_type=jnp.float32).astype(jnp.bfloat16)
    return pre_gate, pre_up, hidden, out_rows


def expert_backward(u_rows, dy_rows, gate_rows, w_gate, w_up, w_down):
    pre_gate, pre_up, hidden, out_rows = expert_forward(u_rows, w_gate, w_up, w_down)
    dgate_rows = jnp.einsum("erd,erd->er", dy_rows, out_rows, preferred_element_type=jnp.float32)
    d_out = (gate_rows[:, :, None] * dy_rows).astype(jnp.bfloat16)
    dw_down = jnp.einsum("erf,erd->efd", hidden, d_out, preferred_element_type=jnp.float32)
    d_hidden = jnp.einsum("erd,efd->erf", d_out, w_down, preferred_element_type=jnp.float32)
    gate_sig = jax.nn.sigmoid(pre_gate)
    d_pre_gate = (d_hidden * pre_up * gate_sig * (1.0 + pre_gate * (1.0 - gate_sig))).astype(jnp.bfloat16)
    d_pre_up = (d_hidden * jax.nn.silu(pre_gate)).astype(jnp.bfloat16)
    dw_gate = jnp.einsum("erd,erf->edf", u_rows, d_pre_gate, preferred_element_type=jnp.float32)
    dw_up = jnp.einsum("erd,erf->edf", u_rows, d_pre_up, preferred_element_type=jnp.float32)
    du_rows = (jnp.einsum("erf,edf->erd", d_pre_gate, w_gate, preferred_element_type=jnp.float32) + jnp.einsum("erf,edf->erd", d_pre_up, w_up, preferred_element_type=jnp.float32)).astype(jnp.bfloat16)
    return du_rows, dgate_rows, dw_gate, dw_up, dw_down


def combine(x_rows, gates, back_rows, pair_row):
    tok_dev, top_k = gates.shape
    out_pairs = jnp.take(back_rows, pair_row, axis=0).reshape(tok_dev, top_k, -1)
    branch = jnp.sum(gates[:, :, None] * out_pairs, axis=1)
    return (x_rows.astype(jnp.float32) + branch).astype(jnp.bfloat16)


def layer_backward(dy_rows, u_rows, gates, row_maps, capacity, w_gate, w_up, w_down):
    pair_row, row_pair = row_maps
    tok_dev, top_k = gates.shape
    dy_sent = send_rows(dy_rows, row_pair // top_k, capacity)
    gate_sent = send_rows(gates.reshape(-1), row_pair, capacity)
    u_rows, dy_sent = lax.optimization_barrier((u_rows, dy_sent))
    du_rows, dgate_rows, dw_gate, dw_up, dw_down = expert_backward(u_rows, dy_sent, gate_sent, w_gate, w_up, w_down)
    du_pairs = jnp.take(send_back(du_rows), pair_row, axis=0).reshape(tok_dev, top_k, -1)
    dx_rows = (dy_rows.astype(jnp.float32) + jnp.sum(du_pairs, axis=1, dtype=jnp.float32)).astype(jnp.bfloat16)
    dgate_out = jnp.take(send_back(dgate_rows), pair_row, axis=0).reshape(tok_dev, top_k)
    return dx_rows, dgate_out, (dw_gate, dw_up, dw_down)


def solution(mesh):
    n_group = mesh.shape["ep"]
    tok_spec = P(("dp", "ep"))
    w_spec = P("ep")

    def device_program(x_in, idx_a, idx_b, gate_a, gate_b, dy_out, w1_a, w3_a, w2_a, w1_b, w3_b, w2_b):
        tok_dev, top_k = idx_a.shape
        experts = w1_a.shape[0] * n_group
        capacity = CAP_FACTOR * tok_dev * top_k // experts
        maps_a = slot_maps(idx_a, experts, capacity)
        maps_b = slot_maps(idx_b, experts, capacity)
        u_rows_a = send_rows(x_in, maps_a[1] // top_k, capacity)
        out_a = expert_forward(u_rows_a, w1_a, w3_a, w2_a)[3]
        x_mid = combine(x_in, gate_a, send_back(out_a), maps_a[0])
        u_rows_b = send_rows(x_mid, maps_b[1] // top_k, capacity)
        out_b = expert_forward(u_rows_b, w1_b, w3_b, w2_b)[3]
        x_out = combine(x_mid, gate_b, send_back(out_b), maps_b[0])
        dx_mid, dgate_b, grads_b = layer_backward(dy_out, u_rows_b, gate_b, maps_b, capacity, w1_b, w3_b, w2_b)
        x_again, dx_mid = lax.optimization_barrier((x_in, dx_mid))
        u_again = send_rows(x_again, maps_a[1] // top_k, capacity)
        dx_in, dgate_a, grads_a = layer_backward(dx_mid, u_again, gate_a, maps_a, capacity, w1_a, w3_a, w2_a)
        return (x_out, dx_in) + grads_a + grads_b + (dgate_a, dgate_b)

    return jax.shard_map(device_program, mesh=mesh, in_specs=(tok_spec,) * 6 + (w_spec,) * 6, out_specs=(tok_spec,) * 10, check_vma=False)
```

profile of v0, /device:TPU:1, one launch (start us, length us, event | category | flops | bytes accessed | tf_op | source)
XLA Modules:
  0.0 744.5 jit_solution(4307207660003926060)
XLA Ops:
  7.7 13.3 %gather_fusion = bf16[3072,512]{1,0:T(8,128)(2,1)} fusion(bf16[96,512]{1,0:T(8,128)(2,1)S(1)} %copy-done.2, s32[3072]{0:T(1024)S(1)} %get-tuple-element.69), kind=kCustom, calls=%fused_computation.clone | custom fusion | bytes 6303744 | tf_op jit(solution)/shard_map/jit(_take)/gather | solution.py:21
  24.0 59.7 %all_to_all.214 = bf16[384,8,512]{2,1,0:T(8,128)(2,1)S(1)} all-to-all(bf16[384,8,512]{2,1,0:T(8,128)(2,1)S(1)} %select_bitcast_fusion.4), channel_id=1, replica_groups=mesh['dp'=1,'ep'=128] {'ep'}, dimensions={0} | all-to-all | bytes 6291456 | tf_op jit(solution)/shard_map/all_to_all | solution.py:23
  86.4 5.3 convolution_convert_fusion.1
  91.7 6.6 copy.113
  98.3 5.5 all-to-all-start.1
  109.1 12.6 %gather_fusion.4 = f32[3072]{0:T(1024)S(1)} fusion(f32[768]{0:T(1024)S(1)} %reshape.233, s32[3072]{0:T(1024)S(1)} %get-tuple-element.70), kind=kCustom, calls=%fused_computation.2.clone | custom fusion | bytes 36864 | tf_op jit(solution)/shard_map/jit(_take)/gather | solution.py:21
  122.7 13.3 %gather_fusion.5 = bf16[3072,512]{1,0:T(8,128)(2,1)} fusion(bf16[96,512]{1,0:T(8,128)(2,1)S(1)} %copy-done.3, s32[3072]{0:T(1024)S(1)} %get-tuple-element.71), kind=kCustom, calls=%fused_computation.5.clone | custom fusion | bytes 6303744 | tf_op jit(solution)/shard_map/jit(_take)/gather | solution.py:21
  136.0 26.3 %all-to-all-done.1 = bf16[3,1024,512]{2,0,1:T(4,128)(2,1)} async-done(((bf16[3,1024,512]{2,0,1:T(4,128)(2,1)}), bf16[3,1024,512]{2,0,1:T(4,128)(2,1)}, u32[]{:S(2)}, u32[]{:S(2)}) %all-to-all-start.1) | async-done | bytes 3145760 | tf_op jit(solution)/shard_map/all_to_all | solution.py:27
  162.4 8.4 %all-to-all-start.4 = ((f32[128,3,8]{2,1,0:T(4,128)}), f32[128,3,8]{2,1,0:T(4,128)S(1)}, u32[]{:S(2)}, u32[]{:S(2)}) async-start(f32[128,3,8]{2,1,0:T(4,128)} %all_to_all.171), calls=%async_computation.4 | async-start | bytes 524288 | tf_op jit(solution)/shard_map/all_to_all | solution.py:23
  181.4 13.3 %gather_fusion.2 = bf16[3072,512]{1,0:T(8,128)(2,1)} fusion(bf16[96,512]{1,0:T(8,128)(2,1)S(1)} %add_convert_fusion.5, s32[3072]{0:T(1024)S(1)} %get-tuple-element.71), kind=kCustom, calls=%fused_computation.4.clone | custom fusion | bytes 6303744 | tf_op jit(solution)/shard_map/jit(_take)/gather | solution.py:21
  194.7 5.3 select_bitcast_fusion.2
  200.0 58.1 %all_to_all.215 = bf16[384,8,512]{2,1,0:T(8,128)(2,1)} all-to-all(bf16[384,8,512]{2,1,0:T(8,128)(2,1)} %get-tuple-element.76), channel_id=1, replica_groups=mesh['dp'=1,'ep'=128] {'ep'}, dimensions={0} | all-to-all | bytes 6291456 | tf_op jit(solution)/shard_map/all_to_all | solution.py:23
  258.1 5.8 all-to-all-start.2
  267.9 40.3 %all-to-all-done.2 = bf16[384,8,512]{2,1,0:T(8,128)(2,1)} async-done(((bf16[384,8,512]{2,1,0:T(8,128)(2,1)}), bf16[384,8,512]{2,1,0:T(8,128)(2,1)}, u32[]{:S(2)}, u32[]{:S(2)}) %all-to-all-start.2) | async-done | bytes 3145760 | tf_op jit(solution)/shard_map/all_to_all | solution.py:23
  322.9 7.6 %all-to-all-start.12 = ((f32[3,128,8]{2,0,1:T(4,128)}), f32[3,128,8]{2,0,1:T(4,128)S(1)}, u32[]{:S(2)}, u32[]{:S(2)}) async-start(f32[3,128,8]{2,0,1:T(4,128)} %copy.142), calls=%async_computation.12 | async-start | bytes 524288 | tf_op jit(solution)/shard_map/all_to_all | solution.py:27
  330.5 5.9 convolution_convert_fusion
  336.4 6.5 copy.122
  343.0 10.6 %all-to-all-start.3 = ((bf16[3,1024,512]{2,0,1:T(4,128)(2,1)}), bf16[3,1024,512]{2,0,1:T(4,128)(2,1)}, u32[]{:S(2)}, u32[]{:S(2)}) async-start(bf16[3,1024,512]{2,0,1:T(4,128)(2,1)} %copy.122), calls=%async_computation.3 | async-start | bytes 8388608 | tf_op jit(solution)/shard_map/all_to_all | solution.py:27
  360.3 51.9 %all-to-all-done.3 = bf16[3,1024,512]{2,0,1:T(4,128)(2,1)} async-done(((bf16[3,1024,512]{2,0,1:T(4,128)(2,1)}), bf16[3,1024,512]{2,0,1:T(4,128)(2,1)}, u32[]{:S(2)}, u32[]{:S(2)}) %all-to-all-start.3) | async-done | bytes 3145760 | tf_op jit(solution)/shard_map/all_to_all | solution.py:27
  412.1 8.9 %all-to-all-start.6 = ((bf16[3,1024,512]{2,0,1:T(4,128)(2,1)}), bf16[3,1024,512]{2,0,1:T(4,128)(2,1)}, u32[]{:S(2)}, u32[]{:S(2)}) async-start(bf16[3,1024,512]{2,0,1:T(4,128)(2,1)} %copy.127), calls=%async_computation.6 | async-start | bytes 8388608 | tf_op jit(solution)/shard_map/all_to_all | solution.py:27
  421.1 12.6 %gather_fusion.7 = f32[3072]{0:T(1024)S(1)} fusion(f32[768]{0:T(1024)S(1)} %reshape.236, s32[3072]{0:T(1024)S(1)} %copy-done.21), kind=kCustom, calls=%fused_computation.11.clone | custom fusion | bytes 36864 | tf_op jit(solution)/shard_map/jit(_take)/gather | solution.py:21
  449.9 29.7 %all-to-all-done.6 = bf16[3,1024,512]{2,0,1:T(4,128)(2,1)} async-done(((bf16[3,1024,512]{2,0,1:T(4,128)(2,1)}), bf16[3,1024,512]{2,0,1:T(4,128)(2,1)}, u32[]{:S(2)}, u32[]{:S(2)}) %all-to-all-start.6) | async-done | bytes 3145760 | tf_op jit(solution)/shard_map/all_to_all | solution.py:27
  479.7 6.7 all-to-all-start.7
  498.1 13.3 %gather_fusion.8 = bf16[3072,512]{1,0:T(8,128)(2,1)} fusion(bf16[96,512]{1,0:T(8,128)(2,1)S(1)} %copy-done.2, s32[3072]{0:T(1024)S(1)} %get-tuple-element.69), kind=kCustom, calls=%fused_computation.6.clone | custom fusion | bytes 6303744 | tf_op jit(solution)/shard_map/jit(_take)/gather | solution.py:21
  511.4 13.3 %gather_fusion.9 = bf16[3072,512]{1,0:T(8,128)(2,1)} fusion(bf16[96,512]{1,0:T(8,128)(2,1)S(1)} %get-tuple-element.22, s32[3072]{0:T(1024)S(1)} %get-tuple-element.69), kind=kCustom, calls=%fused_computation.7.clone | custom fusion | bytes 6303744 | tf_op jit(solution)/shard_map/jit(_take)/gather | solution.py:21
  524.7 5.3 select_bitcast_fusion
  530.0 58.3 %all_to_all.216 = bf16[384,8,512]{2,1,0:T(8,128)(2,1)} all-to-all(bf16[384,8,512]{2,1,0:T(8,128)(2,1)} %get-tuple-element.74), channel_id=1, replica_groups=mesh['dp'=1,'ep'=128] {'ep'}, dimensions={0} | all-to-all | bytes 6291456 | tf_op jit(solution)/shard_map/all_to_all | solution.py:23
  588.2 5.4 all-to-all-start.8
  597.7 43.9 %all-to-all-done.8 = bf16[384,8,512]{2,1,0:T(8,128)(2,1)} async-done(((bf16[384,8,512]{2,1,0:T(8,128)(2,1)}), bf16[384,8,512]{2,1,0:T(8,128)(2,1)}, u32[]{:S(2)}, u32[]{:S(2)}) %all-to-all-start.8) | async-done | bytes 3145760 | tf_op jit(solution)/shard_map/all_to_all | solution.py:23
  652.2 5.3 all-to-all-start.11
  668.3 6.2 all-to-all-start.10
  699.3 33.7 %all-to-all-done.10 = bf16[3,1024,512]{2,0,1:T(4,128)(2,1)} async-done(((bf16[3,1024,512]{2,0,1:T(4,128)(2,1)}), bf16[3,1024,512]{2,0,1:T(4,128)(2,1)}, u32[]{:S(2)}, u32[]{:S(2)}) %all-to-all-start.10) | async-done | bytes 3145760 | tf_op jit(solution)/shard_map/all_to_all | solution.py:27
  (190 shorter events, 143.8 us)
Async XLA Ops:
  0.6 318.1 %copy-start = (bf16[3,512,128]{2,1,0:T(8,128)(2,1)S(1)}, bf16[3,512,128]{2,1,0:T(8,128)(2,1)}, u32[]{:S(2)}) copy-start(bf16[3,512,128]{2,1,0:T(8,128)(2,1)} %param.30) | copy-start | bytes 1179652
  2.9 4.8 copy-start.2
  7.1 13.9 %copy-start.22 = (pred[3072]{0:T(1024)(128)(4,1)}, pred[3072]{0:T(1024)(128)(4,1)S(1)}, u32[]{:S(2)}) copy-start(pred[3072]{0:T(1024)(128)(4,1)S(1)} %compare_and_fusion.1) | copy-start | bytes 9220
  24.0 61.4 %copy-start.15 = (bf16[3,512,128]{2,1,0:T(8,128)(2,1)S(1)}, bf16[3,512,128]{2,1,0:T(8,128)(2,1)}, u32[]{:S(2)}) copy-start(bf16[3,512,128]{2,1,0:T(8,128)(2,1)} %param.26) | copy-start | bytes 1179652
  98.3 5.5 copy-start.26
  98.3 6.0 copy-start.30
  98.3 6.1 copy-start.31
  98.3 64.1 %all-to-all-start.1 = ((bf16[3,1024,512]{2,0,1:T(4,128)(2,1)}), bf16[3,1024,512]{2,0,1:T(4,128)(2,1)}, u32[]{:S(2)}, u32[]{:S(2)}) async-start(bf16[3,1024,512]{2,0,1:T(4,128)(2,1)} %copy.113), calls=%async_computation.1 | async-start | bytes 8388608 | tf_op jit(solution)/shard_map/all_to_all | solution.py:27
  136.0 44.8 %copy-start.24 = (pred[768]{0:T(1024)(128)(4,1)}, pred[768]{0:T(1024)(128)(4,1)S(1)}, u32[]{:S(2)}) copy-start(pred[768]{0:T(1024)(128)(4,1)S(1)} %get-tuple-element.60) | copy-start | bytes 2308
  162.4 37.6 %all-to-all-start.4 = ((f32[128,3,8]{2,1,0:T(4,128)}), f32[128,3,8]{2,1,0:T(4,128)S(1)}, u32[]{:S(2)}, u32[]{:S(2)}) async-start(f32[128,3,8]{2,1,0:T(4,128)} %all_to_all.171), calls=%async_computation.4 | async-start | bytes 524288 | tf_op jit(solution)/shard_map/all_to_all | solution.py:23
  258.1 50.1 %all-to-all-start.2 = ((bf16[384,8,512]{2,1,0:T(8,128)(2,1)}), bf16[384,8,512]{2,1,0:T(8,128)(2,1)}, u32[]{:S(2)}, u32[]{:S(2)}) async-start(bf16[384,8,512]{2,1,0:T(8,128)(2,1)} %get-tuple-element.77), calls=%async_computation.2 | async-start | bytes 6291456 | tf_op jit(solution)/shard_map/all_to_all | solution.py:23
  264.1 52.6 %copy-start.28 = (f32[3,1024]{1,0:T(4,128)}, f32[3,1024]{1,0:T(4,128)S(1)}, u32[]{:S(2)}) copy-start(f32[3,1024]{1,0:T(4,128)S(1)} %mul.145) | copy-start | bytes 36868
  310.5 8.2 %copy-start.4 = (bf16[3,128,8,512]{3,2,1,0:T(8,128)(2,1)}, bf16[3,128,8,512]{3,2,1,0:T(8,128)(2,1)S(1)}, u32[]{:S(2)}) copy-start(bf16[3,128,8,512]{3,2,1,0:T(8,128)(2,1)S(1)} %copy.183) | copy-start | bytes 9437188
  320.0 34.6 %copy-start.12 = (bf16[3,1024,128]{2,1,0:T(8,128)(2,1)}, bf16[3,1024,128]{2,1,0:T(8,128)(2,1)S(1)}, u32[]{:S(2)}) copy-start(bf16[3,1024,128]{2,1,0:T(8,128)(2,1)S(1)} %get-tuple-element.67) | copy-start | bytes 2359300
  322.9 20.0 %all-to-all-start.12 = ((f32[3,128,8]{2,0,1:T(4,128)}), f32[3,128,8]{2,0,1:T(4,128)S(1)}, u32[]{:S(2)}, u32[]{:S(2)}) async-start(f32[3,128,8]{2,0,1:T(4,128)} %copy.142), calls=%async_computation.12 | async-start | bytes 524288 | tf_op jit(solution)/shard_map/all_to_all | solution.py:27
  343.0 69.2 %all-to-all-start.3 = ((bf16[3,1024,512]{2,0,1:T(4,128)(2,1)}), bf16[3,1024,512]{2,0,1:T(4,128)(2,1)}, u32[]{:S(2)}, u32[]{:S(2)}) async-start(bf16[3,1024,512]{2,0,1:T(4,128)(2,1)} %copy.122), calls=%async_computation.3 | async-start | bytes 8388608 | tf_op jit(solution)/shard_map/all_to_all | solution.py:27
  360.3 60.8 %copy-start.21 = (s32[3072]{0:T(1024)S(1)}, s32[3072]{0:T(1024)}, u32[]{:S(2)}) copy-start(s32[3072]{0:T(1024)} %get-tuple-element.68) | copy-start | bytes 36868
  412.1 67.5 %all-to-all-start.6 = ((bf16[3,1024,512]{2,0,1:T(4,128)(2,1)}), bf16[3,1024,512]{2,0,1:T(4,128)(2,1)}, u32[]{:S(2)}, u32[]{:S(2)}) async-start(bf16[3,1024,512]{2,0,1:T(4,128)(2,1)} %copy.127), calls=%async_computation.6 | async-start | bytes 8388608 | tf_op jit(solution)/shard_map/all_to_all | solution.py:27
  479.7 50.3 %all-to-all-start.7 = ((f32[128,3,8]{2,1,0:T(4,128)}), f32[128,3,8]{2,1,0:T(4,128)S(1)}, u32[]{:S(2)}, u32[]{:S(2)}) async-start(f32[128,3,8]{2,1,0:T(4,128)} %all_to_all.181), calls=%async_computation.7 | async-start | bytes 524288 | tf_op jit(solution)/shard_map/all_to_all | solution.py:23
  491.3 5.0 copy-start.17
  511.4 13.3 %copy-start.23 = (pred[3072]{0:T(1024)(128)(4,1)S(1)}, pred[3072]{0:T(1024)(128)(4,1)}, u32[]{:S(2)}) copy-start(pred[3072]{0:T(1024)(128)(4,1)} %copy-done.22) | copy-start | bytes 9220
  588.2 53.4 %all-to-all-start.8 = ((bf16[384,8,512]{2,1,0:T(8,128)(2,1)}), bf16[384,8,512]{2,1,0:T(8,128)(2,1)}, u32[]{:S(2)}, u32[]{:S(2)}) async-start(bf16[384,8,512]{2,1,0:T(8,128)(2,1)} %get-tuple-element.75), calls=%async_computation.8 | async-start | bytes 6291456 | tf_op jit(solution)/shard_map/all_to_all | solution.py:23
  643.8 4.1 copy-start.6
  643.8 3.1 copy-start.34
  652.2 16.1 %all-to-all-start.11 = ((f32[3,128,8]{2,0,1:T(4,128)}), f32[3,128,8]{2,0,1:T(4,128)S(1)}, u32[]{:S(2)}, u32[]{:S(2)}) async-start(f32[3,128,8]{2,0,1:T(4,128)} %copy.141), calls=%async_computation.11 | async-start | bytes 524288 | tf_op jit(solution)/shard_map/all_to_all | solution.py:27
  668.3 64.8 %all-to-all-start.10 = ((bf16[3,1024,512]{2,0,1:T(4,128)(2,1)}), bf16[3,1024,512]{2,0,1:T(4,128)(2,1)}, u32[]{:S(2)}, u32[]{:S(2)}) async-start(bf16[3,1024,512]{2,0,1:T(4,128)(2,1)} %copy.133), calls=%async_computation.10 | async-start | bytes 8388608 | tf_op jit(solution)/shard_map/all_to_all | solution.py:27
  674.4 4.1 copy-start.5
  674.5 4.1 copy-start.13
  687.6 4.1 copy-start.10
  687.6 4.1 copy-start.38
  693.9 4.6 copy-start.25
  738.0 6.3 copy-start.1
  (17 other events, 30.4 us)
where the time goes:
time: 755 us; the launch traced here: 744 us
  waiting for transfers between devices  230 us (30%)
  local copies, waits for them, and re-layouts  197 us (26%)
  blocking collectives  176 us (23%)
  starting transfers between devices  70.4 us (9%)
  matrix products  48.7 us (6%)
  other arithmetic  20.5 us (3%)
    all_to_all x3, blocking collectives, send_rows(): return lax.all_to_all(send_buf, 'ep', 0, 1, tiled=True)  176 us
    all_to_all x6, waiting for transfers between devices, send_back(): back_rows = lax.all_to_all(rows, 'ep', 1, 0, tiled=True)  146 us
    gather x7, local copies, waits for them, and re-layouts, send_rows(): send_buf = jnp.take(rows, index, axis=0, mode='fill', fill_value=0)  91.7 us
    all_to_all x4, waiting for transfers between devices, send_rows(): return lax.all_to_all(send_buf, 'ep', 0, 1, tiled=True)  84.2 us
    all_to_all x6, starting transfers between devices, send_back(): back_rows = lax.all_to_all(rows, 'ep', 1, 0, tiled=True)  44.1 us
    all_to_all x4, starting transfers between devices, send_rows(): return lax.all_to_all(send_buf, 'ep', 0, 1, tiled=True)  26.3 us
    all_to_all x8, local copies, waits for them, and re-layouts, send_back(): back_rows = lax.all_to_all(rows, 'ep', 1, 0, tiled=True)  21.8 us
  transfers between devices with their start and end apart: 10, of which 7 were waited for; matrix products, arithmetic and copies ran while one was open for 26% of the time, Pallas kernels for 0%

commit v1 on v0

v1 whole, which is shorter than its diff:
```python
import jax
import jax.numpy as jnp
from jax import lax
from jax.sharding import PartitionSpec as P

CAP_FACTOR = 4
F32 = jnp.float32
BF16 = jnp.bfloat16


def pair_rows(ids, capacity):
    flat = ids.reshape(-1)
    pair = jnp.arange(flat.shape[0], dtype=jnp.int32)
    earlier = (flat[None, :] == flat[:, None]) & (pair[None, :] < pair[:, None])
    slot = jnp.sum(earlier.astype(jnp.int32), axis=1)
    return (flat * capacity + slot).reshape(ids.shape)


def slot_tables(rows, gates, total):
    tok_dev = rows.shape[0]
    hit = rows[:, :, None] == jnp.arange(total, dtype=jnp.int32)[None, None, :]
    token = jnp.sum(jnp.where(hit, jnp.arange(tok_dev, dtype=F32)[:, None, None] - tok_dev, 0.0), axis=(0, 1)) + tok_dev
    gate = jnp.sum(jnp.where(hit, gates[:, :, None], 0.0), axis=(0, 1))
    return token, gate


def pair_weight(rows, gates, total):
    hit = rows[:, :, None] == jnp.arange(total, dtype=jnp.int32)[None, None, :]
    return jnp.sum(jnp.where(hit, gates[:, :, None], 0.0), axis=1)


def split3(w):
    hi = lax.reduce_precision(w, 8, 7)
    mid = lax.reduce_precision(w - hi, 8, 7)
    low = w - hi - mid
    return jnp.concatenate([hi.astype(BF16), mid.astype(BF16), low.astype(BF16)], axis=0)


def pick_rows(all_rows, token, own):
    n_group, tok_dev, width = all_rows.shape
    pick = (token[:, :, None] == jnp.arange(tok_dev, dtype=F32)[None, None, :]).astype(BF16)
    rows = jnp.einsum("srt,std->srd", pick, all_rows, preferred_element_type=F32).astype(BF16)
    rows = rows.reshape(n_group, own, -1, width).transpose(1, 0, 2, 3)
    return rows.reshape(own, -1, width)


def home_order(rows, n_group):
    own, count, width = rows.shape
    rows = rows.reshape(own, n_group, count // n_group, width).transpose(1, 0, 2, 3)
    return rows.reshape(n_group, -1, width)


def expert_forward(u_rows, w_gate, w_up, w_down):
    pre_gate = jnp.einsum("erd,edf->erf", u_rows, w_gate, preferred_element_type=F32)
    pre_up = jnp.einsum("erd,edf->erf", u_rows, w_up, preferred_element_type=F32)
    hidden = (jax.nn.silu(pre_gate) * pre_up).astype(BF16)
    out_rows = jnp.einsum("erf,efd->erd", hidden, w_down, preferred_element_type=F32).astype(BF16)
    return pre_gate, pre_up, hidden, out_rows


def expert_backward(u_rows, dy_rows, gate_rows, w_gate, w_up, w_down):
    pre_gate, pre_up, hidden, out_rows = expert_forward(u_rows, w_gate, w_up, w_down)
    dgate_rows = jnp.einsum("erd,erd->er", dy_rows, out_rows, preferred_element_type=F32)
    d_out = (gate_rows[:, :, None] * dy_rows).astype(BF16)
    dw_down = jnp.einsum("erf,erd->efd", hidden, d_out, preferred_element_type=F32)
    d_hidden = jnp.einsum("erd,efd->erf", d_out, w_down, preferred_element_type=F32)
    gate_sig = jax.nn.sigmoid(pre_gate)
    d_pre_gate = (d_hidden * pre_up * gate_sig * (1.0 + pre_gate * (1.0 - gate_sig))).astype(BF16)
    d_pre_up = (d_hidden * jax.nn.silu(pre_gate)).astype(BF16)
    dw_gate = jnp.einsum("erd,erf->edf", u_rows, d_pre_gate, preferred_element_type=F32)
    dw_up = jnp.einsum("erd,erf->edf", u_rows, d_pre_up, preferred_element_type=F32)
    du_rows = (jnp.einsum("erf,edf->erd", d_pre_gate, w_gate, preferred_element_type=F32) + jnp.einsum("erf,edf->erd", d_pre_up, w_up, preferred_element_type=F32)).astype(BF16)
    return du_rows, dgate_rows, dw_gate, dw_up, dw_down


def solution(mesh):
    n_group = mesh.shape["ep"]
    tok_spec = P(("dp", "ep"))
    w_spec = P("ep")

    def device_program(x_in, idx_a, idx_b, gate_a, gate_b, dy_out, w1_a, w3_a, w2_a, w1_b, w3_b, w2_b):
        tok_dev, top_k = idx_a.shape
        width = x_in.shape[1]
        own = w1_a.shape[0]
        capacity = CAP_FACTOR * tok_dev * top_k // (own * n_group)
        total = own * n_group * capacity
        block = own * capacity

        rows_a = pair_rows(idx_a, capacity)
        rows_b = pair_rows(idx_b, capacity)
        tables = slot_tables(rows_a, gate_a, total) + slot_tables(rows_b, gate_b, total)
        table = jnp.concatenate([t.reshape(n_group, block) for t in tables], axis=1)
        table = lax.all_to_all(table, "ep", 0, 0, tiled=True)
        token_a, far_gate_a, token_b, far_gate_b = jnp.split(table, 4, axis=1)
        weight_a = split3(pair_weight(rows_a, gate_a, total))
        weight_b = split3(pair_weight(rows_b, gate_b, total))
        ones = jnp.ones_like(gate_a)
        pick_a = pair_weight(rows_a, ones, total).astype(BF16)
        pick_b = pair_weight(rows_b, ones, total).astype(BF16)

        def gather(rows):
            return lax.all_gather(rows, "ep", axis=0, tiled=False)

        def send_back(rows):
            back = lax.all_to_all(home_order(rows, n_group), "ep", 0, 0, tiled=True)
            return back.reshape(total, width)

        def combine(x_rows, back, weight):
            branch = jnp.dot(weight, back, preferred_element_type=F32).reshape(3, tok_dev, width)
            branch = branch[0] + (branch[1] + branch[2])
            return (x_rows.astype(F32) + branch).astype(BF16)

        def layer_backward(dy_rows, dy_all, x_all, token, far_gate, pick, w_gate, w_up, w_down):
            gates = far_gate.reshape(n_group, own, capacity).transpose(1, 0, 2).reshape(own, -1)
            u_rows = pick_rows(x_all, token, own)
            dy_sent = pick_rows(dy_all, token, own)
            du_rows, dgate_rows, dw_gate, dw_up, dw_down = expert_backward(u_rows, dy_sent, gates, w_gate, w_up, w_down)
            branch = jnp.dot(pick, send_back(du_rows), preferred_element_type=F32)
            dx_rows = (dy_rows.astype(F32) + branch).astype(BF16)
            return dx_rows, dgate_rows, (dw_gate, dw_up, dw_down)

        def dgate_home(dgate_rows, rows):
            back = lax.all_to_all(home_order(dgate_rows[:, :, None], n_group).reshape(n_group, block), "ep", 0, 0, tiled=True)
            hit = rows[:, :, None] == jnp.arange(total, dtype=jnp.int32)[None, None, :]
            return jnp.sum(jnp.where(hit, back.reshape(1, 1, total), 0.0), axis=2)

        x_all = gather(x_in)
        dy_all_b = gather(dy_out)
        out_a = expert_forward(pick_rows(x_all, token_a, own), w1_a, w3_a, w2_a)[3]
        x_mid = combine(x_in, send_back(out_a), weight_a)
        mid_all = gather(x_mid)
        out_b = expert_forward(pick_rows(mid_all, token_b, own), w1_b, w3_b, w2_b)[3]
        x_out = combine(x_mid, send_back(out_b), weight_b)
        mid_keep, dy_all_b, out_b = lax.optimization_barrier((mid_all, dy_all_b, out_b))
        dx_mid, dgate_rows_b, grads_b = layer_backward(dy_out, dy_all_b, mid_keep, token_b, far_gate_b, pick_b, w1_b, w3_b, w2_b)
        x_again, _ = lax.optimization_barrier((x_in, out_b))
        again_all = gather(x_again)
        dy_all_a = gather(dx_mid)
        dx_in, dgate_rows_a, grads_a = layer_backward(dx_mid, dy_all_a, again_all, token_a, far_gate_a, pick_a, w1_a, w3_a, w2_a)
        dgate_b = dgate_home(dgate_rows_b, rows_b)
        dgate_a = dgate_home(dgate_rows_a, rows_a)
        return (x_out, dx_in) + grads_a + grads_b + (dgate_a, dgate_b)

    return jax.shard_map(device_program, mesh=mesh, in_specs=(tok_spec,) * 6 + (w_spec,) * 6, out_specs=(tok_spec,) * 10, check_vma=False)
```

time: 755 us -> 602 us (0.80)
  local copies, waits for them, and re-layouts: 197 us -> 29.7 us
  blocking collectives: 176 us -> 21.3 us
  waiting for transfers between devices: 230 us -> 351 us
  matrix products: 48.7 us -> 95.3 us
  starting transfers between devices: 70.4 us -> 39.8 us
  other arithmetic: 20.5 us -> 40.5 us
  between operations: 1.67 us -> 14.9 us
    all_gather x0 -> x5, waiting for transfers between devices: none -> 236 us  [gather(): return lax.all_gather(rows, 'ep', axis=0, tiled=False)]
    all_to_all x3 -> x1, blocking collectives: 176 us -> 21.3 us  [device_program(): table = lax.all_to_all(table, 'ep', 0, 0, tiled=True)]
    gather x13 -> x0, local copies, waits for them, and re-layouts: 121 us -> none  [the longest x7 91.7 us: send_rows(): send_buf = jnp.take(rows, index, axis=0, mode='fill', fill_value=0)]
    all_to_all x10 -> x6, waiting for transfers between devices: 230 us -> 114 us  [the longest x4 104 us: send_back(): back = lax.all_to_all(home_order(rows, n_group), 'ep', 0, 0, tiled=True)]
    dot_general x22 -> x32, matrix products: 48.7 us -> 95.3 us  [the longest x6 34.3 us: pick_rows(): jnp.einsum('srt,std->srd', pick, all_rows, preferred_element_type=F32)]
    all_to_all x16 -> x4, local copies, waits for them, and re-layouts: 35.9 us -> 2.1 us  [the longest x3 2 us: dgate_home(): lax.all_to_all(home_order(dgate_rows[:, :, None], n_group).reshape(n_grou...]
    all_to_all x10 -> x6, starting transfers between devices: 70.4 us -> 39.4 us  [the longest x4 24.1 us: send_back(): back = lax.all_to_all(home_order(rows, n_group), 'ep', 0, 0, tiled=True)]
    reduce_sum x5, other arithmetic: 2.81 us -> 30.5 us  [the longest x2 17.9 us: dgate_home(): return jnp.sum(jnp.where(hit, back.reshape(1, 1, total), 0.0), axis=2)]
  transfers between devices with their start and end apart: 10 -> 11, of which waited for: 7 -> 9; matrix products, arithmetic and copies ran while one was open for 26% -> 22% of each run, Pallas kernels for 0% -> 0%
where the time goes in v1:
time: 602 us; the launch traced here: 593 us
  waiting for transfers between devices  351 us (58%)
  matrix products  95.3 us (16%)
  other arithmetic  40.5 us (7%)
  starting transfers between devices  39.8 us (7%)
  local copies, waits for them, and re-layouts  29.7 us (5%)
  blocking collectives  21.3 us (4%)
  between operations  14.9 us (2%)
    all_gather x5, waiting for transfers between devices, gather(): return lax.all_gather(rows, 'ep', axis=0, tiled=False)  236 us
    all_to_all x4, waiting for transfers between devices, send_back(): back = lax.all_to_all(home_order(rows, n_group), 'ep', 0, 0, tiled=True)  104 us
    dot_general x6, matrix products, pick_rows(): jnp.einsum('srt,std->srd', pick, all_rows, preferred_element_type=F32)  34.3 us
    all_to_all x4, starting transfers between devices, send_back(): back = lax.all_to_all(home_order(rows, n_group), 'ep', 0, 0, tiled=True)  24.1 us
    all_to_all x1, blocking collectives, device_program(): table = lax.all_to_all(table, 'ep', 0, 0, tiled=True)  21.3 us
    reduce_sum x2, other arithmetic, dgate_home(): return jnp.sum(jnp.where(hit, back.reshape(1, 1, total), 0.0), axis=2)  17.9 us
    all_to_all x2, starting transfers between devices, dgate_home(): lax.all_to_all(home_order(dgate_rows[:, :, None], n_group).reshape(n_grou...  15.2 us
    unnamed x104, local copies, waits for them, and re-layouts  15.2 us
  transfers between devices with their start and end apart: 11, of which 9 were waited for; matrix products, arithmetic and copies ran while one was open for 22% of the time, Pallas kernels for 0%

profile of v1, /device:TPU:1, one launch (start us, length us, event | category | flops | bytes accessed | tf_op | source)
XLA Modules:
  0.0 593.1 jit_solution(14987712466472946967)
XLA Ops:
  13.9 11.9 %select_reduce_fusion.3 = (f32[96,3072]{1,0:T(8,128)S(1)}, f32[3072]{0:T(1024)S(1)}, f32[3072]{0:T(1024)S(1)}, f32[3072]{0:T(1024)S(1)}, f32[3072]{0:T(1024)S(1)}, /*index=5*/f32[96,3072]{1,0:T(8,128)}) fusion(f32[96,8]{1,0:T(8,128)S(1)} %copy.145, s32[96,8]{1,0:T(8,128)S(1)} %copy.144, f32[96]{0:T(128)S(1)} %iota_add_fusion, f32[96,8]{1,0:T(8,128)S(1)} %copy.149, ...), kind=kLoop, calls=%fused_computation.3 | loop fusion | flops 27709440 | bytes 2421120 | tf_op jit(solution)/shard_map/reduce_sum | solution.py:29
  26.3 21.3 %all_to_all.50 = f32[128,1,96]{2,1,0:T(1,128)S(1)} all-to-all(f32[128,1,96]{2,1,0:T(1,128)S(1)} %bitcast.179), channel_id=1, replica_groups=mesh['dp'=1,'ep'=128] {'ep'}, dimensions={0} | all-to-all | bytes 98304 | tf_op jit(solution)/shard_map/all_to_all | solution.py:93
  47.9 39.6 %all-gather.11.cloned.1.call-done = bf16[12288,512]{1,0:T(8,128)(2,1)} async-done(((bf16[96,512]{1,0:T(8,128)(2,1)}), bf16[12288,512]{1,0:T(8,128)(2,1)}) %all-gather.11.cloned.1.call-update) | async-done | bytes 12582928 | tf_op jit(solution)/shard_map/all_gather | solution.py:102
  87.5 6.4 %convert_bitcast_fusion.6 = bf16[3,128,8,512]{3,2,0,1:T(8,128)(2,1)S(1)} fusion(bf16[128,96,512]{2,1,0:T(8,128)(2,1)} %bitcast.172, f32[128,24]{1,0:T(8,128)S(1)} %copy.152), kind=kOutput, calls=%fused_computation.58 | convolution fusion | flops 303857664 | bytes 15740928 | tf_op jit(solution)/shard_map/srt,std->srd/dot_general | solution.py:42
  97.8 5.8 convert_bitcast_fusion.5
  103.6 3.8 copy.268
  107.4 7.8 %all-to-all-start.1 = ((bf16[128,24,512]{2,1,0:T(8,128)(2,1)}), bf16[128,24,512]{2,1,0:T(8,128)(2,1)}, u32[]{:S(2)}, u32[]{:S(2)}) async-start(bf16[128,24,512]{2,1,0:T(8,128)(2,1)} %bitcast.168), calls=%async_computation.1 | async-start | bytes 6291456 | tf_op jit(solution)/shard_map/all_to_all | solution.py:105
  115.5 47.6 %all-to-all-done.1 = bf16[128,24,512]{2,1,0:T(8,128)(2,1)} async-done(((bf16[128,24,512]{2,1,0:T(8,128)(2,1)}), bf16[128,24,512]{2,1,0:T(8,128)(2,1)}, u32[]{:S(2)}, u32[]{:S(2)}) %all-to-all-start.1) | async-done | bytes 3145760 | tf_op jit(solution)/shard_map/all_to_all | solution.py:105
  163.1 3.0 fusion.52
  168.5 68.4 %all-gather.13.cloned.1.call-done = bf16[12288,512]{1,0:T(8,128)(2,1)} async-done(((bf16[96,512]{1,0:T(8,128)(2,1)}), bf16[12288,512]{1,0:T(8,128)(2,1)}) %all-gather.13.cloned.1.call-update) | async-done | bytes 12582928 | tf_op jit(solution)/shard_map/all_gather | solution.py:102
  236.9 6.4 %convert_bitcast_fusion.4 = bf16[3,128,8,512]{3,2,0,1:T(8,128)(2,1)S(1)} fusion(bf16[128,96,512]{2,1,0:T(8,128)(2,1)} %bitcast.169, f32[128,24]{1,0:T(8,128)S(1)} %copy.155), kind=kOutput, calls=%fused_computation.56 | convolution fusion | flops 303857664 | bytes 15740928 | tf_op jit(solution)/shard_map/srt,std->srd/dot_general | solution.py:42
  246.0 5.3 convolution_convert_fusion
  251.4 60.9 %all-gather.15.cloned.1.call-done = bf16[12288,512]{1,0:T(8,128)(2,1)} async-done(((bf16[96,512]{1,0:T(8,128)(2,1)}), bf16[12288,512]{1,0:T(8,128)(2,1)}) %all-gather.15.cloned.1.call-update) | async-done | bytes 12582928 | tf_op jit(solution)/shard_map/all_gather | solution.py:102
  312.3 6.5 %convert_bitcast_fusion.2 = bf16[128,3,8,512]{3,2,1,0:T(8,128)(2,1)S(1)} fusion(bf16[128,96,512]{2,1,0:T(8,128)(2,1)} %bitcast.170, f32[128,24]{1,0:T(8,128)S(1)} %copy.155), kind=kOutput, calls=%fused_computation.54 | convolution fusion | flops 303857664 | bytes 15740928 | tf_op jit(solution)/shard_map/srt,std->srd/dot_general | solution.py:42
  329.0 7.9 %all-to-all-start.6 = ((f32[128,1,24]{2,1,0:T(1,128)}), f32[128,1,24]{2,1,0:T(1,128)S(1)}, u32[]{:S(2)}, u32[]{:S(2)}) async-start(f32[128,1,24]{2,1,0:T(1,128)} %copy.175), calls=%async_computation.6 | async-start | bytes 131072 | tf_op jit(solution)/shard_map/all_to_all | solution.py:123
  340.7 5.9 %all-to-all-done.6 = f32[128,1,24]{2,1,0:T(1,128)S(1)} async-done(((f32[128,1,24]{2,1,0:T(1,128)}), f32[128,1,24]{2,1,0:T(1,128)S(1)}, u32[]{:S(2)}, u32[]{:S(2)}) %all-to-all-start.6) | async-done | bytes 12320 | tf_op jit(solution)/shard_map/all_to_all | solution.py:123
  347.3 4.5 all-to-all-start.3
  354.1 8.4 %select_reduce_fusion.4 = (f32[96,8]{1,0:T(8,128)}, bf16[96,3072]{1,0:T(8,128)(2,1)}) fusion(f32[3072]{0:T(1024)S(1)} %broadcast_in_dim.109, s32[96,8]{1,0:T(8,128)S(1)} %copy-done.27), kind=kLoop, calls=%fused_computation.4 | loop fusion | flops 11500800 | bytes 608256 | tf_op jit(solution)/shard_map/reduce_sum | solution.py:125
  362.5 44.8 %all-to-all-done.3 = bf16[128,24,512]{2,1,0:T(8,128)(2,1)S(1)} async-done(((bf16[128,24,512]{2,1,0:T(8,128)(2,1)}), bf16[128,24,512]{2,1,0:T(8,128)(2,1)S(1)}, u32[]{:S(2)}, u32[]{:S(2)}) %all-to-all-start.3) | async-done | bytes 3145760 | tf_op jit(solution)/shard_map/all_to_all | solution.py:105
  414.7 6.1 %all-to-all-start.2 = ((bf16[128,24,512]{2,1,0:T(8,128)(2,1)}), bf16[128,24,512]{2,1,0:T(8,128)(2,1)}, u32[]{:S(2)}, u32[]{:S(2)}) async-start(bf16[128,24,512]{2,1,0:T(8,128)(2,1)} %copy_bitcast_fusion.2), calls=%async_computation.2 | async-start | bytes 6291456 | tf_op jit(solution)/shard_map/all_to_all | solution.py:105
  420.9 6.4 %convert_bitcast_fusion = bf16[128,3,8,512]{3,2,1,0:T(8,128)(2,1)S(1)} fusion(bf16[128,96,512]{2,1,0:T(8,128)(2,1)} %bitcast.171, f32[128,24]{1,0:T(8,128)S(1)} %copy-done.4), kind=kOutput, calls=%fused_computation.52 | convolution fusion | flops 303857664 | bytes 15740928 | tf_op jit(solution)/shard_map/srt,std->srd/dot_general | solution.py:42
  429.5 67.1 %all-gather.17.cloned.1.call-done = bf16[12288,512]{1,0:T(8,128)(2,1)} async-done(((bf16[96,512]{1,0:T(8,128)(2,1)}), bf16[12288,512]{1,0:T(8,128)(2,1)}) %all-gather.17.cloned.1.call-update) | async-done | bytes 12582928 | tf_op jit(solution)/shard_map/all_gather | solution.py:102
  496.6 6.4 %convert_bitcast_fusion.1 = bf16[3,128,8,512]{3,2,0,1:T(8,128)(2,1)S(1)} fusion(bf16[128,96,512]{2,1,0:T(8,128)(2,1)} %bitcast.174, f32[128,24]{1,0:T(8,128)S(1)} %copy-done.4), kind=kOutput, calls=%fused_computation.53 | convolution fusion | flops 303857664 | bytes 15740928 | tf_op jit(solution)/shard_map/srt,std->srd/dot_general | solution.py:42
  511.2 3.6 fusion.99
  514.8 7.3 %all-to-all-start.5 = ((f32[128,1,24]{2,1,0:T(1,128)}), f32[128,1,24]{2,1,0:T(1,128)S(1)}, u32[]{:S(2)}, u32[]{:S(2)}) async-start(f32[128,1,24]{2,1,0:T(1,128)} %copy.173), calls=%async_computation.5 | async-start | bytes 131072 | tf_op jit(solution)/shard_map/all_to_all | solution.py:123
  522.1 3.8 fusion.5
  527.8 4.2 all-to-all-done.5
  532.6 5.8 all-to-all-start.4
  538.4 4.3 fusion.14
  547.7 3.6 fusion.58
  561.7 9.5 %select_reduce_fusion.5 = (f32[96,8]{1,0:T(8,128)}, bf16[96,3072]{1,0:T(8,128)(2,1)}) fusion(f32[3072]{0:T(1024)S(1)} %broadcast_in_dim.107, s32[96,8]{1,0:T(8,128)} %copy-done.25), kind=kLoop, calls=%fused_computation.5 | loop fusion | flops 11500800 | bytes 608256 | tf_op jit(solution)/shard_map/reduce_sum | solution.py:125
  572.6 11.2 %all-to-all-done.4 = bf16[128,24,512]{2,1,0:T(8,128)(2,1)S(1)} async-done(((bf16[128,24,512]{2,1,0:T(8,128)(2,1)}), bf16[128,24,512]{2,1,0:T(8,128)(2,1)S(1)}, u32[]{:S(2)}, u32[]{:S(2)}) %all-to-all-start.4) | async-done | bytes 3145760 | tf_op jit(solution)/shard_map/all_to_all | solution.py:105
  (181 shorter events, 72.5 us)
Async XLA Ops:
  7.2 238.8 %copy-start = (bf16[3,512,128]{2,1,0:T(8,128)(2,1)S(1)}, bf16[3,512,128]{2,1,0:T(8,128)(2,1)}, u32[]{:S(2)}) copy-start(bf16[3,512,128]{2,1,0:T(8,128)(2,1)} %param.22) | copy-start | bytes 1179652
  7.2 80.3 %all-gather.11.cloned.1.call-start = ((), (), s32[]{:S(2)}) async-start(), calls=%async_computation.7 | async-start | bytes 12681216 | tf_op jit(solution)/shard_map/all_gather | solution.py:102
  10.1 37.6 %copy-start.25 = (s32[96,8]{1,0:T(8,128)}, s32[96,8]{1,0:T(8,128)S(1)}, u32[]{:S(2)}) copy-start(s32[96,8]{1,0:T(8,128)S(1)} %copy.144) | copy-start | bytes 9220
  12.3 35.4 %copy-start.26 = (s32[96,8]{1,0:T(8,128)}, s32[96,8]{1,0:T(8,128)S(1)}, u32[]{:S(2)}) copy-start(s32[96,8]{1,0:T(8,128)S(1)} %copy.148) | copy-start | bytes 9220
  47.9 46.1 %copy-start.3 = (f32[128,24]{1,0:T(8,128)}, f32[128,24]{1,0:T(8,128)S(1)}, u32[]{:S(2)}) copy-start(f32[128,24]{1,0:T(8,128)S(1)} %copy.152) | copy-start | bytes 36868
  87.5 8.1 %copy-start.29 = (bf16[3,512,128]{2,1,0:T(8,128)(2,1)S(1)}, bf16[3,512,128]{2,1,0:T(8,128)(2,1)}, u32[]{:S(2)}) copy-start(bf16[3,512,128]{2,1,0:T(8,128)(2,1)} %param.18) | copy-start | bytes 1179652
  107.4 55.7 %all-to-all-start.1 = ((bf16[128,24,512]{2,1,0:T(8,128)(2,1)}), bf16[128,24,512]{2,1,0:T(8,128)(2,1)}, u32[]{:S(2)}, u32[]{:S(2)}) async-start(bf16[128,24,512]{2,1,0:T(8,128)(2,1)} %bitcast.168), calls=%async_computation.1 | async-start | bytes 6291456 | tf_op jit(solution)/shard_map/all_to_all | solution.py:105
  115.1 121.8 %all-gather.13.cloned.1.call-start = ((), (), s32[]{:S(2)}) async-start(), calls=%async_computation.8 | async-start | bytes 12681216 | tf_op jit(solution)/shard_map/all_gather | solution.py:102
  166.8 145.4 %all-gather.15.cloned.1.call-start = ((), (), s32[]{:S(2)}) async-start(), calls=%async_computation.9 | async-start | bytes 12681216 | tf_op jit(solution)/shard_map/all_gather | solution.py:102
  167.6 253.3 %all-gather.19.cloned.1.call-start = ((), (), s32[]{:S(2)}) async-start(), calls=%async_computation.11 | async-start | bytes 12681216 | tf_op jit(solution)/shard_map/all_gather | solution.py:102
  168.5 155.1 %copy-start.39 = (f32[3,1024]{1,0:T(4,128)}, f32[3,1024]{1,0:T(4,128)S(1)}, u32[]{:S(2)}) copy-start(f32[3,1024]{1,0:T(4,128)S(1)} %mul.93) | copy-start | bytes 36868
  236.9 8.1 %copy-start.28 = (bf16[3,512,128]{2,1,0:T(8,128)(2,1)S(1)}, bf16[3,512,128]{2,1,0:T(8,128)(2,1)}, u32[]{:S(2)}) copy-start(bf16[3,512,128]{2,1,0:T(8,128)(2,1)} %param.21) | copy-start | bytes 1179652
  312.3 9.3 %copy-start.2 = (bf16[12288,512]{1,0:T(8,128)(2,1)S(1)}, bf16[12288,512]{1,0:T(8,128)(2,1)}, u32[]{:S(2)}) copy-start(bf16[12288,512]{1,0:T(8,128)(2,1)} %all-gather.15.cloned.1.call-done) | copy-start | bytes 37748740
  318.8 5.8 copy-start.7
  326.1 10.8 %copy-start.18 = (bf16[3,1024,128]{2,1,0:T(8,128)(2,1)}, bf16[3,1024,128]{2,1,0:T(8,128)(2,1)S(1)}, u32[]{:S(2)}) copy-start(bf16[3,1024,128]{2,1,0:T(8,128)(2,1)S(1)} %get-tuple-element.48) | copy-start | bytes 2359300
  326.1 11.8 %copy-start.22 = (bf16[3,1024,128]{2,1,0:T(8,128)(2,1)}, bf16[3,1024,128]{2,1,0:T(8,128)(2,1)S(1)}, u32[]{:S(2)}) copy-start(bf16[3,1024,128]{2,1,0:T(8,128)(2,1)S(1)} %get-tuple-element.49) | copy-start | bytes 2359300
  329.0 17.6 %all-to-all-start.6 = ((f32[128,1,24]{2,1,0:T(1,128)}), f32[128,1,24]{2,1,0:T(1,128)S(1)}, u32[]{:S(2)}, u32[]{:S(2)}) async-start(f32[128,1,24]{2,1,0:T(1,128)} %copy.175), calls=%async_computation.6 | async-start | bytes 131072 | tf_op jit(solution)/shard_map/all_to_all | solution.py:123
  346.6 7.4 %copy-start.27 = (s32[96,8]{1,0:T(8,128)S(1)}, s32[96,8]{1,0:T(8,128)}, u32[]{:S(2)}) copy-start(s32[96,8]{1,0:T(8,128)} %copy-done.26) | copy-start | bytes 9220
  346.6 60.7 %copy-start.32 = (bf16[96,512]{1,0:T(8,128)(2,1)S(1)}, bf16[96,512]{1,0:T(8,128)(2,1)}, u32[]{:S(2)}) copy-start(bf16[96,512]{1,0:T(8,128)(2,1)} %param.17) | copy-start | bytes 294916
  347.3 60.1 %all-to-all-start.3 = ((bf16[128,24,512]{2,1,0:T(8,128)(2,1)}), bf16[128,24,512]{2,1,0:T(8,128)(2,1)S(1)}, u32[]{:S(2)}, u32[]{:S(2)}) async-start(bf16[128,24,512]{2,1,0:T(8,128)(2,1)} %bitcast.167), calls=%async_computation.3 | async-start | bytes 6291456 | tf_op jit(solution)/shard_map/all_to_all | solution.py:105
  351.8 144.9 %all-gather.17.cloned.1.call-start = ((), (), s32[]{:S(2)}) async-start(), calls=%async_computation.10 | async-start | bytes 12681216 | tf_op jit(solution)/shard_map/all_gather | solution.py:102
  414.7 6.2 %copy-start.4 = (f32[128,24]{1,0:T(8,128)S(1)}, f32[128,24]{1,0:T(8,128)}, u32[]{:S(2)}) copy-start(f32[128,24]{1,0:T(8,128)} %copy-done.3) | copy-start | bytes 36868
  414.7 100.1 %all-to-all-start.2 = ((bf16[128,24,512]{2,1,0:T(8,128)(2,1)}), bf16[128,24,512]{2,1,0:T(8,128)(2,1)}, u32[]{:S(2)}, u32[]{:S(2)}) async-start(bf16[128,24,512]{2,1,0:T(8,128)(2,1)} %copy_bitcast_fusion.2), calls=%async_computation.2 | async-start | bytes 6291456 | tf_op jit(solution)/shard_map/all_to_all | solution.py:105
  420.9 6.5 %copy-start.30 = (bf16[3,512,128]{2,1,0:T(8,128)(2,1)S(1)}, bf16[3,512,128]{2,1,0:T(8,128)(2,1)}, u32[]{:S(2)}) copy-start(bf16[3,512,128]{2,1,0:T(8,128)(2,1)} %param.18) | copy-start | bytes 1179652
  427.3 76.8 %copy-start.9 = (bf16[128,3,8,512]{3,2,1,0:T(8,128)(2,1)}, bf16[128,3,8,512]{3,2,1,0:T(8,128)(2,1)S(1)}, u32[]{:S(2)}) copy-start(bf16[128,3,8,512]{3,2,1,0:T(8,128)(2,1)S(1)} %convert_bitcast_fusion) | copy-start | bytes 9437188
  496.6 6.4 %copy-start.43 = (bf16[3,128,512]{2,1,0:T(8,128)(2,1)S(1)}, bf16[3,128,512]{2,1,0:T(8,128)(2,1)}, u32[]{:S(2)}) copy-start(bf16[3,128,512]{2,1,0:T(8,128)(2,1)} %param.20) | copy-start | bytes 1179652
  503.1 5.1 copy-start.11
  511.1 11.0 %copy-start.23 = (bf16[3,1024,128]{2,1,0:T(8,128)(2,1)S(1)}, bf16[3,1024,128]{2,1,0:T(8,128)(2,1)}, u32[]{:S(2)}) copy-start(bf16[3,1024,128]{2,1,0:T(8,128)(2,1)} %get-tuple-element.46) | copy-start | bytes 2359300
  511.1 11.0 %copy-start.35 = (bf16[3,512,128]{2,1,0:T(8,128)(2,1)S(1)}, bf16[3,512,128]{2,1,0:T(8,128)(2,1)}, u32[]{:S(2)}) copy-start(bf16[3,512,128]{2,1,0:T(8,128)(2,1)} %param.19) | copy-start | bytes 1179652
  514.8 17.2 %all-to-all-start.5 = ((f32[128,1,24]{2,1,0:T(1,128)}), f32[128,1,24]{2,1,0:T(1,128)S(1)}, u32[]{:S(2)}, u32[]{:S(2)}) async-start(f32[128,1,24]{2,1,0:T(1,128)} %copy.173), calls=%async_computation.5 | async-start | bytes 131072 | tf_op jit(solution)/shard_map/all_to_all | solution.py:123
  532.6 51.2 %all-to-all-start.4 = ((bf16[128,24,512]{2,1,0:T(8,128)(2,1)}), bf16[128,24,512]{2,1,0:T(8,128)(2,1)S(1)}, u32[]{:S(2)}, u32[]{:S(2)}) async-start(bf16[128,24,512]{2,1,0:T(8,128)(2,1)} %bitcast.166), calls=%async_computation.4 | async-start | bytes 6291456 | tf_op jit(solution)/shard_map/all_to_all | solution.py:105
  556.4 29.8 %copy-start.1 = (bf16[3,512,128]{2,1,0:T(8,128)(2,1)S(1)}, bf16[3,512,128]{2,1,0:T(8,128)(2,1)}, u32[]{:S(2)}) copy-start(bf16[3,512,128]{2,1,0:T(8,128)(2,1)} %param.22) | copy-start | bytes 1179652
  (28 other events, 65.3 us)
Sparse Core Ops, SparseCore 0:
  11.1 76.3 all-gather.10
  167.0 69.8 all-gather.12
  240.0 72.2 all-gather.14
  315.2 94.9 all-gather.18
  413.2 83.4 all-gather.16

commit v2 on v1

--- a/solution.py
+++ b/solution.py
@@ -1,6 +1,10 @@
+import functools
+
 import jax
 import jax.numpy as jnp
 from jax import lax
+from jax.experimental import pallas as pl
+from jax.experimental.pallas import tpu as pltpu
 from jax.sharding import PartitionSpec as P
 
 CAP_FACTOR = 4
@@ -16,14 +20,6 @@
     return (flat * capacity + slot).reshape(ids.shape)
 
 
-def slot_tables(rows, gates, total):
-    tok_dev = rows.shape[0]
-    hit = rows[:, :, None] == jnp.arange(total, dtype=jnp.int32)[None, None, :]
-    token = jnp.sum(jnp.where(hit, jnp.arange(tok_dev, dtype=F32)[:, None, None] - tok_dev, 0.0), axis=(0, 1)) + tok_dev
-    gate = jnp.sum(jnp.where(hit, gates[:, :, None], 0.0), axis=(0, 1))
-    return token, gate
-
-
 def pair_weight(rows, gates, total):
     hit = rows[:, :, None] == jnp.arange(total, dtype=jnp.int32)[None, None, :]
     return jnp.sum(jnp.where(hit, gates[:, :, None], 0.0), axis=1)
@@ -36,12 +32,167 @@
     return jnp.concatenate([hi.astype(BF16), mid.astype(BF16), low.astype(BF16)], axis=0)
 
 
-def pick_rows(all_rows, token, own):
-    n_group, tok_dev, width = all_rows.shape
-    pick = (token[:, :, None] == jnp.arange(tok_dev, dtype=F32)[None, None, :]).astype(BF16)
-    rows = jnp.einsum("srt,std->srd", pick, all_rows, preferred_element_type=F32).astype(BF16)
-    rows = rows.reshape(n_group, own, -1, width).transpose(1, 0, 2, 3)
-    return rows.reshape(own, -1, width)
+SIDE = 4
+
+
+def send_kernel(own, capacity, x_ref, code_ref, u_ref, held, local_sem, send_sem, recv_sem):
+    me = lax.axis_index("ep")
+    core = lax.rem(me, 2)
+    chip = lax.div(me, 2)
+    at = (lax.rem(chip, SIDE), lax.rem(lax.div(chip, SIDE), SIDE), lax.div(chip, SIDE * SIDE))
+    third = x_ref.shape[0] // 3
+    half = third // 2
+
+    def device(dim, step):
+        c = list(at)
+        c[dim] = lax.rem(c[dim] + step + SIDE, SIDE)
+        return ((c[2] * SIDE + c[1]) * SIDE + c[0]) * 2 + core
+
+    partner = chip * 2 + (1 - core)
+
+    def region(part, pos, first, count):
+        idx = [pos[d] if d in pos else at[d] for d in range(3)]
+        idx = [pl.ds(0, SIDE) if i is None else i for i in idx]
+        return held.at[core, idx[2], idx[1], idx[0], pl.ds(part * third + first, count), :]
+
+    copies = {}
+
+    def start(key, ref, to):
+        n = len(copies)
+        copies[key] = pltpu.make_async_remote_copy(src_ref=ref, dst_ref=ref, send_sem=send_sem.at[n], recv_sem=recv_sem.at[n], device_id={"ep": to}, device_id_type=pl.DeviceIdType.MESH)
+        copies[key].start()
+
+    mine = pltpu.make_async_copy(x_ref, held.at[core, at[2], at[1], at[0]], local_sem)
+    mine.start()
+    barrier = pltpu.get_barrier_semaphore()
+    for dim in range(3):
+        for step in (1, -1):
+            pl.semaphore_signal(barrier, inc=1, device_id={"ep": device(dim, step)}, device_id_type=pl.DeviceIdType.MESH)
+    pl.semaphore_signal(barrier, inc=1, device_id={"ep": partner}, device_id_type=pl.DeviceIdType.MESH)
+    mine.wait()
+    pl.semaphore_wait(barrier, 7)
+
+    def dims(part):
+        return part, (part + 1) % 3, (part + 2) % 3
+
+    def shift(dim, step):
+        return lax.rem(at[dim] + step + SIDE, SIDE)
+
+    def row_of(part, b, c, first=0, count=third):
+        d1, d2, d3 = dims(part)
+        return region(part, {d1: None, d2: shift(d2, b), d3: shift(d3, c)}, first, count)
+
+    def across(part, b, c):
+        start(("d2d", part, b, c), row_of(part, b, c), partner)
+
+    def whole_row(part, b):
+        d3 = dims(part)[2]
+        for way in (1, -1):
+            start(("m3", part, b, way), row_of(part, b, 0), device(d3, way))
+        across(part, b, 0)
+
+    def pass_on(part, b, way):
+        d3 = dims(part)[2]
+        copies["m3", part, b, way].wait_recv()
+        start(("f3", part, b, way), row_of(part, b, -way, 0 if way == 1 else half, half), device(d3, way))
+        across(part, b, -way)
+
+    def last_row(part, b):
+        for way in (1, -1):
+            copies["f3", part, b, way].wait_recv()
+        across(part, b, 2)
+
+    for part in range(3):
+        d1 = dims(part)[0]
+        for way in (1, -1):
+            start(("m1", part, way), region(part, {}, 0, third), device(d1, way))
+    for part in range(3):
+        d1 = dims(part)[0]
+        for way in (1, -1):
+            copies["m1", part, way].wait_recv()
+            start(("f1", part, way), region(part, {d1: shift(d1, -way)}, 0 if way == 1 else half, half), device(d1, way))
+    for part in range(3):
+        d2 = dims(part)[1]
+        for way in (1, -1):
+            copies["f1", part, way].wait_recv()
+        for way in (1, -1):
+            start(("m2", part, way), row_of(part, 0, 0), device(d2, way))
+        whole_row(part, 0)
+    for part in range(3):
+        d2 = dims(part)[1]
+        for way in (1, -1):
+            copies["m2", part, way].wait_recv()
+            start(("f2", part, way), row_of(part, -way, 0, 0 if way == 1 else half, half), device(d2, way))
+            whole_row(part, -way)
+    for part in range(3):
+        for way in (1, -1):
+            pass_on(part, 0, way)
+    for part in range(3):
+        for way in (1, -1):
+            copies["f2", part, way].wait_recv()
+        whole_row(part, 2)
+    for b in (-1, 1):
+        for part in range(3):
+            for way in (1, -1):
+                pass_on(part, b, way)
+    for part in range(3):
+        last_row(part, 0)
+    for part in range(3):
+        for way in (1, -1):
+            pass_on(part, 2, way)
+    for b in (-1, 1, 2):
+        for part in range(3):
+            last_row(part, b)
+    for key, copy in copies.items():
+        if key[0] == "d2d":
+            copy.wait_recv()
+
+    block = own * capacity
+    slot = lax.broadcasted_iota(jnp.int32, (block, x_ref.shape[0]), 0) + me * block
+    chips = SIDE ** 3
+    group = 4
+
+    def pick(step, carry):
+        for k in range(group):
+            place = step * group + k
+            rows = []
+            for c in range(2):
+                code = code_ref[place * 2 + c]
+                hit = code[0:1, :] == slot
+                for j in range(1, code.shape[0]):
+                    hit = hit | (code[j:j + 1, :] == slot)
+                tokens = held[c, lax.div(place, SIDE * SIDE), lax.rem(lax.div(place, SIDE), SIDE), lax.rem(place, SIDE)]
+                onehot = jnp.where(hit, 1.0, 0.0).astype(BF16)
+                rows.append(jnp.dot(onehot, tokens, preferred_element_type=F32))
+            for e in range(own):
+                both = jnp.concatenate([r[e * capacity:(e + 1) * capacity] for r in rows], axis=0)
+                u_ref[e, pl.ds(pl.multiple_of(place * 2 * capacity, 2 * capacity), 2 * capacity), :] = both.astype(BF16)
+        return carry
+
+    lax.fori_loop(0, chips // group, pick, 0)
+    for copy in copies.values():
+        copy.wait_send()
+
+
+def send_rows(x, code, own, capacity, call_id):
+    tok_dev, width = x.shape
+    n_group = code.shape[0]
+    count = 120
+    return pl.pallas_call(
+        functools.partial(send_kernel, own, capacity),
+        out_shape=jax.ShapeDtypeStruct((own, n_group * capacity, width), x.dtype),
+        in_specs=[pl.BlockSpec(memory_space=pl.ANY), pl.BlockSpec(memory_space=pltpu.VMEM)],
+        out_specs=pl.BlockSpec(memory_space=pltpu.VMEM),
+        scratch_shapes=[
+            pltpu.VMEM((2, SIDE, SIDE, SIDE, tok_dev, width), x.dtype),
+            pltpu.SemaphoreType.DMA,
+            pltpu.SemaphoreType.DMA((count,)),
+            pltpu.SemaphoreType.DMA((count,)),
+        ],
+        compiler_params=pltpu.CompilerParams(collective_id=call_id, has_side_effects=True, vmem_limit_bytes=40 * 1024 * 1024),
+        cost_estimate=pl.CostEstimate(flops=3 * 10**10, bytes_accessed=n_group * tok_dev * width * 2, transcendentals=0),
+        name=f"send_rows_{call_id}",
+    )(x, code)
 
 
 def home_order(rows, n_group):
@@ -88,19 +239,25 @@
 
         rows_a = pair_rows(idx_a, capacity)
         rows_b = pair_rows(idx_b, capacity)
-        tables = slot_tables(rows_a, gate_a, total) + slot_tables(rows_b, gate_b, total)
-        table = jnp.concatenate([t.reshape(n_group, block) for t in tables], axis=1)
-        table = lax.all_to_all(table, "ep", 0, 0, tiled=True)
-        token_a, far_gate_a, token_b, far_gate_b = jnp.split(table, 4, axis=1)
+        codes = jnp.stack([rows_a.T, rows_b.T])
+        gates = jnp.stack([gate_a.T, gate_b.T])
+        table = jnp.concatenate([codes.astype(F32), gates], axis=0)
+        table = lax.all_gather(table, "ep", axis=0, tiled=False)
+        code_a, code_b = table[:, 0].astype(jnp.int32), table[:, 1].astype(jnp.int32)
+        mine = (lax.axis_index("ep") * block + jnp.arange(block, dtype=jnp.int32)).astype(F32)
+
+        def far_gates(layer):
+            hit = table[:, layer, None] == mine[None, :, None, None]
+            gates = jnp.sum(jnp.where(hit, table[:, 2 + layer, None], 0.0), axis=(2, 3))
+            return gates.reshape(n_group, own, capacity).transpose(1, 0, 2).reshape(own, -1)
+
+        far_gate_a, far_gate_b = far_gates(0), far_gates(1)
         weight_a = split3(pair_weight(rows_a, gate_a, total))
         weight_b = split3(pair_weight(rows_b, gate_b, total))
         ones = jnp.ones_like(gate_a)
         pick_a = pair_weight(rows_a, ones, total).astype(BF16)
         pick_b = pair_weight(rows_b, ones, total).astype(BF16)
 
-        def gather(rows):
-            return lax.all_gather(rows, "ep", axis=0, tiled=False)
-
         def send_back(rows):
             back = lax.all_to_all(home_order(rows, n_group), "ep", 0, 0, tiled=True)
             return back.reshape(total, width)
@@ -110,10 +267,7 @@
             branch = branch[0] + (branch[1] + branch[2])
             return (x_rows.astype(F32) + branch).astype(BF16)
 
-        def layer_backward(dy_rows, dy_all, x_all, token, far_gate, pick, w_gate, w_up, w_down):
-            gates = far_gate.reshape(n_group, own, capacity).transpose(1, 0, 2).reshape(own, -1)
-            u_rows = pick_rows(x_all, token, own)
-            dy_sent = pick_rows(dy_all, token, own)
+        def layer_backward(dy_rows, dy_sent, u_rows, gates, pick, w_gate, w_up, w_down):
             du_rows, dgate_rows, dw_gate, dw_up, dw_down = expert_backward(u_rows, dy_sent, gates, w_gate, w_up, w_down)
             branch = jnp.dot(pick, send_back(du_rows), preferred_element_type=F32)
             dx_rows = (dy_rows.astype(F32) + branch).astype(BF16)
@@ -124,19 +278,20 @@
             hit = rows[:, :, None] == jnp.arange(total, dtype=jnp.int32)[None, None, :]
             return jnp.sum(jnp.where(hit, back.reshape(1, 1, total), 0.0), axis=2)
 
-        x_all = gather(x_in)
-        dy_all_b = gather(dy_out)
-        out_a = expert_forward(pick_rows(x_all, token_a, own), w1_a, w3_a, w2_a)[3]
-        x_mid = combine(x_in, send_back(out_a), weight_a)
-        mid_all = gather(x_mid)
-        out_b = expert_forward(pick_rows(mid_all, token_b, own), w1_b, w3_b, w2_b)[3]
+        u_a = send_rows(x_in, code_a, own, capacity, 0)
+        out_a = expert_forward(u_a, w1_a, w3_a, w2_a)[3]
+        back_a = send_back(out_a)
+        dy_b = send_rows(dy_out, code_b, own, capacity, 1)
+        x_mid = combine(x_in, back_a, weight_a)
+        u_b = send_rows(x_mid, code_b, own, capacity, 2)
+        out_b = expert_forward(u_b, w1_b, w3_b, w2_b)[3]
         x_out = combine(x_mid, send_back(out_b), weight_b)
-        mid_keep, dy_all_b, out_b = lax.optimization_barrier((mid_all, dy_all_b, out_b))
-        dx_mid, dgate_rows_b, grads_b = layer_backward(dy_out, dy_all_b, mid_keep, token_b, far_gate_b, pick_b, w1_b, w3_b, w2_b)
+        u_keep, dy_b, _ = lax.optimization_barrier((u_b, dy_b, out_b))
+        dx_mid, dgate_rows_b, grads_b = layer_backward(dy_out, dy_b, u_keep, far_gate_b, pick_b, w1_b, w3_b, w2_b)
         x_again, _ = lax.optimization_barrier((x_in, out_b))
-        again_all = gather(x_again)
-        dy_all_a = gather(dx_mid)
-        dx_in, dgate_rows_a, grads_a = layer_backward(dx_mid, dy_all_a, again_all, token_a, far_gate_a, pick_a, w1_a, w3_a, w2_a)
+        u_again = send_rows(x_again, code_a, own, capacity, 3)
+        dy_a = send_rows(dx_mid, code_a, own, capacity, 4)
+        dx_in, dgate_rows_a, grads_a = layer_backward(dx_mid, dy_a, u_again, far_gate_a, pick_a, w1_a, w3_a, w2_a)
         dgate_b = dgate_home(dgate_rows_b, rows_b)
         dgate_a = dgate_home(dgate_rows_a, rows_a)
         return (x_out, dx_in) + grads_a + grads_b + (dgate_a, dgate_b)

time: 602 us -> 615 us (1.022)
  Pallas kernels: 0 us -> 317 us
  waiting for transfers between devices: 351 us -> 86.4 us
  matrix products: 95.3 us -> 66.8 us
  blocking collectives: 21.3 us -> 0 us
  local copies, waits for them, and re-layouts: 29.7 us -> 40.6 us
    pallas_call x0 -> x5, Pallas kernels: none -> 317 us  [send_rows(): pl.pallas_call(functools.partial(send_kernel, own, capacity), out_shape=j...]
    all_gather x5 -> x1, waiting for transfers between devices: 236 us -> 59.5 us  [device_program(): table = lax.all_gather(table, 'ep', axis=0, tiled=False)]
    all_to_all x4, waiting for transfers between devices: 104 us -> 21.1 us  [send_back(): back = lax.all_to_all(home_order(rows, n_group), 'ep', 0, 0, tiled=True)]
    dot_general x6 -> x0, matrix products: 34.3 us -> none  [pick_rows(): jnp.einsum('srt,std->srd', pick, all_rows, preferred_element_type=F32)]
    all_to_all x1 -> x0, blocking collectives: 21.3 us -> none  [device_program(): table = lax.all_to_all(table, 'ep', 0, 0, tiled=True)]
    reduce_sum x1, other arithmetic: 11.9 us -> 5.18 us  [pair_weight(): return jnp.sum(jnp.where(hit, gates[:, :, None], 0.0), axis=1)]
    unnamed x104 -> x98, local copies, waits for them, and re-layouts: 15.2 us -> 17.6 us
  transfers between devices with their start and end apart: 11 -> 7, of which waited for: 9 -> 4; matrix products, arithmetic and copies ran while one was open for 22% -> 14% of each run, Pallas kernels for 0% -> 39%
where the time goes in v2:
time: 615 us; the launch traced here: 605 us
  Pallas kernels  317 us (52%)
  waiting for transfers between devices  86.4 us (14%)
  matrix products  66.8 us (11%)
  other arithmetic  40.8 us (7%)
  local copies, waits for them, and re-layouts  40.6 us (7%)
  starting transfers between devices  38 us (6%)
  between operations  15.2 us (2%)
    pallas_call x5, Pallas kernels, send_rows(): pl.pallas_call(functools.partial(send_kernel, own, capacity), out_shape=j...  317 us
    all_gather x1, waiting for transfers between devices, device_program(): table = lax.all_gather(table, 'ep', axis=0, tiled=False)  59.5 us
    all_to_all x4, starting transfers between devices, send_back(): back = lax.all_to_all(home_order(rows, n_group), 'ep', 0, 0, tiled=True)  26.6 us
    all_to_all x4, waiting for transfers between devices, send_back(): back = lax.all_to_all(home_order(rows, n_group), 'ep', 0, 0, tiled=True)  21.1 us
    reduce_sum x2, other arithmetic, dgate_home(): return jnp.sum(jnp.where(hit, back.reshape(1, 1, total), 0.0), axis=2)  19.5 us
    unnamed x98, local copies, waits for them, and re-layouts  17.6 us
    dot_general x4, matrix products, expert_forward(): jnp.einsum('erf,efd->erd', hidden, w_down, preferred_element_type=F32)  12.7 us
  transfers between devices with their start and end apart: 7, of which 4 were waited for; matrix products, arithmetic and copies ran while one was open for 14% of the time, Pallas kernels for 39%

profile of v2, /device:TPU:1, one launch (start us, length us, event | category | flops | bytes accessed | tf_op | source)
XLA Modules:
  0.0 605.3 jit_solution(13792183928843585541)
XLA Ops:
  15.8 5.2 select_reduce_fusion.7
  22.4 59.5 %all-gather.3.cloned.1.call-done = f32[512,8,96]{2,1,0:T(8,128)} async-done(((f32[4,8,96]{2,1,0:T(8,128)}), f32[512,8,96]{2,1,0:T(8,128)}) %all-gather.3.cloned.1.call-update) | async-done | bytes 1572880 | tf_op jit(solution)/shard_map/all_gather | solution.py:245
  81.9 2.7 slice_bitcast_fusion.2
  90.4 41.3 %send_rows_0.1 = bf16[3,1024,512]{2,1,0:T(8,128)(2,1)S(1)} custom-call(bf16[96,512]{1,0:T(8,128)(2,1)S(1)} %copy-done.13, s32[128,8,96]{2,1,0:T(8,128)S(1)} %copy-done.4), custom_call_target="tpu_custom_call" | custom-call | flops 30000001024 | bytes 12582912 | tf_op jit(solution)/shard_map/send_rows_0/pallas_call | solution.py:181
  133.9 4.9 convert_bitcast_fusion
  138.9 3.7 copy.179
  142.6 5.0 all-to-all-start
  151.2 77.3 %send_rows_1.1 = bf16[3,1024,512]{2,1,0:T(8,128)(2,1)S(1)} custom-call(bf16[96,512]{1,0:T(8,128)(2,1)S(1)} %copy-done.16, s32[128,8,96]{2,1,0:T(8,128)S(1)} %copy-done.7), custom_call_target="tpu_custom_call" | custom-call | flops 30000001024 | bytes 12582912 | tf_op jit(solution)/shard_map/send_rows_1/pallas_call | solution.py:181
  230.2 3.0 fusion.16
  233.3 41.8 %send_rows_2.1 = bf16[3,1024,512]{2,1,0:T(8,128)(2,1)S(1)} custom-call(bf16[96,512]{1,0:T(8,128)(2,1)S(1)} %fusion.43.x_ref, s32[128,8,96]{2,1,0:T(8,128)S(1)} %copy-done.8), custom_call_target="tpu_custom_call" | custom-call | flops 30000001024 | bytes 12582912 | tf_op jit(solution)/shard_map/send_rows_2/pallas_call | solution.py:181
  277.4 5.0 convolution_convert_fusion
  286.4 3.1 multiply_convert_fusion.4
  296.6 6.2 %all-to-all-start.5 = ((f32[128,1,24]{2,1,0:T(1,128)}), f32[128,1,24]{2,1,0:T(1,128)}, u32[]{:S(2)}, u32[]{:S(2)}) async-start(f32[128,1,24]{2,1,0:T(1,128)} %copy.152), calls=%async_computation.5 | async-start | bytes 131072 | tf_op jit(solution)/shard_map/all_to_all | solution.py:277
  302.9 2.3 fusion.54
  312.3 8.3 %all-to-all-start.2 = ((bf16[128,24,512]{2,1,0:T(8,128)(2,1)}), bf16[128,24,512]{2,1,0:T(8,128)(2,1)}, u32[]{:S(2)}, u32[]{:S(2)}) async-start(bf16[128,24,512]{2,1,0:T(8,128)(2,1)} %bitcast.120), calls=%async_computation.2 | async-start | bytes 6291456 | tf_op jit(solution)/shard_map/all_to_all | solution.py:262
  322.6 78.4 %send_rows_3.1 = bf16[3,1024,512]{2,1,0:T(8,128)(2,1)S(1)} custom-call(bf16[96,512]{1,0:T(8,128)(2,1)S(1)} %copy-done.15, s32[128,8,96]{2,1,0:T(8,128)S(1)} %copy-done.5), custom_call_target="tpu_custom_call" | custom-call | flops 30000001024 | bytes 12582912 | tf_op jit(solution)/shard_map/send_rows_3/pallas_call | solution.py:181
  407.2 2.3 reduce.11
  410.5 11.9 %select_reduce_fusion = (f32[96,8]{1,0:T(8,128)}, bf16[96,3072]{1,0:T(8,128)(2,1)}, f32[96,3072]{1,0:T(8,128)}) fusion(f32[3072]{0:T(1024)S(1)} %broadcast_in_dim.95, s32[96,8]{1,0:T(8,128)} %copy.131, f32[96,8]{1,0:T(8,128)} %copy.132), kind=kLoop, calls=%fused_computation | loop fusion | flops 15924480 | bytes 1790976 | tf_op jit(solution)/shard_map/reduce_sum | solution.py:279
  422.4 6.5 %all-to-all-start.1 = ((bf16[128,24,512]{2,1,0:T(8,128)(2,1)}), bf16[128,24,512]{2,1,0:T(8,128)(2,1)}, u32[]{:S(2)}, u32[]{:S(2)}) async-start(bf16[128,24,512]{2,1,0:T(8,128)(2,1)} %copy_bitcast_fusion.2), calls=%async_computation.1 | async-start | bytes 6291456 | tf_op jit(solution)/shard_map/all_to_all | solution.py:262
  428.9 2.7 fusion.32.x_ref
  431.6 78.6 %send_rows_4.1 = bf16[3,1024,512]{2,1,0:T(8,128)(2,1)S(1)} custom-call(bf16[96,512]{1,0:T(8,128)(2,1)S(1)} %fusion.32.x_ref, s32[128,8,96]{2,1,0:T(8,128)S(1)} %copy-done.6), custom_call_target="tpu_custom_call" | custom-call | flops 30000001024 | bytes 12582912 | tf_op jit(solution)/shard_map/send_rows_4/pallas_call | solution.py:181
  513.8 2.5 multiply_convert_fusion.1
  520.8 4.9 fusion.56
  525.6 5.2 all-to-all-start.4
  530.8 4.0 fusion.5
  536.7 3.6 all-to-all-done.4
  540.3 6.8 %all-to-all-start.3 = ((bf16[128,24,512]{2,1,0:T(8,128)(2,1)}), bf16[128,24,512]{2,1,0:T(8,128)(2,1)}, u32[]{:S(2)}, u32[]{:S(2)}) async-start(bf16[128,24,512]{2,1,0:T(8,128)(2,1)} %bitcast.119), calls=%async_computation.3 | async-start | bytes 6291456 | tf_op jit(solution)/shard_map/all_to_all | solution.py:262
  547.1 3.2 fusion.59
  553.4 3.1 fusion.22
  565.4 7.6 %select_reduce_fusion.1 = (f32[96,8]{1,0:T(8,128)S(1)}, bf16[96,3072]{1,0:T(8,128)(2,1)S(1)}) fusion(f32[3072]{0:T(1024)S(1)} %broadcast_in_dim.93, s32[96,8]{1,0:T(8,128)S(1)} %copy-done.39), kind=kLoop, calls=%fused_computation.1 | loop fusion | flops 11500800 | bytes 608256 | tf_op jit(solution)/shard_map/reduce_sum | solution.py:279
  573.7 21.1 %all-to-all-done.3 = bf16[128,24,512]{2,1,0:T(8,128)(2,1)} async-done(((bf16[128,24,512]{2,1,0:T(8,128)(2,1)}), bf16[128,24,512]{2,1,0:T(8,128)(2,1)}, u32[]{:S(2)}, u32[]{:S(2)}) %all-to-all-start.3) | async-done | bytes 3145760 | tf_op jit(solution)/shard_map/all_to_all | solution.py:262
  594.8 3.2 fusion.33
  (159 shorter events, 75.1 us)
Async XLA Ops:
  7.2 126.8 %copy-start = (bf16[3,512,128]{2,1,0:T(8,128)(2,1)S(1)}, bf16[3,512,128]{2,1,0:T(8,128)(2,1)}, u32[]{:S(2)}) copy-start(bf16[3,512,128]{2,1,0:T(8,128)(2,1)} %param.19) | copy-start | bytes 1179652
  7.2 74.7 %all-gather.3.cloned.1.call-start = ((), (), s32[]{:S(2)}) async-start(), calls=%async_computation.6 | async-start | bytes 2113536 | tf_op jit(solution)/shard_map/all_gather | solution.py:245
  12.9 69.0 %copy-start.38 = (s32[96,8]{1,0:T(8,128)}, s32[96,8]{1,0:T(8,128)S(1)}, u32[]{:S(2)}) copy-start(s32[96,8]{1,0:T(8,128)S(1)} %copy.125) | copy-start | bytes 9220
  90.4 41.3 %copy-start.22 = (bf16[3,512,128]{2,1,0:T(8,128)(2,1)S(1)}, bf16[3,512,128]{2,1,0:T(8,128)(2,1)}, u32[]{:S(2)}) copy-start(bf16[3,512,128]{2,1,0:T(8,128)(2,1)} %param.18) | copy-start | bytes 1179652
  142.6 5.1 copy-start.28
  142.6 5.1 copy-start.29
  142.6 5.1 copy-start.30
  142.6 5.1 copy-start.31
  142.6 8.5 %copy-start.7 = (s32[128,8,96]{2,1,0:T(8,128)S(1)}, s32[128,8,96]{2,1,0:T(8,128)}, u32[]{:S(2)}) copy-start(s32[128,8,96]{2,1,0:T(8,128)} %get-tuple-element.50.code_ref) | copy-start | bytes 1179652
  142.6 8.5 %copy-start.16 = (bf16[96,512]{1,0:T(8,128)(2,1)S(1)}, bf16[96,512]{1,0:T(8,128)(2,1)}, u32[]{:S(2)}) copy-start(bf16[96,512]{1,0:T(8,128)(2,1)} %x_ref.3) | copy-start | bytes 294916
  142.6 87.5 %all-to-all-start = ((bf16[128,24,512]{2,1,0:T(8,128)(2,1)}), bf16[128,24,512]{2,1,0:T(8,128)(2,1)}, u32[]{:S(2)}, u32[]{:S(2)}) async-start(bf16[128,24,512]{2,1,0:T(8,128)(2,1)} %bitcast.121), calls=%async_computation | async-start | bytes 6291456 | tf_op jit(solution)/shard_map/all_to_all | solution.py:262
  151.1 79.0 %copy-start.35 = (bf16[96,3072]{1,0:T(8,128)(2,1)S(1)}, bf16[96,3072]{1,0:T(8,128)(2,1)}, u32[]{:S(2)}) copy-start(bf16[96,3072]{1,0:T(8,128)(2,1)} %get-tuple-element.58) | copy-start | bytes 1769476
  151.1 79.0 %copy-start.36 = (bf16[96,3072]{1,0:T(8,128)(2,1)S(1)}, bf16[96,3072]{1,0:T(8,128)(2,1)}, u32[]{:S(2)}) copy-start(bf16[96,3072]{1,0:T(8,128)(2,1)} %get-tuple-element.59) | copy-start | bytes 1769476
  151.1 79.0 %copy-start.37 = (bf16[96,3072]{1,0:T(8,128)(2,1)S(1)}, bf16[96,3072]{1,0:T(8,128)(2,1)}, u32[]{:S(2)}) copy-start(bf16[96,3072]{1,0:T(8,128)(2,1)} %get-tuple-element.60) | copy-start | bytes 1769476
  233.3 41.9 %copy-start.9 = (bf16[96,512]{1,0:T(8,128)(2,1)}, bf16[96,512]{1,0:T(8,128)(2,1)S(1)}, u32[]{:S(2)}) copy-start(bf16[96,512]{1,0:T(8,128)(2,1)S(1)} %fusion.43.x_ref) | copy-start | bytes 294916
  233.3 41.9 %copy-start.21 = (bf16[3,512,128]{2,1,0:T(8,128)(2,1)S(1)}, bf16[3,512,128]{2,1,0:T(8,128)(2,1)}, u32[]{:S(2)}) copy-start(bf16[3,512,128]{2,1,0:T(8,128)(2,1)} %param.21) | copy-start | bytes 1179652
  296.6 15.7 %all-to-all-start.5 = ((f32[128,1,24]{2,1,0:T(1,128)}), f32[128,1,24]{2,1,0:T(1,128)}, u32[]{:S(2)}, u32[]{:S(2)}) async-start(f32[128,1,24]{2,1,0:T(1,128)} %copy.152), calls=%async_computation.5 | async-start | bytes 131072 | tf_op jit(solution)/shard_map/all_to_all | solution.py:277
  312.3 110.0 %all-to-all-start.2 = ((bf16[128,24,512]{2,1,0:T(8,128)(2,1)}), bf16[128,24,512]{2,1,0:T(8,128)(2,1)}, u32[]{:S(2)}, u32[]{:S(2)}) async-start(bf16[128,24,512]{2,1,0:T(8,128)(2,1)} %bitcast.120), calls=%async_computation.2 | async-start | bytes 6291456 | tf_op jit(solution)/shard_map/all_to_all | solution.py:262
  322.6 80.2 %copy-start.23 = (bf16[3,512,128]{2,1,0:T(8,128)(2,1)S(1)}, bf16[3,512,128]{2,1,0:T(8,128)(2,1)}, u32[]{:S(2)}) copy-start(bf16[3,512,128]{2,1,0:T(8,128)(2,1)} %param.18) | copy-start | bytes 1179652
  422.4 103.2 %all-to-all-start.1 = ((bf16[128,24,512]{2,1,0:T(8,128)(2,1)}), bf16[128,24,512]{2,1,0:T(8,128)(2,1)}, u32[]{:S(2)}, u32[]{:S(2)}) async-start(bf16[128,24,512]{2,1,0:T(8,128)(2,1)} %copy_bitcast_fusion.2), calls=%async_computation.1 | async-start | bytes 6291456 | tf_op jit(solution)/shard_map/all_to_all | solution.py:262
  431.6 78.6 %copy-start.11 = (bf16[96,512]{1,0:T(8,128)(2,1)}, bf16[96,512]{1,0:T(8,128)(2,1)S(1)}, u32[]{:S(2)}) copy-start(bf16[96,512]{1,0:T(8,128)(2,1)S(1)} %fusion.32.x_ref) | copy-start | bytes 294916
  431.6 78.6 %copy-start.40 = (f32[3,1024]{1,0:T(4,128)S(1)}, f32[3,1024]{1,0:T(4,128)}, u32[]{:S(2)}) copy-start(f32[3,1024]{1,0:T(4,128)} %mul.108) | copy-start | bytes 36868
  431.6 78.6 %copy-start.43 = (bf16[3,128,512]{2,1,0:T(8,128)(2,1)S(1)}, bf16[3,128,512]{2,1,0:T(8,128)(2,1)}, u32[]{:S(2)}) copy-start(bf16[3,128,512]{2,1,0:T(8,128)(2,1)} %param.20) | copy-start | bytes 1179652
  510.3 6.0 copy-start.17
  510.3 3.5 copy-start.32
  525.6 14.7 %all-to-all-start.4 = ((f32[128,1,24]{2,1,0:T(1,128)}), f32[128,1,24]{2,1,0:T(1,128)}, u32[]{:S(2)}, u32[]{:S(2)}) async-start(f32[128,1,24]{2,1,0:T(1,128)} %copy.150), calls=%async_computation.4 | async-start | bytes 131072 | tf_op jit(solution)/shard_map/all_to_all | solution.py:277
  540.3 54.5 %all-to-all-start.3 = ((bf16[128,24,512]{2,1,0:T(8,128)(2,1)}), bf16[128,24,512]{2,1,0:T(8,128)(2,1)}, u32[]{:S(2)}, u32[]{:S(2)}) async-start(bf16[128,24,512]{2,1,0:T(8,128)(2,1)} %bitcast.119), calls=%async_computation.3 | async-start | bytes 6291456 | tf_op jit(solution)/shard_map/all_to_all | solution.py:262
  553.4 3.2 copy-start.10
  553.4 3.9 copy-start.3
  553.4 3.9 copy-start.24
  561.5 3.9 copy-start.39
  561.5 33.3 %copy-start.12 = (bf16[96,512]{1,0:T(8,128)(2,1)S(1)}, bf16[96,512]{1,0:T(8,128)(2,1)}, u32[]{:S(2)}) copy-start(bf16[96,512]{1,0:T(8,128)(2,1)} %copy-done.11) | copy-start | bytes 294916
  (21 other events, 42.0 us)
Sparse Core Ops, SparseCore 0:
  12.9 68.9 all-gather.2

commit v3 on v2

v3 whole, which is shorter than its diff:
```python
import functools

import jax
import jax.numpy as jnp
from jax import lax
from jax.experimental import pallas as pl
from jax.experimental.pallas import tpu as pltpu
from jax.sharding import PartitionSpec as P

CAP_FACTOR = 4
F32 = jnp.float32
BF16 = jnp.bfloat16


def pair_rows(ids, capacity):
    flat = ids.reshape(-1)
    pair = jnp.arange(flat.shape[0], dtype=jnp.int32)
    earlier = (flat[None, :] == flat[:, None]) & (pair[None, :] < pair[:, None])
    slot = jnp.sum(earlier.astype(jnp.int32), axis=1)
    return (flat * capacity + slot).reshape(ids.shape)


def pair_weight(rows, gates, total):
    hit = rows[:, :, None] == jnp.arange(total, dtype=jnp.int32)[None, None, :]
    return jnp.sum(jnp.where(hit, gates[:, :, None], 0.0), axis=1)


def split3(w):
    hi = lax.reduce_precision(w, 8, 7)
    mid = lax.reduce_precision(w - hi, 8, 7)
    low = w - hi - mid
    return jnp.concatenate([hi.astype(BF16), mid.astype(BF16), low.astype(BF16)], axis=0)


SIDE = 4


def send_kernel(own, capacity, layer, plus, first, *refs):
    if first:
        x_ref, tile_ref, u_ref, table_ref, held, local_sem, send_sem, recv_sem, tiles = refs
    else:
        x_ref, table_ref, u_ref, held, local_sem, send_sem, recv_sem = refs
        tiles = table_ref
    me = lax.axis_index("ep")
    core = lax.rem(me, 2)
    chip = lax.div(me, 2)
    at = (lax.rem(chip, SIDE), lax.rem(lax.div(chip, SIDE), SIDE), lax.div(chip, SIDE * SIDE))
    third = x_ref.shape[0] // 3
    spans = {1: (0, plus), -1: (plus, third - plus)}

    def device(dim, step):
        c = list(at)
        c[dim] = lax.rem(c[dim] + step + SIDE, SIDE)
        return ((c[2] * SIDE + c[1]) * SIDE + c[0]) * 2 + core

    partner = chip * 2 + (1 - core)

    def region(part, pos, span):
        idx = [pos[d] if d in pos else at[d] for d in range(3)]
        idx = [pl.ds(0, SIDE) if i is None else i for i in idx]
        where = (core, idx[2], idx[1], idx[0])
        return held.at[where + (pl.ds(part * third + span[0], span[1]),)], where + (part,)

    copies = {}

    def start(key, refs, to, with_tile):
        for kind, ref in (("x", refs[0]), ("t", tiles.at[refs[1]])):
            if kind == "t" and not (first and with_tile) or ref.shape[-2] == 0:
                continue
            n = len(copies)
            copy = pltpu.make_async_remote_copy(src_ref=ref, dst_ref=ref, send_sem=send_sem.at[n], recv_sem=recv_sem.at[n], device_id={"ep": to}, device_id_type=pl.DeviceIdType.MESH)
            copy.start()
            copies[key + (kind,)] = copy

    def arrive(*key):
        for kind in ("x", "t"):
            if key + (kind,) in copies:
                copies[key + (kind,)].wait_recv()

    mine = pltpu.make_async_copy(x_ref, held.at[core, at[2], at[1], at[0]], local_sem)
    mine.start()
    if first:
        own_tile = pltpu.make_async_copy(tile_ref, tiles.at[core, at[2], at[1], at[0]], send_sem.at[0])
        own_tile.start()
        own_tile.wait()
    barrier = pltpu.get_barrier_semaphore()
    for dim in range(3):
        for step in (1, -1):
            pl.semaphore_signal(barrier, inc=1, device_id={"ep": device(dim, step)}, device_id_type=pl.DeviceIdType.MESH)
    pl.semaphore_signal(barrier, inc=1, device_id={"ep": partner}, device_id_type=pl.DeviceIdType.MESH)
    mine.wait()
    pl.semaphore_wait(barrier, 7)

    def dims(part):
        return part, (part + 1) % 3, (part + 2) % 3

    def shift(dim, step):
        return lax.rem(at[dim] + step + SIDE, SIDE)

    whole = (0, third)

    def row_of(part, b, c, span=whole):
        d1, d2, d3 = dims(part)
        return region(part, {d1: None, d2: shift(d2, b), d3: shift(d3, c)}, span)

    def across(part, b, c):
        start(("d2d", part, b, c), row_of(part, b, c), partner, True)

    def whole_row(part, b):
        d3 = dims(part)[2]
        for way in (1, -1):
            start(("m3", part, b, way), row_of(part, b, 0), device(d3, way), True)
        across(part, b, 0)

    def pass_on(part, b, way):
        d3 = dims(part)[2]
        arrive("m3", part, b, way)
        start(("f3", part, b, way), row_of(part, b, -way, spans[way]), device(d3, way), way == -1)
        across(part, b, -way)

    def last_row(part, b):
        for way in (1, -1):
            arrive("f3", part, b, way)
        across(part, b, 2)

    block = own * capacity
    slot = lax.broadcasted_iota(jnp.int32, (block, 128), 0) + me * block
    tok_dev = x_ref.shape[0]

    def pick(offsets):
        x, y, z = (lax.rem(at[d] + offsets[d] + SIDE, SIDE) for d in range(3))
        rows = []
        for c in range(2):
            code = tiles[c, z, y, x, layer].astype(jnp.int32)
            hit = code[0:1, :] == slot
            for j in range(1, code.shape[0]):
                hit = hit | (code[j:j + 1, :] == slot)
            onehot = jnp.where(hit, 1.0, 0.0)[:, :tok_dev].astype(BF16)
            rows.append(jnp.dot(onehot, held[c, z, y, x], preferred_element_type=F32))
        place = ((z * SIDE + y) * SIDE + x) * 2 * capacity
        for e in range(own):
            both = jnp.concatenate([r[e * capacity:(e + 1) * capacity] for r in rows], axis=0)
            u_ref[e, pl.ds(pl.multiple_of(place, 2 * capacity), 2 * capacity), :] = both.astype(BF16)

    def near_rows(step, carry):
        for k in (-1, 0, 1):
            pick((k, lax.rem(step, 3) - 1, lax.div(step, 3) - 1))
        return carry

    def far_rows(step, carry):
        b, c = lax.rem(step, 3) - 1, lax.div(step, 3) - 1
        for offsets in ((2, b, c), (b, 2, c), (b, c, 2)):
            pick(offsets)
        return carry

    def farthest_rows(step, carry):
        for offsets in ((2, 2, step - 1), (2, step - 1, 2), (step - 1, 2, 2)):
            pick(offsets)
        return carry

    def arrive_across(wanted):
        for part in range(3):
            for b in (0, -1, 1, 2):
                for c in (0, -1, 1, 2):
                    if (b == 2) + (c == 2) == wanted:
                        arrive("d2d", part, b, c)

    for part in range(3):
        d1 = dims(part)[0]
        for way in (1, -1):
            start(("m1", part, way), region(part, {}, whole), device(d1, way), True)
    for part in range(3):
        d1 = dims(part)[0]
        for way in (1, -1):
            arrive("m1", part, way)
            start(("f1", part, way), region(part, {d1: shift(d1, -way)}, spans[way]), device(d1, way), way == -1)
    for part in range(3):
        d2 = dims(part)[1]
        for way in (1, -1):
            arrive("f1", part, way)
        for way in (1, -1):
            start(("m2", part, way), row_of(part, 0, 0), device(d2, way), True)
        whole_row(part, 0)
    for part in range(3):
        d2 = dims(part)[1]
        for way in (1, -1):
            arrive("m2", part, way)
            start(("f2", part, way), row_of(part, -way, 0, spans[way]), device(d2, way), way == -1)
            whole_row(part, -way)
    for part in range(3):
        for way in (1, -1):
            pass_on(part, 0, way)
    for part in range(3):
        for way in (1, -1):
            arrive("f2", part, way)
        whole_row(part, 2)
    for b in (-1, 1):
        for part in range(3):
            for way in (1, -1):
                pass_on(part, b, way)
    arrive_across(0)
    lax.fori_loop(0, 9, near_rows, 0)
    for part in range(3):
        last_row(part, 0)
    for part in range(3):
        for way in (1, -1):
            pass_on(part, 2, way)
    for b in (-1, 1):
        for part in range(3):
            last_row(part, b)
    arrive_across(1)
    lax.fori_loop(0, 9, far_rows, 0)
    for part in range(3):
        last_row(part, 2)
    arrive_across(2)
    lax.fori_loop(0, 3, farthest_rows, 0)
    pick((2, 2, 2))
    if first:
        table_ref[...] = tiles[...]
    for copy in copies.values():
        copy.wait_send()


def send_rows(x, table, layer, own, capacity, call_id, plus, first=False):
    tok_dev, width = x.shape
    devices = 2 * SIDE ** 3
    count = 240 if first else 120
    u_shape = jax.ShapeDtypeStruct((own, devices * capacity, width), x.dtype)
    table_shape = jax.ShapeDtypeStruct((2, SIDE, SIDE, SIDE, 3, 8, 128), F32)
    vmem = pl.BlockSpec(memory_space=pltpu.VMEM)
    hbm = pl.BlockSpec(memory_space=pl.ANY)
    return pl.pallas_call(
        functools.partial(send_kernel, own, capacity, layer, plus, first),
        out_shape=(u_shape, table_shape) if first else u_shape,
        in_specs=[hbm, hbm if first else vmem],
        out_specs=(vmem, vmem) if first else vmem,
        scratch_shapes=[
            pltpu.VMEM((2, SIDE, SIDE, SIDE, tok_dev, width), x.dtype),
            pltpu.SemaphoreType.DMA,
            pltpu.SemaphoreType.DMA((count,)),
            pltpu.SemaphoreType.DMA((count,)),
        ] + ([pltpu.VMEM(table_shape.shape, F32)] if first else []),
        compiler_params=pltpu.CompilerParams(collective_id=call_id, has_side_effects=True, vmem_limit_bytes=40 * 1024 * 1024),
        cost_estimate=pl.CostEstimate(flops=3 * 10**10, bytes_accessed=devices * tok_dev * width * 2, transcendentals=0),
        name=f"send_rows_{call_id}",
    )(x, table)


def home_order(rows, n_group):
    own, count, width = rows.shape
    rows = rows.reshape(own, n_group, count // n_group, width).transpose(1, 0, 2, 3)
    return rows.reshape(n_group, -1, width)


def expert_forward(u_rows, w_gate, w_up, w_down):
    pre_gate = jnp.einsum("erd,edf->erf", u_rows, w_gate, preferred_element_type=F32)
    pre_up = jnp.einsum("erd,edf->erf", u_rows, w_up, preferred_element_type=F32)
    hidden = (jax.nn.silu(pre_gate) * pre_up).astype(BF16)
    out_rows = jnp.einsum("erf,efd->erd", hidden, w_down, preferred_element_type=F32).astype(BF16)
    return pre_gate, pre_up, hidden, out_rows


def expert_backward(u_rows, dy_rows, gate_rows, w_gate, w_up, w_down):
    pre_gate, pre_up, hidden, out_rows = expert_forward(u_rows, w_gate, w_up, w_down)
    dgate_rows = jnp.einsum("erd,erd->er", dy_rows, out_rows, preferred_element_type=F32)
    d_out = (gate_rows[:, :, None] * dy_rows).astype(BF16)
    dw_down = jnp.einsum("erf,erd->efd", hidden, d_out, preferred_element_type=F32)
    d_hidden = jnp.einsum("erd,efd->erf", d_out, w_down, preferred_element_type=F32)
    gate_sig = jax.nn.sigmoid(pre_gate)
    d_pre_gate = (d_hidden * pre_up * gate_sig * (1.0 + pre_gate * (1.0 - gate_sig))).astype(BF16)
    d_pre_up = (d_hidden * jax.nn.silu(pre_gate)).astype(BF16)
    dw_gate = jnp.einsum("erd,erf->edf", u_rows, d_pre_gate, preferred_element_type=F32)
    dw_up = jnp.einsum("erd,erf->edf", u_rows, d_pre_up, preferred_element_type=F32)
    du_rows = (jnp.einsum("erf,edf->erd", d_pre_gate, w_gate, preferred_element_type=F32) + jnp.einsum("erf,edf->erd", d_pre_up, w_up, preferred_element_type=F32)).astype(BF16)
    return du_rows, dgate_rows, dw_gate, dw_up, dw_down


def solution(mesh):
    n_group = mesh.shape["ep"]
    tok_spec = P(("dp", "ep"))
    w_spec = P("ep")

    def device_program(x_in, idx_a, idx_b, gate_a, gate_b, dy_out, w1_a, w3_a, w2_a, w1_b, w3_b, w2_b):
        tok_dev, top_k = idx_a.shape
        width = x_in.shape[1]
        own = w1_a.shape[0]
        capacity = CAP_FACTOR * tok_dev * top_k // (own * n_group)
        total = own * n_group * capacity
        block = own * capacity

        rows_a = pair_rows(idx_a, capacity)
        rows_b = pair_rows(idx_b, capacity)
        lanes = [rows_a.T.astype(F32), rows_b.T.astype(F32), gate_a.T]
        rest = gate_b.T
        cut = 128 - tok_dev
        tile = jnp.stack([jnp.concatenate([lanes[i], rest[:, i * cut:(i + 1) * cut]], axis=1) for i in range(3)])
        third = tok_dev // 3
        even = third // 2
        u_a, table = send_rows(x_in, tile, 0, own, capacity, 0, even, True)
        by_device = table.reshape(2, n_group // 2, 3, 8, 128).transpose(1, 0, 2, 3, 4).reshape(n_group, 3, 8, 128)
        mine = (lax.axis_index("ep") * block + jnp.arange(block, dtype=jnp.int32)).astype(F32)

        def far_gates(code, gates):
            hit = code[:, None] == mine[None, :, None, None]
            gates = jnp.sum(jnp.where(hit, gates[:, None], 0.0), axis=(2, 3))
            return gates.reshape(n_group, own, capacity).transpose(1, 0, 2).reshape(own, -1)

        far_gate_a = far_gates(by_device[:, 0, :, :tok_dev], by_device[:, 2, :, :tok_dev])
        spread_b = jnp.concatenate([by_device[:, i, :, tok_dev:] for i in range(3)], axis=2)
        far_gate_b = far_gates(by_device[:, 1, :, :tok_dev], spread_b)
        weight_a = split3(pair_weight(rows_a, gate_a, total))
        weight_b = split3(pair_weight(rows_b, gate_b, total))
        ones = jnp.ones_like(gate_a)
        pick_a = pair_weight(rows_a, ones, total).astype(BF16)
        pick_b = pair_weight(rows_b, ones, total).astype(BF16)

        def send_back(rows):
            back = lax.all_to_all(home_order(rows, n_group), "ep", 0, 0, tiled=True)
            return back.reshape(total, width)

        def combine(x_rows, back, weight):
            branch = jnp.dot(weight, back, preferred_element_type=F32).reshape(3, tok_dev, width)
            branch = branch[0] + (branch[1] + branch[2])
            return (x_rows.astype(F32) + branch).astype(BF16)

        def layer_backward(dy_rows, dy_sent, u_rows, gates, pick, w_gate, w_up, w_down):
            du_rows, dgate_rows, dw_gate, dw_up, dw_down = expert_backward(u_rows, dy_sent, gates, w_gate, w_up, w_down)
            branch = jnp.dot(pick, send_back(du_rows), preferred_element_type=F32)
            dx_rows = (dy_rows.astype(F32) + branch).astype(BF16)
            return dx_rows, dgate_rows, (dw_gate, dw_up, dw_down)

        def by_home(dgate_rows):
            return dgate_rows.reshape(own, n_group, capacity).transpose(1, 0, 2).reshape(n_group, block)

        def look_up(back, rows):
            flat = rows.reshape(-1)
            expert = lax.div(flat, capacity)[:, None] == jnp.arange(own * n_group, dtype=jnp.int32)[None, :]
            picked = jnp.dot(expert.astype(F32), back.reshape(own * n_group, capacity), precision=lax.Precision.HIGHEST)
            slot = lax.rem(flat, capacity)[:, None] == jnp.arange(capacity, dtype=jnp.int32)[None, :]
            return jnp.sum(jnp.where(slot, picked, 0.0), axis=1).reshape(rows.shape)

        out_a = expert_forward(u_a, w1_a, w3_a, w2_a)[3]
        back_a = send_back(out_a)
        dy_b = send_rows(dy_out, table, 1, own, capacity, 1, 0)
        x_mid = combine(x_in, back_a, weight_a)
        u_b = send_rows(x_mid, table, 1, own, capacity, 2, even)
        out_b = expert_forward(u_b, w1_b, w3_b, w2_b)[3]
        x_out = combine(x_mid, send_back(out_b), weight_b)
        u_keep, dy_b, _ = lax.optimization_barrier((u_b, dy_b, out_b))
        dx_mid, dgate_rows_b, grads_b = layer_backward(dy_out, dy_b, u_keep, far_gate_b, pick_b, w1_b, w3_b, w2_b)
        x_again, _ = lax.optimization_barrier((x_in, out_b))
        u_again = send_rows(x_again, table, 0, own, capacity, 3, 0)
        dy_a = send_rows(dx_mid, table, 0, own, capacity, 4, 0)
        dx_in, dgate_rows_a, grads_a = layer_backward(dx_mid, dy_a, u_again, far_gate_a, pick_a, w1_a, w3_a, w2_a)
        dgates = jnp.concatenate([by_home(dgate_rows_a), by_home(dgate_rows_b)], axis=1)
        dgates = lax.all_to_all(dgates, "ep", 0, 0, tiled=True)
        dgate_a = look_up(dgates[:, :block], rows_a)
        dgate_b = look_up(dgates[:, block:], rows_b)
        return (x_out, dx_in) + grads_a + grads_b + (dgate_a, dgate_b)

    return jax.shard_map(device_program, mesh=mesh, in_specs=(tok_spec,) * 6 + (w_spec,) * 6, out_specs=(tok_spec,) * 10, check_vma=False)
```

time: 615 us -> 523 us (0.85)
  waiting for transfers between devices: 86.4 us -> 30.4 us
  between operations: 15.2 us -> 1.65 us
  Pallas kernels: 317 us -> 304 us
  other arithmetic: 40.8 us -> 34.5 us
    all_gather x1 -> x0, waiting for transfers between devices: 59.5 us -> none  [device_program(): table = lax.all_gather(table, 'ep', axis=0, tiled=False)]
    reduce_sum x3 -> x1, other arithmetic: 21.8 us -> 3.39 us  [far_gates(): gates = jnp.sum(jnp.where(hit, gates[:, None], 0.0), axis=(2, 3))]
    reduce_sum x1 -> x2, other arithmetic: 5.18 us -> 19.6 us  [pair_weight(): return jnp.sum(jnp.where(hit, gates[:, :, None], 0.0), axis=1)]
    pallas_call x5, Pallas kernels: 317 us -> 304 us  [send_rows(): pl.pallas_call(functools.partial(send_kernel, own, capacity, layer, plus,...]
    unnamed x98 -> x134, local copies, waits for them, and re-layouts: 17.6 us -> 15.1 us
  transfers between devices with their start and end apart: 7 -> 5, of which waited for: 4 -> 2; matrix products, arithmetic and copies ran while one was open for 14% -> 17% of each run, Pallas kernels for 39% -> 40%
where the time goes in v3:
time: 523 us; the launch traced here: 516 us
  Pallas kernels  304 us (58%)
  matrix products  68.2 us (13%)
  local copies, waits for them, and re-layouts  41.6 us (8%)
  starting transfers between devices  36 us (7%)
  other arithmetic  34.5 us (7%)
  waiting for transfers between devices  30.4 us (6%)
    pallas_call x5, Pallas kernels, send_rows(): pl.pallas_call(functools.partial(send_kernel, own, capacity, layer, plus,...  304 us
    all_to_all x4, starting transfers between devices, send_back(): back = lax.all_to_all(home_order(rows, n_group), 'ep', 0, 0, tiled=True)  29 us
    all_to_all x4, waiting for transfers between devices, send_back(): back = lax.all_to_all(home_order(rows, n_group), 'ep', 0, 0, tiled=True)  26.6 us
    reduce_sum x2, other arithmetic, pair_weight(): return jnp.sum(jnp.where(hit, gates[:, :, None], 0.0), axis=1)  19.6 us
    unnamed x134, local copies, waits for them, and re-layouts  15.1 us
    dot_general x4, matrix products, expert_forward(): jnp.einsum('erf,efd->erd', hidden, w_down, preferred_element_type=F32)  12.7 us
  transfers between devices with their start and end apart: 5, of which 2 were waited for; matrix products, arithmetic and copies ran while one was open for 17% of the time, Pallas kernels for 40%

profile of v3, /device:TPU:1, one launch (start us, length us, event | category | flops | bytes accessed | tf_op | source)
XLA Modules:
  0.0 516.2 jit_solution(6822664483613487708)
XLA Ops:
  8.6 52.8 %send_rows_0.1 = (bf16[3,1024,512]{2,1,0:T(8,128)(2,1)S(1)}, f32[2,4,4,4,3,8,128]{6,5,4,3,2,1,0:T(8,128)S(1)}) custom-call(bf16[96,512]{1,0:T(8,128)(2,1)S(1)} %copy-done.14, f32[3,8,128]{2,1,0:T(8,128)S(1)} %pad_maximum_fusion.1.refs_1_), custom_call_target="tpu_custom_call" | custom-call | flops 30000001024 | bytes 12582912 | tf_op jit(solution)/shard_map/send_rows_0/pallas_call | solution.py:232
  62.6 2.2 fusion.58
  64.7 5.1 convert_bitcast_fusion
  69.8 3.7 copy.147
  73.5 5.0 all-to-all-start
  81.6 9.7 %select_reduce_fusion.1 = (bf16[96,3072]{1,0:T(8,128)(2,1)}, f32[96,3072]{1,0:T(8,128)S(1)}) fusion(s32[96,8]{1,0:T(8,128)S(1)} %copy.93, f32[96,8]{1,0:T(8,128)S(1)} %copy.94), kind=kLoop, calls=%fused_computation.1 | loop fusion | flops 11206656 | bytes 1775616 | tf_op jit(solution)/shard_map/reduce_sum | solution.py:25
  92.7 9.9 %select_reduce_fusion.3 = (bf16[96,3072]{1,0:T(8,128)(2,1)}, f32[96,3072]{1,0:T(8,128)S(1)}) fusion(s32[96,8]{1,0:T(8,128)S(1)} %copy.98, f32[96,8]{1,0:T(8,128)S(1)} %copy.99), kind=kLoop, calls=%fused_computation.3 | loop fusion | flops 11206656 | bytes 1775616 | tf_op jit(solution)/shard_map/reduce_sum | solution.py:25
  109.7 3.4 select_reduce_fusion
  116.0 46.2 %send_rows_1.1 = bf16[3,1024,512]{2,1,0:T(8,128)(2,1)S(1)} custom-call(bf16[96,512]{1,0:T(8,128)(2,1)S(1)} %copy-done.17, f32[2,4,4,4,3,8,128]{6,5,4,3,2,1,0:T(8,128)S(1)} %copy-done.6), custom_call_target="tpu_custom_call" | custom-call | flops 30000001024 | bytes 12582912 | tf_op jit(solution)/shard_map/send_rows_1/pallas_call | solution.py:232
  163.9 3.3 fusion.16
  167.3 42.9 %send_rows_2.1 = bf16[3,1024,512]{2,1,0:T(8,128)(2,1)S(1)} custom-call(bf16[96,512]{1,0:T(8,128)(2,1)S(1)} %fusion.51.refs_0_, f32[2,4,4,4,3,8,128]{6,5,4,3,2,1,0:T(8,128)S(1)} %copy-done.7), custom_call_target="tpu_custom_call" | custom-call | flops 30000001024 | bytes 12582912 | tf_op jit(solution)/shard_map/send_rows_2/pallas_call | solution.py:232
  212.4 4.9 convolution_convert_fusion
  220.5 2.5 multiply_convert_fusion
  226.7 2.3 fusion.61
  231.9 7.2 %all-to-all-start.2 = ((bf16[128,24,512]{2,1,0:T(8,128)(2,1)}), bf16[128,24,512]{2,1,0:T(8,128)(2,1)}, u32[]{:S(2)}, u32[]{:S(2)}) async-start(bf16[128,24,512]{2,1,0:T(8,128)(2,1)} %bitcast.132), calls=%async_computation.2 | async-start | bytes 6291456 | tf_op jit(solution)/shard_map/all_to_all | solution.py:318
  240.5 79.6 %send_rows_3.1 = bf16[3,1024,512]{2,1,0:T(8,128)(2,1)S(1)} custom-call(bf16[96,512]{1,0:T(8,128)(2,1)S(1)} %copy-done.16, f32[2,4,4,4,3,8,128]{6,5,4,3,2,1,0:T(8,128)S(1)} %copy-done.8), custom_call_target="tpu_custom_call" | custom-call | flops 30000001024 | bytes 12582912 | tf_op jit(solution)/shard_map/send_rows_3/pallas_call | solution.py:232
  321.9 2.1 fusion.62
  325.9 10.4 %all-to-all-start.1 = ((bf16[128,24,512]{2,1,0:T(8,128)(2,1)}), bf16[128,24,512]{2,1,0:T(8,128)(2,1)}, u32[]{:S(2)}, u32[]{:S(2)}) async-start(bf16[128,24,512]{2,1,0:T(8,128)(2,1)} %copy_bitcast_fusion.2), calls=%async_computation.1 | async-start | bytes 6291456 | tf_op jit(solution)/shard_map/all_to_all | solution.py:318
  336.4 2.8 fusion.34.refs_0_
  339.2 82.3 %send_rows_4.1 = bf16[3,1024,512]{2,1,0:T(8,128)(2,1)S(1)} custom-call(bf16[96,512]{1,0:T(8,128)(2,1)S(1)} %fusion.34.refs_0_, f32[2,4,4,4,3,8,128]{6,5,4,3,2,1,0:T(8,128)S(1)} %copy-done.9), custom_call_target="tpu_custom_call" | custom-call | flops 30000001024 | bytes 12582912 | tf_op jit(solution)/shard_map/send_rows_4/pallas_call | solution.py:232
  425.2 2.4 multiply_convert_fusion.1
  436.1 4.8 fusion.63
  440.9 7.1 %all-to-all-start.4 = ((f32[128,1,48]{2,1,0:T(1,128)}), f32[128,1,48]{2,1,0:T(1,128)S(1)}, u32[]{:S(2)}, u32[]{:S(2)}) async-start(f32[128,1,48]{2,1,0:T(1,128)} %copy.120), calls=%async_computation.4 | async-start | bytes 131072 | tf_op jit(solution)/shard_map/all_to_all | solution.py:356
  448.0 4.1 fusion.5
  454.0 3.8 all-to-all-done.4
  458.4 6.4 %all-to-all-start.3 = ((bf16[128,24,512]{2,1,0:T(8,128)(2,1)}), bf16[128,24,512]{2,1,0:T(8,128)(2,1)}, u32[]{:S(2)}, u32[]{:S(2)}) async-start(bf16[128,24,512]{2,1,0:T(8,128)(2,1)} %bitcast.131), calls=%async_computation.3 | async-start | bytes 6291456 | tf_op jit(solution)/shard_map/all_to_all | solution.py:318
  464.8 3.3 fusion.66
  470.2 2.1 fusion.10
  472.4 3.1 fusion.22
  480.6 2.2 fusion.6
  486.1 26.6 %all-to-all-done.3 = bf16[128,24,512]{2,1,0:T(8,128)(2,1)} async-done(((bf16[128,24,512]{2,1,0:T(8,128)(2,1)}), bf16[128,24,512]{2,1,0:T(8,128)(2,1)}, u32[]{:S(2)}, u32[]{:S(2)}) %all-to-all-start.3) | async-done | bytes 3145760 | tf_op jit(solution)/shard_map/all_to_all | solution.py:318
  512.8 3.2 fusion.35
  (198 shorter events, 67.2 us)
Async XLA Ops:
  0.6 211.7 %copy-start = (bf16[3,512,128]{2,1,0:T(8,128)(2,1)S(1)}, bf16[3,512,128]{2,1,0:T(8,128)(2,1)}, u32[]{:S(2)}) copy-start(bf16[3,512,128]{2,1,0:T(8,128)(2,1)} %param.22) | copy-start | bytes 1179652
  8.6 54.0 %copy-start.25 = (bf16[3,512,128]{2,1,0:T(8,128)(2,1)S(1)}, bf16[3,512,128]{2,1,0:T(8,128)(2,1)}, u32[]{:S(2)}) copy-start(bf16[3,512,128]{2,1,0:T(8,128)(2,1)} %param.18) | copy-start | bytes 1179652
  73.5 5.0 copy-start.47
  73.5 5.1 copy-start.46
  73.5 5.2 %copy-start.6 = (f32[2,4,4,4,3,8,128]{6,5,4,3,2,1,0:T(8,128)S(1)}, f32[2,4,4,4,3,8,128]{6,5,4,3,2,1,0:T(8,128)}, u32[]{:S(2)}) copy-start(f32[2,4,4,4,3,8,128]{6,5,4,3,2,1,0:T(8,128)} %copy-done.5) | copy-start | bytes 4718596
  73.5 90.4 %all-to-all-start = ((bf16[128,24,512]{2,1,0:T(8,128)(2,1)}), bf16[128,24,512]{2,1,0:T(8,128)(2,1)}, u32[]{:S(2)}, u32[]{:S(2)}) async-start(bf16[128,24,512]{2,1,0:T(8,128)(2,1)} %bitcast.130), calls=%async_computation | async-start | bytes 6291456 | tf_op jit(solution)/shard_map/all_to_all | solution.py:318
  92.7 11.4 %copy-start.34 = (f32[128,8,32]{2,1,0:T(8,128)S(1)}, f32[128,8,32]{2,1,0:T(8,128)}, u32[]{:S(2)}) copy-start(f32[128,8,32]{2,1,0:T(8,128)} %get-tuple-element.69) | copy-start | bytes 393220
  92.7 11.4 %copy-start.35 = (f32[128,8,32]{2,1,0:T(8,128)S(1)}, f32[128,8,32]{2,1,0:T(8,128)}, u32[]{:S(2)}) copy-start(f32[128,8,32]{2,1,0:T(8,128)} %get-tuple-element.70) | copy-start | bytes 393220
  92.7 11.4 %copy-start.36 = (f32[128,8,32]{2,1,0:T(8,128)S(1)}, f32[128,8,32]{2,1,0:T(8,128)}, u32[]{:S(2)}) copy-start(f32[128,8,32]{2,1,0:T(8,128)} %get-tuple-element.71) | copy-start | bytes 393220
  105.2 10.8 %copy-start.17 = (bf16[96,512]{1,0:T(8,128)(2,1)S(1)}, bf16[96,512]{1,0:T(8,128)(2,1)}, u32[]{:S(2)}) copy-start(bf16[96,512]{1,0:T(8,128)(2,1)} %refs_0_.3) | copy-start | bytes 294916
  116.0 47.9 %copy-start.43 = (bf16[96,3072]{1,0:T(8,128)(2,1)S(1)}, bf16[96,3072]{1,0:T(8,128)(2,1)}, u32[]{:S(2)}) copy-start(bf16[96,3072]{1,0:T(8,128)(2,1)} %get-tuple-element.75) | copy-start | bytes 1769476
  116.0 47.9 %copy-start.44 = (bf16[96,3072]{1,0:T(8,128)(2,1)S(1)}, bf16[96,3072]{1,0:T(8,128)(2,1)}, u32[]{:S(2)}) copy-start(bf16[96,3072]{1,0:T(8,128)(2,1)} %get-tuple-element.76) | copy-start | bytes 1769476
  167.3 42.9 %copy-start.10 = (bf16[96,512]{1,0:T(8,128)(2,1)}, bf16[96,512]{1,0:T(8,128)(2,1)S(1)}, u32[]{:S(2)}) copy-start(bf16[96,512]{1,0:T(8,128)(2,1)S(1)} %fusion.51.refs_0_) | copy-start | bytes 294916
  167.3 42.9 %copy-start.24 = (bf16[3,512,128]{2,1,0:T(8,128)(2,1)S(1)}, bf16[3,512,128]{2,1,0:T(8,128)(2,1)}, u32[]{:S(2)}) copy-start(bf16[3,512,128]{2,1,0:T(8,128)(2,1)} %param.21) | copy-start | bytes 1179652
  231.9 7.2 %copy-start.16 = (bf16[96,512]{1,0:T(8,128)(2,1)S(1)}, bf16[96,512]{1,0:T(8,128)(2,1)}, u32[]{:S(2)}) copy-start(bf16[96,512]{1,0:T(8,128)(2,1)} %refs_0_.4) | copy-start | bytes 294916
  231.9 94.0 %all-to-all-start.2 = ((bf16[128,24,512]{2,1,0:T(8,128)(2,1)}), bf16[128,24,512]{2,1,0:T(8,128)(2,1)}, u32[]{:S(2)}, u32[]{:S(2)}) async-start(bf16[128,24,512]{2,1,0:T(8,128)(2,1)} %bitcast.132), calls=%async_computation.2 | async-start | bytes 6291456 | tf_op jit(solution)/shard_map/all_to_all | solution.py:318
  240.5 81.4 %copy-start.26 = (bf16[3,512,128]{2,1,0:T(8,128)(2,1)S(1)}, bf16[3,512,128]{2,1,0:T(8,128)(2,1)}, u32[]{:S(2)}) copy-start(bf16[3,512,128]{2,1,0:T(8,128)(2,1)} %param.18) | copy-start | bytes 1179652
  325.9 10.5 %copy-start.18 = (bf16[96,512]{1,0:T(8,128)(2,1)S(1)}, bf16[96,512]{1,0:T(8,128)(2,1)}, u32[]{:S(2)}) copy-start(bf16[96,512]{1,0:T(8,128)(2,1)} %refs_0_.3) | copy-start | bytes 294916
  325.9 115.0 %all-to-all-start.1 = ((bf16[128,24,512]{2,1,0:T(8,128)(2,1)}), bf16[128,24,512]{2,1,0:T(8,128)(2,1)}, u32[]{:S(2)}, u32[]{:S(2)}) async-start(bf16[128,24,512]{2,1,0:T(8,128)(2,1)} %copy_bitcast_fusion.2), calls=%async_computation.1 | async-start | bytes 6291456 | tf_op jit(solution)/shard_map/all_to_all | solution.py:318
  339.2 82.4 %copy-start.12 = (bf16[96,512]{1,0:T(8,128)(2,1)}, bf16[96,512]{1,0:T(8,128)(2,1)S(1)}, u32[]{:S(2)}) copy-start(bf16[96,512]{1,0:T(8,128)(2,1)S(1)} %fusion.34.refs_0_) | copy-start | bytes 294916
  339.2 82.4 %copy-start.50 = (f32[3,1024]{1,0:T(4,128)S(1)}, f32[3,1024]{1,0:T(4,128)}, u32[]{:S(2)}) copy-start(f32[3,1024]{1,0:T(4,128)} %mul.126) | copy-start | bytes 36868
  339.2 82.4 %copy-start.59 = (bf16[3,128,512]{2,1,0:T(8,128)(2,1)S(1)}, bf16[3,128,512]{2,1,0:T(8,128)(2,1)}, u32[]{:S(2)}) copy-start(bf16[3,128,512]{2,1,0:T(8,128)(2,1)} %param.20) | copy-start | bytes 1179652
  421.6 6.0 %copy-start.22 = (bf16[3,1024,512]{2,1,0:T(8,128)(2,1)}, bf16[3,1024,512]{2,1,0:T(8,128)(2,1)S(1)}, u32[]{:S(2)}) copy-start(bf16[3,1024,512]{2,1,0:T(8,128)(2,1)S(1)} %send_rows_4.1) | copy-start | bytes 9437188
  427.6 8.5 %copy-start.27 = (bf16[3,512,128]{2,1,0:T(8,128)(2,1)S(1)}, bf16[3,512,128]{2,1,0:T(8,128)(2,1)}, u32[]{:S(2)}) copy-start(bf16[3,512,128]{2,1,0:T(8,128)(2,1)} %param.18) | copy-start | bytes 1179652
  440.9 16.9 %all-to-all-start.4 = ((f32[128,1,48]{2,1,0:T(1,128)}), f32[128,1,48]{2,1,0:T(1,128)S(1)}, u32[]{:S(2)}, u32[]{:S(2)}) async-start(f32[128,1,48]{2,1,0:T(1,128)} %copy.120), calls=%async_computation.4 | async-start | bytes 131072 | tf_op jit(solution)/shard_map/all_to_all | solution.py:356
  458.4 54.3 %all-to-all-start.3 = ((bf16[128,24,512]{2,1,0:T(8,128)(2,1)}), bf16[128,24,512]{2,1,0:T(8,128)(2,1)}, u32[]{:S(2)}, u32[]{:S(2)}) async-start(bf16[128,24,512]{2,1,0:T(8,128)(2,1)} %bitcast.131), calls=%async_computation.3 | async-start | bytes 6291456 | tf_op jit(solution)/shard_map/all_to_all | solution.py:318
  472.4 3.9 copy-start.4
  480.6 4.0 copy-start.54
  480.6 4.0 copy-start.55
  480.6 32.2 %copy-start.13 = (bf16[96,512]{1,0:T(8,128)(2,1)S(1)}, bf16[96,512]{1,0:T(8,128)(2,1)}, u32[]{:S(2)}) copy-start(bf16[96,512]{1,0:T(8,128)(2,1)} %copy-done.12) | copy-start | bytes 294916
  480.6 32.1 %copy-start.33 = (bf16[96,3072]{1,0:T(8,128)(2,1)S(1)}, bf16[96,3072]{1,0:T(8,128)(2,1)}, u32[]{:S(2)}) copy-start(bf16[96,3072]{1,0:T(8,128)(2,1)} %get-tuple-element.50) | copy-start | bytes 1769476
  480.6 35.3 %copy-start.1 = (bf16[3,512,128]{2,1,0:T(8,128)(2,1)S(1)}, bf16[3,512,128]{2,1,0:T(8,128)(2,1)}, u32[]{:S(2)}) copy-start(bf16[3,512,128]{2,1,0:T(8,128)(2,1)} %param.22) | copy-start | bytes 1179652
  (37 other events, 84.4 us)

commit v4 on v3

--- a/solution.py
+++ b/solution.py
@@ -20,27 +20,16 @@
     return (flat * capacity + slot).reshape(ids.shape)
 
 
-def pair_weight(rows, gates, total):
-    hit = rows[:, :, None] == jnp.arange(total, dtype=jnp.int32)[None, None, :]
-    return jnp.sum(jnp.where(hit, gates[:, :, None], 0.0), axis=1)
-
-
-def split3(w):
-    hi = lax.reduce_precision(w, 8, 7)
-    mid = lax.reduce_precision(w - hi, 8, 7)
-    low = w - hi - mid
-    return jnp.concatenate([hi.astype(BF16), mid.astype(BF16), low.astype(BF16)], axis=0)
-
-
 SIDE = 4
 
 
-def send_kernel(own, capacity, layer, plus, first, *refs):
+def send_kernel(own, capacity, layer, plus, first, scaled, *refs):
     if first:
         x_ref, tile_ref, u_ref, table_ref, held, local_sem, send_sem, recv_sem, tiles = refs
+    elif scaled:
+        x_ref, tiles, u_ref, q_ref, held, local_sem, send_sem, recv_sem = refs
     else:
-        x_ref, table_ref, u_ref, held, local_sem, send_sem, recv_sem = refs
-        tiles = table_ref
+        x_ref, tiles, u_ref, held, local_sem, send_sem, recv_sem = refs
     me = lax.axis_index("ep")
     core = lax.rem(me, 2)
     chip = lax.div(me, 2)
@@ -56,16 +45,20 @@
     partner = chip * 2 + (1 - core)
 
     def region(part, pos, span):
+        if span[1] == 0:
+            return None
         idx = [pos[d] if d in pos else at[d] for d in range(3)]
         idx = [pl.ds(0, SIDE) if i is None else i for i in idx]
         where = (core, idx[2], idx[1], idx[0])
-        return held.at[where + (pl.ds(part * third + span[0], span[1]),)], where + (part,)
+        return held.at[where + (pl.ds(part * third + span[0], span[1]),)], where + (pl.ds(part, 2 if part == 2 else 1),)
 
     copies = {}
 
     def start(key, refs, to, with_tile):
+        if refs is None:
+            return
         for kind, ref in (("x", refs[0]), ("t", tiles.at[refs[1]])):
-            if kind == "t" and not (first and with_tile) or ref.shape[-2] == 0:
+            if kind == "t" and not (first and with_tile):
                 continue
             n = len(copies)
             copy = pltpu.make_async_remote_copy(src_ref=ref, dst_ref=ref, send_sem=send_sem.at[n], recv_sem=recv_sem.at[n], device_id={"ep": to}, device_id_type=pl.DeviceIdType.MESH)
@@ -129,18 +122,26 @@
 
     def pick(offsets):
         x, y, z = (lax.rem(at[d] + offsets[d] + SIDE, SIDE) for d in range(3))
-        rows = []
+        rows, scaled_rows = [], []
         for c in range(2):
             code = tiles[c, z, y, x, layer].astype(jnp.int32)
+            gate = tiles[c, z, y, x, 2 + layer] if scaled else None
             hit = code[0:1, :] == slot
+            weight = jnp.where(hit, gate[0:1, :], 0.0) if scaled else None
             for j in range(1, code.shape[0]):
-                hit = hit | (code[j:j + 1, :] == slot)
+                hit_j = code[j:j + 1, :] == slot
+                hit = hit | hit_j
+                if scaled:
+                    weight = jnp.where(hit_j, gate[j:j + 1, :], weight)
             onehot = jnp.where(hit, 1.0, 0.0)[:, :tok_dev].astype(BF16)
             rows.append(jnp.dot(onehot, held[c, z, y, x], preferred_element_type=F32))
+            if scaled:
+                scaled_rows.append(jnp.sum(weight, axis=1, keepdims=True) * rows[-1])
         place = ((z * SIDE + y) * SIDE + x) * 2 * capacity
-        for e in range(own):
-            both = jnp.concatenate([r[e * capacity:(e + 1) * capacity] for r in rows], axis=0)
-            u_ref[e, pl.ds(pl.multiple_of(place, 2 * capacity), 2 * capacity), :] = both.astype(BF16)
+        for out_ref, parts in ((u_ref, rows),) + (((q_ref, scaled_rows),) if scaled else ()):
+            for e in range(own):
+                both = jnp.concatenate([r[e * capacity:(e + 1) * capacity] for r in parts], axis=0)
+                out_ref[e, pl.ds(pl.multiple_of(place, 2 * capacity), 2 * capacity), :] = both.astype(BF16)
 
     def near_rows(step, carry):
         for k in (-1, 0, 1):
@@ -180,6 +181,7 @@
             arrive("f1", part, way)
         for way in (1, -1):
             start(("m2", part, way), row_of(part, 0, 0), device(d2, way), True)
+    for part in range(3):
         whole_row(part, 0)
     for part in range(3):
         d2 = dims(part)[1]
@@ -221,19 +223,20 @@
         copy.wait_send()
 
 
-def send_rows(x, table, layer, own, capacity, call_id, plus, first=False):
+def send_rows(x, table, layer, own, capacity, call_id, plus, first=False, scaled=False):
     tok_dev, width = x.shape
     devices = 2 * SIDE ** 3
     count = 240 if first else 120
     u_shape = jax.ShapeDtypeStruct((own, devices * capacity, width), x.dtype)
-    table_shape = jax.ShapeDtypeStruct((2, SIDE, SIDE, SIDE, 3, 8, 128), F32)
+    table_shape = jax.ShapeDtypeStruct((2, SIDE, SIDE, SIDE, 4, 8, 128), F32)
+    outs = (u_shape, table_shape) if first else (u_shape, u_shape) if scaled else (u_shape,)
     vmem = pl.BlockSpec(memory_space=pltpu.VMEM)
     hbm = pl.BlockSpec(memory_space=pl.ANY)
     return pl.pallas_call(
-        functools.partial(send_kernel, own, capacity, layer, plus, first),
-        out_shape=(u_shape, table_shape) if first else u_shape,
+        functools.partial(send_kernel, own, capacity, layer, plus, first, scaled),
+        out_shape=outs,
         in_specs=[hbm, hbm if first else vmem],
-        out_specs=(vmem, vmem) if first else vmem,
+        out_specs=(vmem,) * len(outs),
         scratch_shapes=[
             pltpu.VMEM((2, SIDE, SIDE, SIDE, tok_dev, width), x.dtype),
             pltpu.SemaphoreType.DMA,
@@ -246,6 +249,42 @@
     )(x, table)
 
 
+def combine_kernel(gated, x_ref, row_ref, gate_ref, back_ref, out_ref):
+    tok_dev, width = x_ref.shape
+    chunk = 512
+    codes, gates = row_ref[...], gate_ref[...]
+    total = jnp.zeros((tok_dev, width), F32)
+    for base in range(0, back_ref.shape[0], chunk):
+        lane = lax.broadcasted_iota(jnp.int32, (tok_dev, chunk), 1) + base
+        weight = jnp.zeros((tok_dev, chunk), F32)
+        for j in range(codes.shape[1]):
+            weight = jnp.where(codes[:, j:j + 1] == lane, gates[:, j:j + 1] if gated else 1.0, weight)
+        hi = weight.astype(BF16)
+        terms = [hi]
+        if gated:
+            rest = weight - hi.astype(F32)
+            mid = rest.astype(BF16)
+            terms += [mid, (rest - mid.astype(F32)).astype(BF16)]
+        part = jnp.dot(jnp.concatenate(terms, axis=0), back_ref[pl.ds(base, chunk), :], preferred_element_type=F32)
+        for k in reversed(range(len(terms))):
+            total = total + part[k * tok_dev:(k + 1) * tok_dev]
+    out_ref[...] = (x_ref[...].astype(F32) + total).astype(out_ref.dtype)
+
+
+def combine(x, rows, gates, back, gated):
+    tok_dev, width = x.shape
+    flops = 2 * tok_dev * back.shape[0] * width
+    return pl.pallas_call(
+        functools.partial(combine_kernel, gated),
+        out_shape=jax.ShapeDtypeStruct(x.shape, x.dtype),
+        in_specs=[pl.BlockSpec(memory_space=pltpu.VMEM)] * 4,
+        out_specs=pl.BlockSpec(memory_space=pltpu.VMEM),
+        compiler_params=pltpu.CompilerParams(vmem_limit_bytes=24 * 1024 * 1024),
+        cost_estimate=pl.CostEstimate(flops=flops * (3 if gated else 1), bytes_accessed=back.size * 2, transcendentals=0),
+        name="combine",
+    )(x, rows, gates, back)
+
+
 def home_order(rows, n_group):
     own, count, width = rows.shape
     rows = rows.reshape(own, n_group, count // n_group, width).transpose(1, 0, 2, 3)
@@ -260,10 +299,9 @@
     return pre_gate, pre_up, hidden, out_rows
 
 
-def expert_backward(u_rows, dy_rows, gate_rows, w_gate, w_up, w_down):
+def expert_backward(u_rows, dy_rows, d_out, w_gate, w_up, w_down):
     pre_gate, pre_up, hidden, out_rows = expert_forward(u_rows, w_gate, w_up, w_down)
     dgate_rows = jnp.einsum("erd,erd->er", dy_rows, out_rows, preferred_element_type=F32)
-    d_out = (gate_rows[:, :, None] * dy_rows).astype(BF16)
     dw_down = jnp.einsum("erf,erd->efd", hidden, d_out, preferred_element_type=F32)
     d_hidden = jnp.einsum("erd,efd->erf", d_out, w_down, preferred_element_type=F32)
     gate_sig = jax.nn.sigmoid(pre_gate)
@@ -290,44 +328,15 @@
 
         rows_a = pair_rows(idx_a, capacity)
         rows_b = pair_rows(idx_b, capacity)
-        lanes = [rows_a.T.astype(F32), rows_b.T.astype(F32), gate_a.T]
-        rest = gate_b.T
-        cut = 128 - tok_dev
-        tile = jnp.stack([jnp.concatenate([lanes[i], rest[:, i * cut:(i + 1) * cut]], axis=1) for i in range(3)])
+        pad = ((0, 0), (0, 128 - tok_dev))
+        tile = jnp.stack([jnp.pad(rows_a.T.astype(F32), pad, constant_values=-1.0), jnp.pad(rows_b.T.astype(F32), pad, constant_values=-1.0), jnp.pad(gate_a.T, pad), jnp.pad(gate_b.T, pad)])
         third = tok_dev // 3
         even = third // 2
-        u_a, table = send_rows(x_in, tile, 0, own, capacity, 0, even, True)
-        by_device = table.reshape(2, n_group // 2, 3, 8, 128).transpose(1, 0, 2, 3, 4).reshape(n_group, 3, 8, 128)
-        mine = (lax.axis_index("ep") * block + jnp.arange(block, dtype=jnp.int32)).astype(F32)
-
-        def far_gates(code, gates):
-            hit = code[:, None] == mine[None, :, None, None]
-            gates = jnp.sum(jnp.where(hit, gates[:, None], 0.0), axis=(2, 3))
-            return gates.reshape(n_group, own, capacity).transpose(1, 0, 2).reshape(own, -1)
-
-        far_gate_a = far_gates(by_device[:, 0, :, :tok_dev], by_device[:, 2, :, :tok_dev])
-        spread_b = jnp.concatenate([by_device[:, i, :, tok_dev:] for i in range(3)], axis=2)
-        far_gate_b = far_gates(by_device[:, 1, :, :tok_dev], spread_b)
-        weight_a = split3(pair_weight(rows_a, gate_a, total))
-        weight_b = split3(pair_weight(rows_b, gate_b, total))
-        ones = jnp.ones_like(gate_a)
-        pick_a = pair_weight(rows_a, ones, total).astype(BF16)
-        pick_b = pair_weight(rows_b, ones, total).astype(BF16)
+        u_a, table = send_rows(x_in, tile, 0, own, capacity, 0, even, first=True)
 
         def send_back(rows):
             back = lax.all_to_all(home_order(rows, n_group), "ep", 0, 0, tiled=True)
             return back.reshape(total, width)
-
-        def combine(x_rows, back, weight):
-            branch = jnp.dot(weight, back, preferred_element_type=F32).reshape(3, tok_dev, width)
-            branch = branch[0] + (branch[1] + branch[2])
-            return (x_rows.astype(F32) + branch).astype(BF16)
-
-        def layer_backward(dy_rows, dy_sent, u_rows, gates, pick, w_gate, w_up, w_down):
-            du_rows, dgate_rows, dw_gate, dw_up, dw_down = expert_backward(u_rows, dy_sent, gates, w_gate, w_up, w_down)
-            branch = jnp.dot(pick, send_back(du_rows), preferred_element_type=F32)
-            dx_rows = (dy_rows.astype(F32) + branch).astype(BF16)
-            return dx_rows, dgate_rows, (dw_gate, dw_up, dw_down)
 
         def by_home(dgate_rows):
             return dgate_rows.reshape(own, n_group, capacity).transpose(1, 0, 2).reshape(n_group, block)
@@ -341,21 +350,23 @@
 
         out_a = expert_forward(u_a, w1_a, w3_a, w2_a)[3]
         back_a = send_back(out_a)
-        dy_b = send_rows(dy_out, table, 1, own, capacity, 1, 0)
-        x_mid = combine(x_in, back_a, weight_a)
-        u_b = send_rows(x_mid, table, 1, own, capacity, 2, even)
+        dy_b, q_b = send_rows(dy_out, table, 1, own, capacity, 1, third, scaled=True)
+        x_mid = combine(x_in, rows_a, gate_a, back_a, True)
+        u_b, = send_rows(x_mid, table, 1, own, capacity, 2, even)
         out_b = expert_forward(u_b, w1_b, w3_b, w2_b)[3]
-        x_out = combine(x_mid, send_back(out_b), weight_b)
         u_keep, dy_b, _ = lax.optimization_barrier((u_b, dy_b, out_b))
-        dx_mid, dgate_rows_b, grads_b = layer_backward(dy_out, dy_b, u_keep, far_gate_b, pick_b, w1_b, w3_b, w2_b)
+        du_b, dgate_rows_b, *grads_b = expert_backward(u_keep, dy_b, q_b, w1_b, w3_b, w2_b)
         x_again, _ = lax.optimization_barrier((x_in, out_b))
-        u_again = send_rows(x_again, table, 0, own, capacity, 3, 0)
-        dy_a = send_rows(dx_mid, table, 0, own, capacity, 4, 0)
-        dx_in, dgate_rows_a, grads_a = layer_backward(dx_mid, dy_a, u_again, far_gate_a, pick_a, w1_a, w3_a, w2_a)
+        u_again, = send_rows(x_again, table, 0, own, capacity, 3, third)
+        dx_mid = combine(dy_out, rows_b, gate_b, send_back(du_b), False)
+        dy_a, q_a = send_rows(dx_mid, table, 0, own, capacity, 4, third, scaled=True)
+        x_out = combine(x_mid, rows_b, gate_b, send_back(out_b), True)
+        du_a, dgate_rows_a, *grads_a = expert_backward(u_again, dy_a, q_a, w1_a, w3_a, w2_a)
+        dx_in = combine(dx_mid, rows_a, gate_a, send_back(du_a), False)
         dgates = jnp.concatenate([by_home(dgate_rows_a), by_home(dgate_rows_b)], axis=1)
         dgates = lax.all_to_all(dgates, "ep", 0, 0, tiled=True)
         dgate_a = look_up(dgates[:, :block], rows_a)
         dgate_b = look_up(dgates[:, block:], rows_b)
-        return (x_out, dx_in) + grads_a + grads_b + (dgate_a, dgate_b)
+        return (x_out, dx_in) + tuple(grads_a) + tuple(grads_b) + (dgate_a, dgate_b)
 
     return jax.shard_map(device_program, mesh=mesh, in_specs=(tok_spec,) * 6 + (w_spec,) * 6, out_specs=(tok_spec,) * 10, check_vma=False)

time: 523 us -> 513 us (0.981)
  Pallas kernels: 304 us -> 346 us
  other arithmetic: 34.5 us -> 3.45 us
  matrix products: 68.2 us -> 56.1 us
    pallas_call x5, Pallas kernels: 304 us -> 334 us  [send_rows(): pl.pallas_call(functools.partial(send_kernel, own, capacity, layer, plus,...]
    reduce_sum x3 -> x0, other arithmetic: 23 us -> none  [the longest x2 19.6 us: pair_weight(): return jnp.sum(jnp.where(hit, gates[:, :, None], 0.0), axis=1)]
    dot_general x4 -> x0, matrix products: 12.3 us -> none  [the longest x2 6.37 us: combine(): jnp.dot(weight, back, preferred_element_type=F32).reshape(3, tok_dev, width)]
    pallas_call x0 -> x4, Pallas kernels: none -> 12.1 us  [combine(): pl.pallas_call(functools.partial(combine_kernel, gated), out_shape=jax.Sh...]
    unnamed x134 -> x126, local copies, waits for them, and re-layouts: 15.1 us -> 24.8 us
    reshape x4 -> x0, local copies, waits for them, and re-layouts: 7.56 us -> none  [the longest x3 7.44 us: home_order(): rows.reshape(own, n_group, count // n_group, width).transpose(1, 0, 2, 3)]
    transpose x2 -> x3, local copies, waits for them, and re-layouts: 0.24 us -> 7.43 us  [home_order(): rows.reshape(own, n_group, count // n_group, width).transpose(1, 0, 2, 3)]
  transfers between devices with their start and end apart: 5 -> 5, of which waited for: 2 -> 2; matrix products, arithmetic and copies ran while one was open for 17% -> 8% of each run, Pallas kernels for 40% -> 49%
where the time goes in v4:
time: 513 us; the launch traced here: 506 us
  Pallas kernels  346 us (67%)
  matrix products  56.1 us (11%)
  local copies, waits for them, and re-layouts  38.7 us (8%)
  starting transfers between devices  34 us (7%)
  waiting for transfers between devices  26.1 us (5%)
    pallas_call x5, Pallas kernels, send_rows(): pl.pallas_call(functools.partial(send_kernel, own, capacity, layer, plus,...  334 us
    all_to_all x4, starting transfers between devices, send_back(): back = lax.all_to_all(home_order(rows, n_group), 'ep', 0, 0, tiled=True)  28.4 us
    unnamed x126, local copies, waits for them, and re-layouts  24.8 us
    all_to_all x4, waiting for transfers between devices, send_back(): back = lax.all_to_all(home_order(rows, n_group), 'ep', 0, 0, tiled=True)  22.3 us
    pallas_call x4, Pallas kernels, combine(): pl.pallas_call(functools.partial(combine_kernel, gated), out_shape=jax.Sh...  12.1 us
    dot_general x4, matrix products, expert_forward(): jnp.einsum('erf,efd->erd', hidden, w_down, preferred_element_type=F32)  12.1 us
  transfers between devices with their start and end apart: 5, of which 2 were waited for; matrix products, arithmetic and copies ran while one was open for 8% of the time, Pallas kernels for 49%

profile of v4, /device:TPU:1, one launch (start us, length us, event | category | flops | bytes accessed | tf_op | source)
XLA Modules:
  0.0 505.9 jit_solution(2599898174121281159)
XLA Ops:
  8.6 50.8 %send_rows_0.1 = (bf16[3,1024,512]{2,1,0:T(8,128)(2,1)S(1)}, f32[2,4,4,4,4,8,128]{6,5,4,3,2,1,0:T(8,128)S(1)}) custom-call(bf16[96,512]{1,0:T(8,128)(2,1)S(1)} %copy-done.18, f32[4,8,128]{2,1,0:T(8,128)S(1)} %pad_maximum_fusion.refs_1_), custom_call_target="tpu_custom_call" | custom-call | flops 30000001024 | bytes 12582912 | tf_op jit(solution)/shard_map/send_rows_0/pallas_call | solution.py:235
  60.7 2.2 fusion.21
  62.9 5.1 %convert_bitcast_fusion = bf16[128,3,8,512]{3,2,0,1:T(8,128)(2,1)} fusion(bf16[3,128,512]{2,1,0:T(8,128)(2,1)} %param.20, f32[3,1024,128]{2,1,0:T(8,128)} %fusion.21, bf16[3,1024,512]{2,1,0:T(8,128)(2,1)S(1)} %get-tuple-element.19, bf16[3,512,128]{2,1,0:T(8,128)(2,1)} %param.19), kind=kOutput, calls=%fused_computation.12 | convolution fusion | flops 809238528 | bytes 8650752 | tf_op jit(solution)/shard_map/erf,efd->erd/dot_general | solution.py:298
  68.0 3.7 copy.173
  71.7 7.1 %all-to-all-start = ((bf16[128,24,512]{2,1,0:T(8,128)(2,1)}), bf16[128,24,512]{2,1,0:T(8,128)(2,1)S(1)}, u32[]{:S(2)}, u32[]{:S(2)}) async-start(bf16[128,24,512]{2,1,0:T(8,128)(2,1)} %bitcast.103), calls=%async_computation | async-start | bytes 6291456 | tf_op jit(solution)/shard_map/all_to_all | solution.py:338
  82.7 79.2 %send_rows_1.1 = (bf16[3,1024,512]{2,1,0:T(8,128)(2,1)S(1)}, bf16[3,1024,512]{2,1,0:T(8,128)(2,1)S(1)}) custom-call(bf16[96,512]{1,0:T(8,128)(2,1)S(1)} %copy-done.21, f32[2,4,4,4,4,8,128]{6,5,4,3,2,1,0:T(8,128)S(1)} %copy-done.26), custom_call_target="tpu_custom_call" | custom-call | flops 30000001024 | bytes 12582912 | tf_op jit(solution)/shard_map/send_rows_1/pallas_call | solution.py:235
  165.3 2.1 fusion.23
  171.5 41.9 %send_rows_2.1 = bf16[3,1024,512]{2,1,0:T(8,128)(2,1)S(1)} custom-call(bf16[96,512]{1,0:T(8,128)(2,1)S(1)} %combine.4.refs_0_.x_ref, f32[2,4,4,4,4,8,128]{6,5,4,3,2,1,0:T(8,128)S(1)} %copy-done.27), custom_call_target="tpu_custom_call" | custom-call | flops 30000001024 | bytes 12582912 | tf_op jit(solution)/shard_map/send_rows_2/pallas_call | solution.py:235
  213.4 2.2 fusion.22
  215.7 4.9 convolution_convert_fusion
  222.7 2.5 multiply_convert_fusion
  228.9 2.3 fusion.25
  234.1 5.7 %all-to-all-start.2 = ((bf16[128,24,512]{2,1,0:T(8,128)(2,1)}), bf16[128,24,512]{2,1,0:T(8,128)(2,1)}, u32[]{:S(2)}, u32[]{:S(2)}) async-start(bf16[128,24,512]{2,1,0:T(8,128)(2,1)} %bitcast.104), calls=%async_computation.2 | async-start | bytes 6291456 | tf_op jit(solution)/shard_map/all_to_all | solution.py:338
  241.4 80.0 %send_rows_3.1 = bf16[3,1024,512]{2,1,0:T(8,128)(2,1)S(1)} custom-call(bf16[96,512]{1,0:T(8,128)(2,1)S(1)} %copy-done.20, f32[2,4,4,4,4,8,128]{6,5,4,3,2,1,0:T(8,128)S(1)} %copy-done.28), custom_call_target="tpu_custom_call" | custom-call | flops 30000001024 | bytes 12582912 | tf_op jit(solution)/shard_map/send_rows_3/pallas_call | solution.py:235
  323.1 2.1 fusion.27
  327.2 8.8 %all-to-all-start.1 = ((bf16[128,24,512]{2,1,0:T(8,128)(2,1)}), bf16[128,24,512]{2,1,0:T(8,128)(2,1)}, u32[]{:S(2)}, u32[]{:S(2)}) async-start(bf16[128,24,512]{2,1,0:T(8,128)(2,1)} %copy_bitcast_fusion.2), calls=%async_computation.1 | async-start | bytes 6291456 | tf_op jit(solution)/shard_map/all_to_all | solution.py:338
  336.0 3.0 combine.6.refs_0_.x_ref
  339.1 81.8 %send_rows_4.1 = (bf16[3,1024,512]{2,1,0:T(8,128)(2,1)S(1)}, bf16[3,1024,512]{2,1,0:T(8,128)(2,1)S(1)}) custom-call(bf16[96,512]{1,0:T(8,128)(2,1)S(1)} %combine.6.refs_0_.x_ref, f32[2,4,4,4,4,8,128]{6,5,4,3,2,1,0:T(8,128)S(1)} %copy-done.29), custom_call_target="tpu_custom_call" | custom-call | flops 30000001024 | bytes 12582912 | tf_op jit(solution)/shard_map/send_rows_4/pallas_call | solution.py:235
  424.5 2.4 multiply_convert_fusion.1
  429.8 4.9 fusion.28
  434.7 5.6 %all-to-all-start.4 = ((f32[128,1,48]{2,1,0:T(1,128)}), f32[128,1,48]{2,1,0:T(1,128)S(1)}, u32[]{:S(2)}, u32[]{:S(2)}) async-start(f32[128,1,48]{2,1,0:T(1,128)} %copy.148), calls=%async_computation.4 | async-start | bytes 131072 | tf_op jit(solution)/shard_map/all_to_all | solution.py:367
  440.3 4.2 fusion.3
  446.3 3.8 all-to-all-done.4
  450.7 6.8 %all-to-all-start.3 = ((bf16[128,24,512]{2,1,0:T(8,128)(2,1)}), bf16[128,24,512]{2,1,0:T(8,128)(2,1)}, u32[]{:S(2)}, u32[]{:S(2)}) async-start(bf16[128,24,512]{2,1,0:T(8,128)(2,1)} %bitcast.102), calls=%async_computation.3 | async-start | bytes 6291456 | tf_op jit(solution)/shard_map/all_to_all | solution.py:338
  457.6 3.7 fusion.34
  461.4 2.1 fusion.32
  463.5 2.1 fusion.33
  465.6 4.0 combine.5
  472.0 2.1 fusion.29
  474.1 2.1 fusion.30
  479.6 22.3 %all-to-all-done.3 = bf16[128,24,512]{2,1,0:T(8,128)(2,1)} async-done(((bf16[128,24,512]{2,1,0:T(8,128)(2,1)}), bf16[128,24,512]{2,1,0:T(8,128)(2,1)}, u32[]{:S(2)}, u32[]{:S(2)}) %all-to-all-start.3) | async-done | bytes 3145760 | tf_op jit(solution)/shard_map/all_to_all | solution.py:338
  501.9 3.5 combine.7
  (172 shorter events, 49.1 us)
Async XLA Ops:
  0.6 215.0 %copy-start = (bf16[3,512,128]{2,1,0:T(8,128)(2,1)S(1)}, bf16[3,512,128]{2,1,0:T(8,128)(2,1)}, u32[]{:S(2)}) copy-start(bf16[3,512,128]{2,1,0:T(8,128)(2,1)} %param.22) | copy-start | bytes 1179652
  8.6 52.2 %copy-start.31 = (bf16[3,512,128]{2,1,0:T(8,128)(2,1)S(1)}, bf16[3,512,128]{2,1,0:T(8,128)(2,1)}, u32[]{:S(2)}) copy-start(bf16[3,512,128]{2,1,0:T(8,128)(2,1)} %param.18) | copy-start | bytes 1179652
  71.7 7.1 %copy-start.58 = (f32[96,8]{0,1:T(8,128)S(1)}, f32[96,8]{0,1:T(8,128)}, u32[]{:S(2)}) copy-start(f32[96,8]{0,1:T(8,128)} %param.15) | copy-start | bytes 9220
  71.7 7.8 %copy-start.59 = (f32[96,8]{0,1:T(8,128)S(1)}, f32[96,8]{0,1:T(8,128)}, u32[]{:S(2)}) copy-start(f32[96,8]{0,1:T(8,128)} %param.16) | copy-start | bytes 9220
  71.7 95.8 %all-to-all-start = ((bf16[128,24,512]{2,1,0:T(8,128)(2,1)}), bf16[128,24,512]{2,1,0:T(8,128)(2,1)S(1)}, u32[]{:S(2)}, u32[]{:S(2)}) async-start(bf16[128,24,512]{2,1,0:T(8,128)(2,1)} %bitcast.103), calls=%async_computation | async-start | bytes 6291456 | tf_op jit(solution)/shard_map/all_to_all | solution.py:338
  82.7 82.6 %copy-start.46 = (bf16[3,128,512]{2,1,0:T(8,128)(2,1)S(1)}, bf16[3,128,512]{2,1,0:T(8,128)(2,1)}, u32[]{:S(2)}) copy-start(bf16[3,128,512]{2,1,0:T(8,128)(2,1)} %param.23) | copy-start | bytes 1179652
  171.5 41.9 %copy-start.14 = (bf16[96,512]{1,0:T(8,128)(2,1)}, bf16[96,512]{1,0:T(8,128)(2,1)S(1)}, u32[]{:S(2)}) copy-start(bf16[96,512]{1,0:T(8,128)(2,1)S(1)} %combine.4.refs_0_.x_ref) | copy-start | bytes 294916
  171.5 41.9 %copy-start.30 = (bf16[3,512,128]{2,1,0:T(8,128)(2,1)S(1)}, bf16[3,512,128]{2,1,0:T(8,128)(2,1)}, u32[]{:S(2)}) copy-start(bf16[3,512,128]{2,1,0:T(8,128)(2,1)} %param.21) | copy-start | bytes 1179652
  234.1 5.7 %copy-start.20 = (bf16[96,512]{1,0:T(8,128)(2,1)S(1)}, bf16[96,512]{1,0:T(8,128)(2,1)}, u32[]{:S(2)}) copy-start(bf16[96,512]{1,0:T(8,128)(2,1)} %refs_0_.4) | copy-start | bytes 294916
  234.1 93.1 %all-to-all-start.2 = ((bf16[128,24,512]{2,1,0:T(8,128)(2,1)}), bf16[128,24,512]{2,1,0:T(8,128)(2,1)}, u32[]{:S(2)}, u32[]{:S(2)}) async-start(bf16[128,24,512]{2,1,0:T(8,128)(2,1)} %bitcast.104), calls=%async_computation.2 | async-start | bytes 6291456 | tf_op jit(solution)/shard_map/all_to_all | solution.py:338
  241.4 81.7 %copy-start.32 = (bf16[3,512,128]{2,1,0:T(8,128)(2,1)S(1)}, bf16[3,512,128]{2,1,0:T(8,128)(2,1)}, u32[]{:S(2)}) copy-start(bf16[3,512,128]{2,1,0:T(8,128)(2,1)} %param.18) | copy-start | bytes 1179652
  327.1 8.9 %copy-start.12 = (s32[96,8]{1,0:T(8,128)S(1)}, s32[96,8]{1,0:T(8,128)}, u32[]{:S(2)}) copy-start(s32[96,8]{1,0:T(8,128)} %get-tuple-element.71.row_ref) | copy-start | bytes 9220
  327.1 8.9 %copy-start.13 = (f32[96,8]{1,0:T(8,128)S(1)}, f32[96,8]{1,0:T(8,128)}, u32[]{:S(2)}) copy-start(f32[96,8]{1,0:T(8,128)} %copy.135.gate_ref) | copy-start | bytes 9220
  327.1 8.9 %copy-start.22 = (bf16[96,512]{1,0:T(8,128)(2,1)S(1)}, bf16[96,512]{1,0:T(8,128)(2,1)}, u32[]{:S(2)}) copy-start(bf16[96,512]{1,0:T(8,128)(2,1)} %x_ref.3) | copy-start | bytes 294916
  327.2 107.5 %all-to-all-start.1 = ((bf16[128,24,512]{2,1,0:T(8,128)(2,1)}), bf16[128,24,512]{2,1,0:T(8,128)(2,1)}, u32[]{:S(2)}, u32[]{:S(2)}) async-start(bf16[128,24,512]{2,1,0:T(8,128)(2,1)} %copy_bitcast_fusion.2), calls=%async_computation.1 | async-start | bytes 6291456 | tf_op jit(solution)/shard_map/all_to_all | solution.py:338
  339.1 81.8 %copy-start.16 = (bf16[96,512]{1,0:T(8,128)(2,1)}, bf16[96,512]{1,0:T(8,128)(2,1)S(1)}, u32[]{:S(2)}) copy-start(bf16[96,512]{1,0:T(8,128)(2,1)S(1)} %combine.6.refs_0_.x_ref) | copy-start | bytes 294916
  339.1 81.9 %copy-start.48 = (bf16[3,128,512]{2,1,0:T(8,128)(2,1)S(1)}, bf16[3,128,512]{2,1,0:T(8,128)(2,1)}, u32[]{:S(2)}) copy-start(bf16[3,128,512]{2,1,0:T(8,128)(2,1)} %param.20) | copy-start | bytes 1179652
  420.9 6.0 %copy-start.6 = (bf16[3,1024,512]{2,1,0:T(8,128)(2,1)}, bf16[3,1024,512]{2,1,0:T(8,128)(2,1)S(1)}, u32[]{:S(2)}) copy-start(bf16[3,1024,512]{2,1,0:T(8,128)(2,1)S(1)} %get-tuple-element.24) | copy-start | bytes 9437188
  421.0 3.5 copy-start.49
  434.7 15.4 %all-to-all-start.4 = ((f32[128,1,48]{2,1,0:T(1,128)}), f32[128,1,48]{2,1,0:T(1,128)S(1)}, u32[]{:S(2)}, u32[]{:S(2)}) async-start(f32[128,1,48]{2,1,0:T(1,128)} %copy.148), calls=%async_computation.4 | async-start | bytes 131072 | tf_op jit(solution)/shard_map/all_to_all | solution.py:367
  450.1 7.4 %copy-start.51 = (s32[768]{0:T(1024)S(1)}, s32[768]{0:T(1024)}, u32[]{:S(2)}) copy-start(s32[768]{0:T(1024)} %copy-done.50) | copy-start | bytes 9220
  450.1 7.4 %copy-start.55 = (s32[768]{0:T(1024)S(1)}, s32[768]{0:T(1024)}, u32[]{:S(2)}) copy-start(s32[768]{0:T(1024)} %copy-done.54) | copy-start | bytes 9220
  450.1 7.5 %copy-start.53 = (s32[768]{0:T(1024)S(1)}, s32[768]{0:T(1024)}, u32[]{:S(2)}) copy-start(s32[768]{0:T(1024)} %copy-done.52) | copy-start | bytes 9220
  450.1 7.5 %copy-start.57 = (s32[768]{0:T(1024)S(1)}, s32[768]{0:T(1024)}, u32[]{:S(2)}) copy-start(s32[768]{0:T(1024)} %copy-done.56) | copy-start | bytes 9220
  450.7 51.2 %all-to-all-start.3 = ((bf16[128,24,512]{2,1,0:T(8,128)(2,1)}), bf16[128,24,512]{2,1,0:T(8,128)(2,1)}, u32[]{:S(2)}, u32[]{:S(2)}) async-start(bf16[128,24,512]{2,1,0:T(8,128)(2,1)} %bitcast.102), calls=%async_computation.3 | async-start | bytes 6291456 | tf_op jit(solution)/shard_map/all_to_all | solution.py:338
  457.6 3.7 copy-start.33
  463.4 6.2 %copy-start.7 = (bf16[3,1024,512]{2,1,0:T(8,128)(2,1)S(1)}, bf16[3,1024,512]{2,1,0:T(8,128)(2,1)}, u32[]{:S(2)}) copy-start(bf16[3,1024,512]{2,1,0:T(8,128)(2,1)} %copy-done.6) | copy-start | bytes 9437188
  463.5 6.2 %copy-start.43 = (bf16[3,1024,128]{2,1,0:T(8,128)(2,1)S(1)}, bf16[3,1024,128]{2,1,0:T(8,128)(2,1)}, u32[]{:S(2)}) copy-start(bf16[3,1024,128]{2,1,0:T(8,128)(2,1)} %copy-done.42) | copy-start | bytes 2359300
  474.1 27.8 %copy-start.9 = (s32[96,8]{1,0:T(8,128)S(1)}, s32[96,8]{1,0:T(8,128)}, u32[]{:S(2)}) copy-start(s32[96,8]{1,0:T(8,128)} %get-tuple-element.69.row_ref) | copy-start | bytes 9220
  474.1 27.8 %copy-start.11 = (f32[96,8]{1,0:T(8,128)S(1)}, f32[96,8]{1,0:T(8,128)}, u32[]{:S(2)}) copy-start(f32[96,8]{1,0:T(8,128)} %copy.133.gate_ref) | copy-start | bytes 9220
  474.1 27.8 %copy-start.17 = (bf16[96,512]{1,0:T(8,128)(2,1)S(1)}, bf16[96,512]{1,0:T(8,128)(2,1)}, u32[]{:S(2)}) copy-start(bf16[96,512]{1,0:T(8,128)(2,1)} %copy-done.16) | copy-start | bytes 294916
  474.1 31.3 %copy-start.1 = (bf16[3,512,128]{2,1,0:T(8,128)(2,1)S(1)}, bf16[3,512,128]{2,1,0:T(8,128)(2,1)}, u32[]{:S(2)}) copy-start(bf16[3,512,128]{2,1,0:T(8,128)(2,1)} %param.22) | copy-start | bytes 1179652
  (33 other events, 57.0 us)

commit v5 on v4

--- a/solution.py
+++ b/solution.py
@@ -78,11 +78,11 @@
         own_tile.wait()
     barrier = pltpu.get_barrier_semaphore()
     for dim in range(3):
-        for step in (1, -1):
+        for step in (1, -1, 2):
             pl.semaphore_signal(barrier, inc=1, device_id={"ep": device(dim, step)}, device_id_type=pl.DeviceIdType.MESH)
     pl.semaphore_signal(barrier, inc=1, device_id={"ep": partner}, device_id_type=pl.DeviceIdType.MESH)
     mine.wait()
-    pl.semaphore_wait(barrier, 7)
+    pl.semaphore_wait(barrier, 10)
 
     def dims(part):
         return part, (part + 1) % 3, (part + 2) % 3
@@ -168,33 +168,25 @@
 
     for part in range(3):
         d1 = dims(part)[0]
-        for way in (1, -1):
+        for way in (2, 1, -1):
             start(("m1", part, way), region(part, {}, whole), device(d1, way), True)
     for part in range(3):
-        d1 = dims(part)[0]
-        for way in (1, -1):
+        d2 = dims(part)[1]
+        for way in (1, -1, 2):
             arrive("m1", part, way)
-            start(("f1", part, way), region(part, {d1: shift(d1, -way)}, spans[way]), device(d1, way), way == -1)
-    for part in range(3):
-        d2 = dims(part)[1]
-        for way in (1, -1):
-            arrive("f1", part, way)
-        for way in (1, -1):
+        for way in (2, 1, -1):
             start(("m2", part, way), row_of(part, 0, 0), device(d2, way), True)
     for part in range(3):
         whole_row(part, 0)
     for part in range(3):
-        d2 = dims(part)[1]
         for way in (1, -1):
             arrive("m2", part, way)
-            start(("f2", part, way), row_of(part, -way, 0, spans[way]), device(d2, way), way == -1)
             whole_row(part, -way)
     for part in range(3):
         for way in (1, -1):
             pass_on(part, 0, way)
     for part in range(3):
-        for way in (1, -1):
-            arrive("f2", part, way)
+        arrive("m2", part, 2)
         whole_row(part, 2)
     for b in (-1, 1):
         for part in range(3):
@@ -226,7 +218,7 @@
 def send_rows(x, table, layer, own, capacity, call_id, plus, first=False, scaled=False):
     tok_dev, width = x.shape
     devices = 2 * SIDE ** 3
-    count = 240 if first else 120
+    count = 228 if first else 114
     u_shape = jax.ShapeDtypeStruct((own, devices * capacity, width), x.dtype)
     table_shape = jax.ShapeDtypeStruct((2, SIDE, SIDE, SIDE, 4, 8, 128), F32)
     outs = (u_shape, table_shape) if first else (u_shape, u_shape) if scaled else (u_shape,)
@@ -285,32 +277,104 @@
     )(x, rows, gates, back)
 
 
-def home_order(rows, n_group):
-    own, count, width = rows.shape
-    rows = rows.reshape(own, n_group, count // n_group, width).transpose(1, 0, 2, 3)
-    return rows.reshape(n_group, -1, width)
-
-
-def expert_forward(u_rows, w_gate, w_up, w_down):
-    pre_gate = jnp.einsum("erd,edf->erf", u_rows, w_gate, preferred_element_type=F32)
-    pre_up = jnp.einsum("erd,edf->erf", u_rows, w_up, preferred_element_type=F32)
-    hidden = (jax.nn.silu(pre_gate) * pre_up).astype(BF16)
-    out_rows = jnp.einsum("erf,efd->erd", hidden, w_down, preferred_element_type=F32).astype(BF16)
-    return pre_gate, pre_up, hidden, out_rows
-
-
-def expert_backward(u_rows, dy_rows, d_out, w_gate, w_up, w_down):
-    pre_gate, pre_up, hidden, out_rows = expert_forward(u_rows, w_gate, w_up, w_down)
-    dgate_rows = jnp.einsum("erd,erd->er", dy_rows, out_rows, preferred_element_type=F32)
-    dw_down = jnp.einsum("erf,erd->efd", hidden, d_out, preferred_element_type=F32)
-    d_hidden = jnp.einsum("erd,efd->erf", d_out, w_down, preferred_element_type=F32)
-    gate_sig = jax.nn.sigmoid(pre_gate)
-    d_pre_gate = (d_hidden * pre_up * gate_sig * (1.0 + pre_gate * (1.0 - gate_sig))).astype(BF16)
-    d_pre_up = (d_hidden * jax.nn.silu(pre_gate)).astype(BF16)
-    dw_gate = jnp.einsum("erd,erf->edf", u_rows, d_pre_gate, preferred_element_type=F32)
-    dw_up = jnp.einsum("erd,erf->edf", u_rows, d_pre_up, preferred_element_type=F32)
-    du_rows = (jnp.einsum("erf,edf->erd", d_pre_gate, w_gate, preferred_element_type=F32) + jnp.einsum("erf,edf->erd", d_pre_up, w_up, preferred_element_type=F32)).astype(BF16)
-    return du_rows, dgate_rows, dw_gate, dw_up, dw_down
+def forward_rows(u, w_both, w_down):
+    ff = w_down.shape[0]
+    pre = jnp.dot(u, w_both, preferred_element_type=F32)
+    pre_gate, pre_up = pre[:, :ff], pre[:, ff:]
+    sig = 1.0 / (1.0 + jnp.exp(-pre_gate))
+    silu = pre_gate * sig
+    hidden = (silu * pre_up).astype(BF16)
+    out = jnp.dot(hidden, w_down, preferred_element_type=F32)
+    return pre_gate, pre_up, sig, silu, hidden, out
+
+
+def store_home(out_ref, step, rows):
+    count, width = rows.shape
+    slots = out_ref.shape[1]
+    sources = count // slots
+    out_ref[pl.ds(step * sources, sources)] = rows.reshape(sources, slots, width).astype(out_ref.dtype)
+
+
+def forward_kernel(chunk, u_ref, w1_ref, w3_ref, w2_ref, out_ref):
+    w_both = jnp.concatenate([w1_ref[0], w3_ref[0]], axis=1)
+
+    def body(step, carry):
+        rows = pl.ds(pl.multiple_of(step * chunk, chunk), chunk)
+        out = forward_rows(u_ref[0, rows, :], w_both, w2_ref[0])[-1]
+        store_home(out_ref, step, out)
+        return carry
+
+    lax.fori_loop(0, u_ref.shape[1] // chunk, body, 0)
+
+
+def backward_kernel(chunk, u_ref, dy_ref, q_ref, w1_ref, w3_ref, w2_ref, du_ref, dgate_ref, hidden_ref, da_ref, db_ref):
+    ff = w2_ref.shape[1]
+    w_both = jnp.concatenate([w1_ref[0], w3_ref[0]], axis=1)
+    last = (((1,), (1,)), ((), ()))
+
+    def body(step, carry):
+        rows = pl.ds(pl.multiple_of(step * chunk, chunk), chunk)
+        pre_gate, pre_up, sig, silu, hidden, out = forward_rows(u_ref[0, rows, :], w_both, w2_ref[0])
+        dgate = jnp.sum(dy_ref[0, rows, :].astype(F32) * out.astype(BF16).astype(F32), axis=1, keepdims=True)
+        diagonal = lax.broadcasted_iota(jnp.int32, (128, 128), 0) == lax.broadcasted_iota(jnp.int32, (128, 128), 1)
+        for k in range(chunk // 128):
+            line = jnp.sum(jnp.where(diagonal, dgate[k * 128:(k + 1) * 128], 0.0), axis=0, keepdims=True)
+            dgate_ref[0, pl.ds(step * (chunk // 128) + k, 1), :] = line
+        d_hidden = lax.dot_general(q_ref[0, rows, :], w2_ref[0], last, preferred_element_type=F32)
+        da = (d_hidden * pre_up * sig * (1.0 + pre_gate * (1.0 - sig))).astype(BF16)
+        db = (d_hidden * silu).astype(BF16)
+        hidden_ref[0, rows, :] = hidden
+        da_ref[0, rows, :] = da
+        db_ref[0, rows, :] = db
+        both = jnp.concatenate([da, db], axis=1)
+        store_home(du_ref, step, lax.dot_general(both, w_both, last, preferred_element_type=F32))
+        return carry
+
+    lax.fori_loop(0, u_ref.shape[1] // chunk, body, 0)
+
+
+def expert_call(kernel, inputs, outs, weights, n_group, name):
+    own, count, width = inputs[0].shape
+    ff = weights[2].shape[1]
+    slots = count // n_group
+
+    def each(shape):
+        return pl.BlockSpec((1,) + shape, lambda e: (e, 0, 0))
+
+    home = (jax.ShapeDtypeStruct((n_group, own * slots, width), BF16), pl.BlockSpec((n_group, slots, width), lambda e: (0, e, 0)))
+    kinds = {
+        "home": home,
+        "gate": (jax.ShapeDtypeStruct((own, count // 128, 128), F32), each((count // 128, 128))),
+        "ff": (jax.ShapeDtypeStruct((own, count, ff), BF16), each((count, ff))),
+    }
+    steps = 3 if len(outs) == 1 else 8
+    return pl.pallas_call(
+        functools.partial(kernel, 256),
+        out_shape=tuple(kinds[k][0] for k in outs),
+        grid=(own,),
+        in_specs=[each((count, width))] * len(inputs) + [each((width, ff)), each((width, ff)), each((ff, width))],
+        out_specs=tuple(kinds[k][1] for k in outs),
+        compiler_params=pltpu.CompilerParams(vmem_limit_bytes=32 * 1024 * 1024),
+        cost_estimate=pl.CostEstimate(flops=2 * steps * own * count * width * ff, bytes_accessed=own * count * width * 2 * (len(inputs) + 1), transcendentals=own * count * ff),
+        name=name,
+    )(*inputs, *weights)
+
+
+def expert_forward(u_rows, weights, n_group):
+    return expert_call(forward_kernel, (u_rows,), ("home",), weights, n_group, "expert_forward")[0]
+
+
+def expert_backward(u_rows, dy_rows, q_rows, weights, n_group):
+    outs = ("home", "gate", "ff", "ff", "ff")
+    du, dgate, hidden, da, db = expert_call(backward_kernel, (u_rows, dy_rows, q_rows), outs, weights, n_group, "expert_backward")
+
+    def grads(u_rows, q_rows, hidden, da, db):
+        dw_gate = jnp.einsum("erd,erf->edf", u_rows, da, preferred_element_type=F32)
+        dw_up = jnp.einsum("erd,erf->edf", u_rows, db, preferred_element_type=F32)
+        dw_down = jnp.einsum("erf,erd->efd", hidden, q_rows, preferred_element_type=F32)
+        return dw_gate, dw_up, dw_down
+
+    return du, dgate, grads(u_rows, q_rows, hidden, da, db)
 
 
 def solution(mesh):
@@ -335,8 +399,7 @@
         u_a, table = send_rows(x_in, tile, 0, own, capacity, 0, even, first=True)
 
         def send_back(rows):
-            back = lax.all_to_all(home_order(rows, n_group), "ep", 0, 0, tiled=True)
-            return back.reshape(total, width)
+            return lax.all_to_all(rows, "ep", 0, 0, tiled=True).reshape(total, width)
 
         def by_home(dgate_rows):
             return dgate_rows.reshape(own, n_group, capacity).transpose(1, 0, 2).reshape(n_group, block)
@@ -348,20 +411,19 @@
             slot = lax.rem(flat, capacity)[:, None] == jnp.arange(capacity, dtype=jnp.int32)[None, :]
             return jnp.sum(jnp.where(slot, picked, 0.0), axis=1).reshape(rows.shape)
 
-        out_a = expert_forward(u_a, w1_a, w3_a, w2_a)[3]
-        back_a = send_back(out_a)
-        dy_b, q_b = send_rows(dy_out, table, 1, own, capacity, 1, third, scaled=True)
+        weights_a, weights_b = (w1_a, w3_a, w2_a), (w1_b, w3_b, w2_b)
+        back_a = send_back(expert_forward(u_a, weights_a, n_group))
+        dy_b, q_b = send_rows(dy_out, table, 1, own, capacity, 1, even, scaled=True)
         x_mid = combine(x_in, rows_a, gate_a, back_a, True)
         u_b, = send_rows(x_mid, table, 1, own, capacity, 2, even)
-        out_b = expert_forward(u_b, w1_b, w3_b, w2_b)[3]
-        u_keep, dy_b, _ = lax.optimization_barrier((u_b, dy_b, out_b))
-        du_b, dgate_rows_b, *grads_b = expert_backward(u_keep, dy_b, q_b, w1_b, w3_b, w2_b)
-        x_again, _ = lax.optimization_barrier((x_in, out_b))
-        u_again, = send_rows(x_again, table, 0, own, capacity, 3, third)
+        out_b = expert_forward(u_b, weights_b, n_group)
+        du_b, dgate_rows_b, grads_b = expert_backward(u_b, dy_b, q_b, weights_b, n_group)
+        x_again, du_b = lax.optimization_barrier((x_in, du_b))
+        u_again, = send_rows(x_again, table, 0, own, capacity, 3, even)
         dx_mid = combine(dy_out, rows_b, gate_b, send_back(du_b), False)
-        dy_a, q_a = send_rows(dx_mid, table, 0, own, capacity, 4, third, scaled=True)
+        dy_a, q_a = send_rows(dx_mid, table, 0, own, capacity, 4, even, scaled=True)
         x_out = combine(x_mid, rows_b, gate_b, send_back(out_b), True)
-        du_a, dgate_rows_a, *grads_a = expert_backward(u_again, dy_a, q_a, w1_a, w3_a, w2_a)
+        du_a, dgate_rows_a, grads_a = expert_backward(u_again, dy_a, q_a, weights_a, n_group)
         dx_in = combine(dx_mid, rows_a, gate_a, send_back(du_a), False)
         dgates = jnp.concatenate([by_home(dgate_rows_a), by_home(dgate_rows_b)], axis=1)
         dgates = lax.all_to_all(dgates, "ep", 0, 0, tiled=True)

time: 513 us -> 475 us (0.926); the launches traced: 506 us -> 473 us
  matrix products: 56.1 us -> 15.2 us
  blocking collectives: 0 us -> 18.4 us
    dot_general x22 -> x6, matrix products: 54.6 us -> 13.7 us  [the longest x2 5.27 us: grads(): jnp.einsum('erf,erd->efd', hidden, q_rows, preferred_element_type=F32)]
    pallas_call x0 -> x4, Pallas kernels: none -> 33.3 us  [expert_call(): pl.pallas_call(functools.partial(kernel, 256), out_shape=tuple((kinds[k][...]
    pallas_call x5, Pallas kernels: 334 us -> 301 us  [send_rows(): pl.pallas_call(functools.partial(send_kernel, own, capacity, layer, plus,...]
    all_to_all x0 -> x1, blocking collectives: none -> 18.4 us  [device_program(): dgates = lax.all_to_all(dgates, 'ep', 0, 0, tiled=True)]
    transpose x3 -> x0, local copies, waits for them, and re-layouts: 7.43 us -> none  [home_order(): rows.reshape(own, n_group, count // n_group, width).transpose(1, 0, 2, 3)]
    all_to_all x5 -> x4, starting transfers between devices: 34 us -> 29.2 us  [send_back(): return lax.all_to_all(rows, 'ep', 0, 0, tiled=True).reshape(total, width)]
    unnamed x126 -> x120, local copies, waits for them, and re-layouts: 24.8 us -> 28.7 us
    all_to_all x5 -> x4, waiting for transfers between devices: 26.1 us -> 22.4 us  [send_back(): return lax.all_to_all(rows, 'ep', 0, 0, tiled=True).reshape(total, width)]
  transfers between devices with their start and end apart: 5 -> 4, of which waited for: 2 -> 1; matrix products, arithmetic and copies ran while one was open for 8% -> 5% of each run, Pallas kernels for 49% -> 50%
where the time goes in v5:
time: 475 us; the launch traced here: 473 us
  Pallas kernels  347 us (73%)
  local copies, waits for them, and re-layouts  36.2 us (8%)
  starting transfers between devices  29.2 us (6%)
  waiting for transfers between devices  22.4 us (5%)
  blocking collectives  18.4 us (4%)
  matrix products  15.2 us (3%)
    pallas_call x5, Pallas kernels, send_rows(): pl.pallas_call(functools.partial(send_kernel, own, capacity, layer, plus,...  301 us
    pallas_call x4, Pallas kernels, expert_call(): pl.pallas_call(functools.partial(kernel, 256), out_shape=tuple((kinds[k][...  33.3 us
    all_to_all x4, starting transfers between devices, send_back(): return lax.all_to_all(rows, 'ep', 0, 0, tiled=True).reshape(total, width)  29.2 us
    unnamed x120, local copies, waits for them, and re-layouts  28.7 us
    all_to_all x4, waiting for transfers between devices, send_back(): return lax.all_to_all(rows, 'ep', 0, 0, tiled=True).reshape(total, width)  22.4 us
    all_to_all x1, blocking collectives, device_program(): dgates = lax.all_to_all(dgates, 'ep', 0, 0, tiled=True)  18.4 us
    pallas_call x4, Pallas kernels, combine(): pl.pallas_call(functools.partial(combine_kernel, gated), out_shape=jax.Sh...  12.1 us
  transfers between devices with their start and end apart: 4, of which 1 were waited for; matrix products, arithmetic and copies ran while one was open for 5% of the time, Pallas kernels for 50%

profile of v5, /device:TPU:1, one launch (start us, length us, event | category | flops | bytes accessed | tf_op | source)
XLA Modules:
  0.0 473.5 jit_solution(15580970129461887409)
XLA Ops:
  8.2 48.5 %send_rows_0.1 = (bf16[3,1024,512]{2,1,0:T(8,128)(2,1)S(1)}, f32[2,4,4,4,4,8,128]{6,5,4,3,2,1,0:T(8,128)S(1)}) custom-call(bf16[96,512]{1,0:T(8,128)(2,1)S(1)} %copy-done.33, f32[4,8,128]{2,1,0:T(8,128)S(1)} %pad_maximum_fusion.refs_1_), custom_call_target="tpu_custom_call" | custom-call | flops 30000001024 | bytes 12582912 | tf_op jit(solution)/shard_map/send_rows_0/pallas_call | solution.py:227
  58.1 7.0 %expert_forward.2 = bf16[128,24,512]{2,1,0:T(8,128)(2,1)} custom-call(bf16[3,1024,512]{2,1,0:T(8,128)(2,1)S(1)} %get-tuple-element.28.u_ref, bf16[3,512,128]{2,1,0:T(8,128)(2,1)S(1)} %copy-done.27, bf16[3,512,128]{2,1,0:T(8,128)(2,1)S(1)} %copy-done.29, bf16[3,128,512]{2,1,0:T(8,128)(2,1)S(1)} %copy-done.31), custom_call_target="tpu_custom_call" | custom-call | flops 1207959552 | bytes 6291456 | tf_op jit(solution)/shard_map/expert_forward/pallas_call | solution.py:351
  65.0 7.4 %all-to-all-start = ((bf16[128,24,512]{2,1,0:T(8,128)(2,1)}), bf16[128,24,512]{2,1,0:T(8,128)(2,1)S(1)}, u32[]{:S(2)}, u32[]{:S(2)}) async-start(bf16[128,24,512]{2,1,0:T(8,128)(2,1)} %expert_forward.2), calls=%async_computation | async-start | bytes 6291456 | tf_op jit(solution)/shard_map/all_to_all | solution.py:402
  72.5 1.6 copy-done.40
  74.1 75.7 %send_rows_1.1 = (bf16[3,1024,512]{2,1,0:T(8,128)(2,1)S(1)}, bf16[3,1024,512]{2,1,0:T(8,128)(2,1)S(1)}) custom-call(bf16[96,512]{1,0:T(8,128)(2,1)S(1)} %copy-done.35, f32[2,4,4,4,4,8,128]{6,5,4,3,2,1,0:T(8,128)S(1)} %copy-done.40), custom_call_target="tpu_custom_call" | custom-call | flops 30000001024 | bytes 12582912 | tf_op jit(solution)/shard_map/send_rows_1/pallas_call | solution.py:227
  149.8 1.6 copy-done.4
  151.4 1.7 copy-done.37
  154.8 40.3 %send_rows_2.1.u_ref = bf16[3,1024,512]{2,1,0:T(8,128)(2,1)S(1)} custom-call(bf16[96,512]{1,0:T(8,128)(2,1)S(1)} %combine.4.refs_0_.x_ref, f32[2,4,4,4,4,8,128]{6,5,4,3,2,1,0:T(8,128)S(1)} %copy-done.41), custom_call_target="tpu_custom_call" | custom-call | flops 30000001024 | bytes 12582912 | tf_op jit(solution)/shard_map/send_rows_2/pallas_call | solution.py:227
  195.1 10.1 %expert_backward.2 = (bf16[128,24,512]{2,1,0:T(8,128)(2,1)S(1)}, f32[3,8,128]{2,1,0:T(8,128)S(1)}, bf16[3,1024,128]{2,1,0:T(8,128)(2,1)S(1)}, bf16[3,1024,128]{2,1,0:T(8,128)(2,1)S(1)}, bf16[3,1024,128]{2,1,0:T(8,128)(2,1)S(1)}) custom-call(bf16[3,1024,512]{2,1,0:T(8,128)(2,1)S(1)} %send_rows_2.1.u_ref, bf16[3,1024,512]{2,1,0:T(8,128)(2,1)S(1)} %copy-done.38, ...), custom_call_target="tpu_custom_call" | custom-call | flops 3221225472 | bytes 12582912 | tf_op jit(solution)/shard_map/expert_backward/pallas_call | solution.py:351
  205.2 1.7 copy-done.9
  209.6 6.3 %all-to-all-start.2 = ((bf16[128,24,512]{2,1,0:T(8,128)(2,1)}), bf16[128,24,512]{2,1,0:T(8,128)(2,1)}, u32[]{:S(2)}, u32[]{:S(2)}) async-start(bf16[128,24,512]{2,1,0:T(8,128)(2,1)} %copy-done.9), calls=%async_computation.2 | async-start | bytes 6291456 | tf_op jit(solution)/shard_map/all_to_all | solution.py:402
  216.8 1.6 copy.127
  221.4 6.1 %expert_forward.3 = bf16[128,24,512]{2,1,0:T(8,128)(2,1)S(1)} custom-call(bf16[3,1024,512]{2,1,0:T(8,128)(2,1)S(1)} %send_rows_2.1.u_ref, bf16[3,512,128]{2,1,0:T(8,128)(2,1)S(1)} %copy-done.22, bf16[3,512,128]{2,1,0:T(8,128)(2,1)S(1)} %copy-done.24, bf16[3,128,512]{2,1,0:T(8,128)(2,1)S(1)} %copy-done.26), custom_call_target="tpu_custom_call" | custom-call | flops 1207959552 | bytes 6291456 | tf_op jit(solution)/shard_map/expert_forward/pallas_call | solution.py:351
  227.6 1.6 copy-done
  229.2 62.6 %send_rows_3.1.u_ref = bf16[3,1024,512]{2,1,0:T(8,128)(2,1)S(1)} custom-call(bf16[96,512]{1,0:T(8,128)(2,1)S(1)} %copy-done.34, f32[2,4,4,4,4,8,128]{6,5,4,3,2,1,0:T(8,128)S(1)} %copy-done.42), custom_call_target="tpu_custom_call" | custom-call | flops 30000001024 | bytes 12582912 | tf_op jit(solution)/shard_map/send_rows_3/pallas_call | solution.py:227
  291.8 1.7 copy-done.1
  293.5 10.2 %all-to-all-start.1 = ((bf16[128,24,512]{2,1,0:T(8,128)(2,1)}), bf16[128,24,512]{2,1,0:T(8,128)(2,1)}, u32[]{:S(2)}, u32[]{:S(2)}) async-start(bf16[128,24,512]{2,1,0:T(8,128)(2,1)} %copy-done), calls=%async_computation.1 | async-start | bytes 6291456 | tf_op jit(solution)/shard_map/all_to_all | solution.py:402
  304.6 3.0 combine.6.refs_0_.x_ref
  307.7 74.4 %send_rows_4.1 = (bf16[3,1024,512]{2,1,0:T(8,128)(2,1)S(1)}, bf16[3,1024,512]{2,1,0:T(8,128)(2,1)S(1)}) custom-call(bf16[96,512]{1,0:T(8,128)(2,1)S(1)} %combine.6.refs_0_.x_ref, f32[2,4,4,4,4,8,128]{6,5,4,3,2,1,0:T(8,128)S(1)} %copy-done.43), custom_call_target="tpu_custom_call" | custom-call | flops 30000001024 | bytes 12582912 | tf_op jit(solution)/shard_map/send_rows_4/pallas_call | solution.py:227
  382.1 10.1 %expert_backward.3 = (bf16[128,24,512]{2,1,0:T(8,128)(2,1)S(1)}, f32[3,8,128]{2,1,0:T(8,128)S(1)}, bf16[3,1024,128]{2,1,0:T(8,128)(2,1)S(1)}, bf16[3,1024,128]{2,1,0:T(8,128)(2,1)S(1)}, bf16[3,1024,128]{2,1,0:T(8,128)(2,1)S(1)}) custom-call(bf16[3,1024,512]{2,1,0:T(8,128)(2,1)S(1)} %copy-done.2, bf16[3,1024,512]{2,1,0:T(8,128)(2,1)S(1)} %get-tuple-element.35.dy_ref, ...), custom_call_target="tpu_custom_call" | custom-call | flops 3221225472 | bytes 12582912 | tf_op jit(solution)/shard_map/expert_backward/pallas_call | solution.py:351
  392.2 1.7 copy-done.8
  401.2 18.4 %all_to_all.32 = f32[128,1,48]{2,1,0:T(1,128)} all-to-all(f32[128,1,48]{2,1,0:T(1,128)} %copy.128), channel_id=1, replica_groups=mesh['dp'=1,'ep'=128] {'ep'}, dimensions={0} | all-to-all | bytes 49152 | tf_op jit(solution)/shard_map/all_to_all | solution.py:429
  419.6 5.4 %all-to-all-start.3 = ((bf16[128,24,512]{2,1,0:T(8,128)(2,1)}), bf16[128,24,512]{2,1,0:T(8,128)(2,1)}, u32[]{:S(2)}, u32[]{:S(2)}) async-start(bf16[128,24,512]{2,1,0:T(8,128)(2,1)} %copy-done.8), calls=%async_computation.3 | async-start | bytes 6291456 | tf_op jit(solution)/shard_map/all_to_all | solution.py:402
  425.6 3.7 fusion.16
  429.3 2.1 fusion.14
  431.4 2.1 fusion.15
  433.5 4.0 combine.5
  437.6 1.5 fusion.13
  439.9 2.1 fusion.11
  442.1 2.1 fusion.12
  447.5 22.4 %all-to-all-done.3 = bf16[128,24,512]{2,1,0:T(8,128)(2,1)} async-done(((bf16[128,24,512]{2,1,0:T(8,128)(2,1)}), bf16[128,24,512]{2,1,0:T(8,128)(2,1)}, u32[]{:S(2)}, u32[]{:S(2)}) %all-to-all-start.3) | async-done | bytes 3145760 | tf_op jit(solution)/shard_map/all_to_all | solution.py:402
  469.9 3.5 combine.7
  (149 shorter events, 30.0 us)
Async XLA Ops:
  8.2 49.8 %copy-start.27 = (bf16[3,512,128]{2,1,0:T(8,128)(2,1)S(1)}, bf16[3,512,128]{2,1,0:T(8,128)(2,1)}, u32[]{:S(2)}) copy-start(bf16[3,512,128]{2,1,0:T(8,128)(2,1)} %w1_ref.7) | copy-start | bytes 1179652
  8.2 49.8 %copy-start.29 = (bf16[3,512,128]{2,1,0:T(8,128)(2,1)S(1)}, bf16[3,512,128]{2,1,0:T(8,128)(2,1)}, u32[]{:S(2)}) copy-start(bf16[3,512,128]{2,1,0:T(8,128)(2,1)} %w3_ref.7) | copy-start | bytes 1179652
  8.2 49.8 %copy-start.31 = (bf16[3,128,512]{2,1,0:T(8,128)(2,1)S(1)}, bf16[3,128,512]{2,1,0:T(8,128)(2,1)}, u32[]{:S(2)}) copy-start(bf16[3,128,512]{2,1,0:T(8,128)(2,1)} %w2_ref.7) | copy-start | bytes 1179652
  65.0 7.4 %copy-start.53 = (f32[96,8]{0,1:T(8,128)S(1)}, f32[96,8]{0,1:T(8,128)}, u32[]{:S(2)}) copy-start(f32[96,8]{0,1:T(8,128)} %param.15) | copy-start | bytes 9220
  65.0 7.5 %copy-start.35 = (bf16[96,512]{1,0:T(8,128)(2,1)S(1)}, bf16[96,512]{1,0:T(8,128)(2,1)}, u32[]{:S(2)}) copy-start(bf16[96,512]{1,0:T(8,128)(2,1)} %x_ref.3) | copy-start | bytes 294916
  65.0 88.1 %all-to-all-start = ((bf16[128,24,512]{2,1,0:T(8,128)(2,1)}), bf16[128,24,512]{2,1,0:T(8,128)(2,1)S(1)}, u32[]{:S(2)}, u32[]{:S(2)}) async-start(bf16[128,24,512]{2,1,0:T(8,128)(2,1)} %expert_forward.2), calls=%async_computation | async-start | bytes 6291456 | tf_op jit(solution)/shard_map/all_to_all | solution.py:402
  74.1 79.1 %copy-start.34 = (bf16[96,512]{1,0:T(8,128)(2,1)S(1)}, bf16[96,512]{1,0:T(8,128)(2,1)}, u32[]{:S(2)}) copy-start(bf16[96,512]{1,0:T(8,128)(2,1)} %refs_0_.4) | copy-start | bytes 294916
  154.8 40.3 %copy-start.5 = (bf16[3,1024,512]{2,1,0:T(8,128)(2,1)S(1)}, bf16[3,1024,512]{2,1,0:T(8,128)(2,1)}, u32[]{:S(2)}) copy-start(bf16[3,1024,512]{2,1,0:T(8,128)(2,1)} %copy-done.4) | copy-start | bytes 9437188
  154.8 40.3 %copy-start.21 = (bf16[3,512,128]{2,1,0:T(8,128)(2,1)S(1)}, bf16[3,512,128]{2,1,0:T(8,128)(2,1)}, u32[]{:S(2)}) copy-start(bf16[3,512,128]{2,1,0:T(8,128)(2,1)} %w1_ref.6) | copy-start | bytes 1179652
  154.8 40.3 %copy-start.23 = (bf16[3,512,128]{2,1,0:T(8,128)(2,1)S(1)}, bf16[3,512,128]{2,1,0:T(8,128)(2,1)}, u32[]{:S(2)}) copy-start(bf16[3,512,128]{2,1,0:T(8,128)(2,1)} %w3_ref.6) | copy-start | bytes 1179652
  154.8 40.3 %copy-start.25 = (bf16[3,128,512]{2,1,0:T(8,128)(2,1)S(1)}, bf16[3,128,512]{2,1,0:T(8,128)(2,1)}, u32[]{:S(2)}) copy-start(bf16[3,128,512]{2,1,0:T(8,128)(2,1)} %w2_ref.6) | copy-start | bytes 1179652
  154.8 40.4 %copy-start.38 = (bf16[3,1024,512]{2,1,0:T(8,128)(2,1)S(1)}, bf16[3,1024,512]{2,1,0:T(8,128)(2,1)}, u32[]{:S(2)}) copy-start(bf16[3,1024,512]{2,1,0:T(8,128)(2,1)} %copy-done.37) | copy-start | bytes 9437188
  209.6 6.3 %copy-start.54 = (f32[96,8]{0,1:T(8,128)S(1)}, f32[96,8]{0,1:T(8,128)}, u32[]{:S(2)}) copy-start(f32[96,8]{0,1:T(8,128)} %param.16) | copy-start | bytes 9220
  209.6 83.9 %all-to-all-start.2 = ((bf16[128,24,512]{2,1,0:T(8,128)(2,1)}), bf16[128,24,512]{2,1,0:T(8,128)(2,1)}, u32[]{:S(2)}, u32[]{:S(2)}) async-start(bf16[128,24,512]{2,1,0:T(8,128)(2,1)} %copy-done.9), calls=%async_computation.2 | async-start | bytes 6291456 | tf_op jit(solution)/shard_map/all_to_all | solution.py:402
  221.4 7.8 %copy-start.42 = (f32[2,4,4,4,4,8,128]{6,5,4,3,2,1,0:T(8,128)S(1)}, f32[2,4,4,4,4,8,128]{6,5,4,3,2,1,0:T(8,128)}, u32[]{:S(2)}) copy-start(f32[2,4,4,4,4,8,128]{6,5,4,3,2,1,0:T(8,128)} %copy-done.39) | copy-start | bytes 6291460
  293.5 107.7 %all-to-all-start.1 = ((bf16[128,24,512]{2,1,0:T(8,128)(2,1)}), bf16[128,24,512]{2,1,0:T(8,128)(2,1)}, u32[]{:S(2)}, u32[]{:S(2)}) async-start(bf16[128,24,512]{2,1,0:T(8,128)(2,1)} %copy-done), calls=%async_computation.1 | async-start | bytes 6291456 | tf_op jit(solution)/shard_map/all_to_all | solution.py:402
  304.6 3.0 copy-start.43
  307.6 74.4 %copy-start.2 = (bf16[3,1024,512]{2,1,0:T(8,128)(2,1)S(1)}, bf16[3,1024,512]{2,1,0:T(8,128)(2,1)}, u32[]{:S(2)}) copy-start(bf16[3,1024,512]{2,1,0:T(8,128)(2,1)} %copy-done.1) | copy-start | bytes 9437188
  307.7 74.4 %copy-start.28 = (bf16[3,512,128]{2,1,0:T(8,128)(2,1)S(1)}, bf16[3,512,128]{2,1,0:T(8,128)(2,1)}, u32[]{:S(2)}) copy-start(bf16[3,512,128]{2,1,0:T(8,128)(2,1)} %w1_ref.7) | copy-start | bytes 1179652
  307.7 74.4 %copy-start.30 = (bf16[3,512,128]{2,1,0:T(8,128)(2,1)S(1)}, bf16[3,512,128]{2,1,0:T(8,128)(2,1)}, u32[]{:S(2)}) copy-start(bf16[3,512,128]{2,1,0:T(8,128)(2,1)} %w3_ref.7) | copy-start | bytes 1179652
  307.7 74.4 %copy-start.32 = (bf16[3,128,512]{2,1,0:T(8,128)(2,1)S(1)}, bf16[3,128,512]{2,1,0:T(8,128)(2,1)}, u32[]{:S(2)}) copy-start(bf16[3,128,512]{2,1,0:T(8,128)(2,1)} %w2_ref.7) | copy-start | bytes 1179652
  382.0 10.1 %copy-start.6 = (bf16[3,1024,512]{2,1,0:T(8,128)(2,1)}, bf16[3,1024,512]{2,1,0:T(8,128)(2,1)S(1)}, u32[]{:S(2)}) copy-start(bf16[3,1024,512]{2,1,0:T(8,128)(2,1)S(1)} %get-tuple-element.36.q_ref) | copy-start | bytes 9437188
  419.5 5.4 %copy-start.46 = (s32[768]{0:T(1024)S(1)}, s32[768]{0:T(1024)}, u32[]{:S(2)}) copy-start(s32[768]{0:T(1024)} %copy-done.45) | copy-start | bytes 9220
  419.6 5.4 %copy-start.50 = (s32[768]{0:T(1024)S(1)}, s32[768]{0:T(1024)}, u32[]{:S(2)}) copy-start(s32[768]{0:T(1024)} %copy-done.49) | copy-start | bytes 9220
  419.6 6.0 %copy-start.48 = (s32[768]{0:T(1024)S(1)}, s32[768]{0:T(1024)}, u32[]{:S(2)}) copy-start(s32[768]{0:T(1024)} %copy-done.47) | copy-start | bytes 9220
  419.6 6.0 %copy-start.52 = (s32[768]{0:T(1024)S(1)}, s32[768]{0:T(1024)}, u32[]{:S(2)}) copy-start(s32[768]{0:T(1024)} %copy-done.51) | copy-start | bytes 9220
  419.6 50.4 %all-to-all-start.3 = ((bf16[128,24,512]{2,1,0:T(8,128)(2,1)}), bf16[128,24,512]{2,1,0:T(8,128)(2,1)}, u32[]{:S(2)}, u32[]{:S(2)}) async-start(bf16[128,24,512]{2,1,0:T(8,128)(2,1)} %copy-done.8), calls=%async_computation.3 | async-start | bytes 6291456 | tf_op jit(solution)/shard_map/all_to_all | solution.py:402
  425.6 3.8 copy-start.16
  431.4 6.2 %copy-start.7 = (bf16[3,1024,512]{2,1,0:T(8,128)(2,1)S(1)}, bf16[3,1024,512]{2,1,0:T(8,128)(2,1)}, u32[]{:S(2)}) copy-start(bf16[3,1024,512]{2,1,0:T(8,128)(2,1)} %copy-done.6) | copy-start | bytes 9437188
  431.4 6.2 %copy-start.12 = (bf16[3,1024,128]{2,1,0:T(8,128)(2,1)S(1)}, bf16[3,1024,128]{2,1,0:T(8,128)(2,1)}, u32[]{:S(2)}) copy-start(bf16[3,1024,128]{2,1,0:T(8,128)(2,1)} %copy-done.11) | copy-start | bytes 2359300
  442.1 3.9 copy-start.55
  442.1 4.0 copy-start.56
  (29 other events, 38.8 us)

commit v6 on v5

--- a/solution.py
+++ b/solution.py
@@ -241,14 +241,13 @@
     )(x, table)
 
 
-def combine_kernel(gated, x_ref, row_ref, gate_ref, back_ref, out_ref):
-    tok_dev, width = x_ref.shape
-    chunk = 512
+def pair_sum(gated, row_ref, gate_ref, back):
     codes, gates = row_ref[...], gate_ref[...]
-    total = jnp.zeros((tok_dev, width), F32)
-    for base in range(0, back_ref.shape[0], chunk):
-        lane = lax.broadcasted_iota(jnp.int32, (tok_dev, chunk), 1) + base
-        weight = jnp.zeros((tok_dev, chunk), F32)
+    tok_dev = codes.shape[0]
+    total = 0.0
+    for base, rows in back:
+        lane = lax.broadcasted_iota(jnp.int32, (tok_dev, rows.shape[0]), 1) + base
+        weight = jnp.zeros(lane.shape, F32)
         for j in range(codes.shape[1]):
             weight = jnp.where(codes[:, j:j + 1] == lane, gates[:, j:j + 1] if gated else 1.0, weight)
         hi = weight.astype(BF16)
@@ -257,10 +256,71 @@
             rest = weight - hi.astype(F32)
             mid = rest.astype(BF16)
             terms += [mid, (rest - mid.astype(F32)).astype(BF16)]
-        part = jnp.dot(jnp.concatenate(terms, axis=0), back_ref[pl.ds(base, chunk), :], preferred_element_type=F32)
+        part = jnp.dot(jnp.concatenate(terms, axis=0), rows, preferred_element_type=F32)
         for k in reversed(range(len(terms))):
             total = total + part[k * tok_dev:(k + 1) * tok_dev]
-    out_ref[...] = (x_ref[...].astype(F32) + total).astype(out_ref.dtype)
+    return total
+
+
+def combine_kernel(gated, x_ref, row_ref, gate_ref, back_ref, out_ref):
+    chunk = 512
+    back = ((base, back_ref[pl.ds(base, chunk), :]) for base in range(0, back_ref.shape[0], chunk))
+    out_ref[...] = (x_ref[...].astype(F32) + pair_sum(gated, row_ref, gate_ref, back)).astype(out_ref.dtype)
+
+
+def return_kernel(x_ref, row_ref, gate_ref, rows_ref, line_ref, out_ref, line_out, back, sems):
+    me = lax.axis_index("ep")
+    devices = rows_ref.shape[0]
+    chip, core = lax.div(me, 2), lax.rem(me, 2)
+    x, y, z = lax.rem(chip, SIDE), lax.rem(lax.div(chip, SIDE), SIDE), lax.div(chip, SIDE * SIDE)
+
+    def target(step):
+        d = lax.rem(step * 37, devices)
+        tx = lax.rem(x + lax.rem(lax.div(d, 2), SIDE), SIDE)
+        ty = lax.rem(y + lax.rem(lax.div(d, 2 * SIDE), SIDE), SIDE)
+        tz = lax.rem(z + lax.div(d, 2 * SIDE * SIDE), SIDE)
+        return ((tz * SIDE + ty) * SIDE + tx) * 2 + lax.rem(core + lax.rem(d, 2), 2)
+
+    barrier = pltpu.get_barrier_semaphore()
+
+    def hello(step, carry):
+        pl.semaphore_signal(barrier, inc=1, device_id={"ep": target(step)}, device_id_type=pl.DeviceIdType.MESH)
+        return carry
+
+    lax.fori_loop(1, devices, hello, 0)
+    pl.semaphore_wait(barrier, devices - 1)
+
+    def send(step, carry):
+        to = target(step)
+        for src, dst, k in ((rows_ref, back, 0), (line_ref, line_out, 2)):
+            pltpu.make_async_remote_copy(src_ref=src.at[to], dst_ref=dst.at[me], send_sem=sems.at[k], recv_sem=sems.at[k + 1], device_id={"ep": to}, device_id_type=pl.DeviceIdType.MESH).start()
+        return carry
+
+    lax.fori_loop(1, devices, send, 0)
+    back[me] = rows_ref[me]
+    line_out[me] = line_ref[me]
+    others = pl.ds(0, devices - 1)
+    for src, dst, k in ((rows_ref, back, 0), (line_ref, line_out, 2)):
+        for sem in (sems.at[k], sems.at[k + 1]):
+            pltpu.make_async_copy(src.at[others], dst.at[others], sem).wait()
+    group = 16
+    count, width = rows_ref.shape[1], rows_ref.shape[2]
+    blocks = ((g * count, back[pl.ds(g, group)].reshape(group * count, width)) for g in range(0, devices, group))
+    out_ref[...] = (x_ref[...].astype(F32) + pair_sum(False, row_ref, gate_ref, blocks)).astype(out_ref.dtype)
+
+
+def return_home(x, rows, gates, sent, lines, call_id):
+    vmem = pl.BlockSpec(memory_space=pltpu.VMEM)
+    return pl.pallas_call(
+        return_kernel,
+        out_shape=(jax.ShapeDtypeStruct(x.shape, x.dtype), jax.ShapeDtypeStruct(lines.shape, lines.dtype)),
+        in_specs=[vmem] * 5,
+        out_specs=(vmem, vmem),
+        scratch_shapes=[pltpu.VMEM(sent.shape, sent.dtype), pltpu.SemaphoreType.DMA((4,))],
+        compiler_params=pltpu.CompilerParams(collective_id=call_id, has_side_effects=True, vmem_limit_bytes=32 * 1024 * 1024),
+        cost_estimate=pl.CostEstimate(flops=3 * 10**10, bytes_accessed=sent.size * 4, transcendentals=0),
+        name="return_home",
+    )(x, rows, gates, sent, lines)
 
 
 def combine(x, rows, gates, back, gated):
@@ -424,11 +484,11 @@
         dy_a, q_a = send_rows(dx_mid, table, 0, own, capacity, 4, even, scaled=True)
         x_out = combine(x_mid, rows_b, gate_b, send_back(out_b), True)
         du_a, dgate_rows_a, grads_a = expert_backward(u_again, dy_a, q_a, weights_a, n_group)
-        dx_in = combine(dx_mid, rows_a, gate_a, send_back(du_a), False)
-        dgates = jnp.concatenate([by_home(dgate_rows_a), by_home(dgate_rows_b)], axis=1)
-        dgates = lax.all_to_all(dgates, "ep", 0, 0, tiled=True)
-        dgate_a = look_up(dgates[:, :block], rows_a)
-        dgate_b = look_up(dgates[:, block:], rows_b)
+        lines = jnp.concatenate([by_home(dgate_rows_a), by_home(dgate_rows_b)], axis=1)
+        lines = jnp.pad(lines, ((0, 0), (0, 128 - 2 * block)))[:, None, :]
+        dx_in, lines = return_home(dx_mid, rows_a, gate_a, du_a, lines, 5)
+        dgate_a = look_up(lines[:, 0, :block], rows_a)
+        dgate_b = look_up(lines[:, 0, block:2 * block], rows_b)
         return (x_out, dx_in) + tuple(grads_a) + tuple(grads_b) + (dgate_a, dgate_b)
 
     return jax.shard_map(device_program, mesh=mesh, in_specs=(tok_spec,) * 6 + (w_spec,) * 6, out_specs=(tok_spec,) * 10, check_vma=False)

time: 475 us -> 497 us (1.046)
  Pallas kernels: 347 us -> 378 us
  waiting for transfers between devices: 22.4 us -> 44.3 us
  blocking collectives: 18.4 us -> 0 us
  local copies, waits for them, and re-layouts: 36.2 us -> 23.4 us
  starting transfers between devices: 29.2 us -> 23.6 us
    pallas_call x0 -> x1, Pallas kernels: none -> 57.2 us  [return_home(): pl.pallas_call(return_kernel, out_shape=(jax.ShapeDtypeStruct(x.shape, x....]
    pallas_call x5, Pallas kernels: 301 us -> 279 us  [send_rows(): pl.pallas_call(functools.partial(send_kernel, own, capacity, layer, plus,...]
    all_to_all x4 -> x3, waiting for transfers between devices: 22.4 us -> 44.3 us  [send_back(): return lax.all_to_all(rows, 'ep', 0, 0, tiled=True).reshape(total, width)]
    all_to_all x1 -> x0, blocking collectives: 18.4 us -> none  [device_program(): dgates = lax.all_to_all(dgates, 'ep', 0, 0, tiled=True)]
    unnamed x120 -> x85, local copies, waits for them, and re-layouts: 28.7 us -> 16.8 us
    all_to_all x4 -> x3, starting transfers between devices: 29.2 us -> 23.6 us  [send_back(): return lax.all_to_all(rows, 'ep', 0, 0, tiled=True).reshape(total, width)]
    pallas_call x4 -> x3, Pallas kernels: 12.1 us -> 8.64 us  [combine(): pl.pallas_call(functools.partial(combine_kernel, gated), out_shape=jax.Sh...]
  transfers between devices with their start and end apart: 4 -> 3, of which waited for: 1 -> 1; matrix products, arithmetic and copies ran while one was open for 5% -> 3% of each run, Pallas kernels for 50% -> 34%
where the time goes in v6:
time: 497 us; the launch traced here: 493 us
  Pallas kernels  378 us (76%)
  waiting for transfers between devices  44.3 us (9%)
  starting transfers between devices  23.6 us (5%)
  local copies, waits for them, and re-layouts  23.4 us (5%)
  matrix products  19 us (4%)
    pallas_call x5, Pallas kernels, send_rows(): pl.pallas_call(functools.partial(send_kernel, own, capacity, layer, plus,...  279 us
    pallas_call x1, Pallas kernels, return_home(): pl.pallas_call(return_kernel, out_shape=(jax.ShapeDtypeStruct(x.shape, x....  57.2 us
    all_to_all x3, waiting for transfers between devices, send_back(): return lax.all_to_all(rows, 'ep', 0, 0, tiled=True).reshape(total, width)  44.3 us
    pallas_call x4, Pallas kernels, expert_call(): pl.pallas_call(functools.partial(kernel, 256), out_shape=tuple((kinds[k][...  33.3 us
    all_to_all x3, starting transfers between devices, send_back(): return lax.all_to_all(rows, 'ep', 0, 0, tiled=True).reshape(total, width)  23.6 us
    unnamed x85, local copies, waits for them, and re-layouts  16.8 us
  transfers between devices with their start and end apart: 3, of which 1 were waited for; matrix products, arithmetic and copies ran while one was open for 3% of the time, Pallas kernels for 34%

profile of v6, /device:TPU:1, one launch (start us, length us, event | category | flops | bytes accessed | tf_op | source)
XLA Modules:
  0.0 492.8 jit_solution(10024307279283125734)
XLA Ops:
  5.8 0.9 copy-done.22
  6.7 48.5 %send_rows_0.1 = (bf16[3,1024,512]{2,1,0:T(8,128)(2,1)S(1)}, f32[2,4,4,4,4,8,128]{6,5,4,3,2,1,0:T(8,128)S(1)}) custom-call(bf16[96,512]{1,0:T(8,128)(2,1)S(1)} %copy-done.22, f32[4,8,128]{2,1,0:T(8,128)S(1)} %pad_maximum_fusion.1.refs_1_), custom_call_target="tpu_custom_call" | custom-call | flops 30000001024 | bytes 12582912 | tf_op jit(solution)/shard_map/send_rows_0/pallas_call | solution.py:227
  55.2 1.3 copy-done.28
  56.5 7.0 %expert_forward.2 = bf16[128,24,512]{2,1,0:T(8,128)(2,1)} custom-call(bf16[3,1024,512]{2,1,0:T(8,128)(2,1)S(1)} %get-tuple-element.30.u_ref, bf16[3,512,128]{2,1,0:T(8,128)(2,1)S(1)} %copy-done.16, bf16[3,512,128]{2,1,0:T(8,128)(2,1)S(1)} %copy-done.18, bf16[3,128,512]{2,1,0:T(8,128)(2,1)S(1)} %copy-done.20), custom_call_target="tpu_custom_call" | custom-call | flops 1207959552 | bytes 6291456 | tf_op jit(solution)/shard_map/expert_forward/pallas_call | solution.py:411
  63.5 7.4 %all-to-all-start = ((bf16[128,24,512]{2,1,0:T(8,128)(2,1)}), bf16[128,24,512]{2,1,0:T(8,128)(2,1)S(1)}, u32[]{:S(2)}, u32[]{:S(2)}) async-start(bf16[128,24,512]{2,1,0:T(8,128)(2,1)} %expert_forward.2), calls=%async_computation | async-start | bytes 6291456 | tf_op jit(solution)/shard_map/all_to_all | solution.py:462
  72.3 44.3 %all-to-all-done = bf16[128,24,512]{2,1,0:T(8,128)(2,1)S(1)} async-done(((bf16[128,24,512]{2,1,0:T(8,128)(2,1)}), bf16[128,24,512]{2,1,0:T(8,128)(2,1)S(1)}, u32[]{:S(2)}, u32[]{:S(2)}) %all-to-all-start) | async-done | bytes 3145760 | tf_op jit(solution)/shard_map/all_to_all | solution.py:462
  116.5 1.5 combine.3.refs_0_.x_ref
  118.1 38.8 %send_rows_2.1.u_ref = bf16[3,1024,512]{2,1,0:T(8,128)(2,1)S(1)} custom-call(bf16[96,512]{1,0:T(8,128)(2,1)S(1)} %combine.3.refs_0_.x_ref, f32[2,4,4,4,4,8,128]{6,5,4,3,2,1,0:T(8,128)S(1)} %copy-done.29), custom_call_target="tpu_custom_call" | custom-call | flops 30000001024 | bytes 12582912 | tf_op jit(solution)/shard_map/send_rows_2/pallas_call | solution.py:227
  157.0 6.2 %expert_forward.3 = bf16[128,24,512]{2,1,0:T(8,128)(2,1)S(1)} custom-call(bf16[3,1024,512]{2,1,0:T(8,128)(2,1)S(1)} %send_rows_2.1.u_ref, bf16[3,512,128]{2,1,0:T(8,128)(2,1)S(1)} %copy-done.10, bf16[3,512,128]{2,1,0:T(8,128)(2,1)S(1)} %copy-done.12, bf16[3,128,512]{2,1,0:T(8,128)(2,1)S(1)} %copy-done.14), custom_call_target="tpu_custom_call" | custom-call | flops 1207959552 | bytes 6291456 | tf_op jit(solution)/shard_map/expert_forward/pallas_call | solution.py:411
  163.2 1.7 copy-done
  164.8 7.5 %all-to-all-start.1 = ((bf16[128,24,512]{2,1,0:T(8,128)(2,1)}), bf16[128,24,512]{2,1,0:T(8,128)(2,1)}, u32[]{:S(2)}, u32[]{:S(2)}) async-start(bf16[128,24,512]{2,1,0:T(8,128)(2,1)} %copy-done), calls=%async_computation.1 | async-start | bytes 6291456 | tf_op jit(solution)/shard_map/all_to_all | solution.py:462
  173.3 1.6 copy-done.30
  174.9 77.0 %send_rows_1.1 = (bf16[3,1024,512]{2,1,0:T(8,128)(2,1)S(1)}, bf16[3,1024,512]{2,1,0:T(8,128)(2,1)S(1)}) custom-call(bf16[96,512]{1,0:T(8,128)(2,1)S(1)} %copy-done.24, f32[2,4,4,4,4,8,128]{6,5,4,3,2,1,0:T(8,128)S(1)} %copy-done.30), custom_call_target="tpu_custom_call" | custom-call | flops 30000001024 | bytes 12582912 | tf_op jit(solution)/shard_map/send_rows_1/pallas_call | solution.py:227
  251.9 10.1 %expert_backward.2 = (bf16[128,24,512]{2,1,0:T(8,128)(2,1)S(1)}, f32[3,8,128]{2,1,0:T(8,128)S(1)}, bf16[3,1024,128]{2,1,0:T(8,128)(2,1)S(1)}, bf16[3,1024,128]{2,1,0:T(8,128)(2,1)S(1)}, bf16[3,1024,128]{2,1,0:T(8,128)(2,1)S(1)}) custom-call(bf16[3,1024,512]{2,1,0:T(8,128)(2,1)S(1)} %send_rows_2.1.u_ref, bf16[3,1024,512]{2,1,0:T(8,128)(2,1)S(1)} %get-tuple-element.32.dy_ref, ...), custom_call_target="tpu_custom_call" | custom-call | flops 3221225472 | bytes 12582912 | tf_op jit(solution)/shard_map/expert_backward/pallas_call | solution.py:411
  262.0 1.7 copy-done.2
  267.1 1.0 copy.122
  268.1 3.8 fusion.15
  271.9 2.1 fusion.13
  274.0 8.7 %all-to-all-start.2 = ((bf16[128,24,512]{2,1,0:T(8,128)(2,1)}), bf16[128,24,512]{2,1,0:T(8,128)(2,1)}, u32[]{:S(2)}, u32[]{:S(2)}) async-start(bf16[128,24,512]{2,1,0:T(8,128)(2,1)} %copy-done.2), calls=%async_computation.2 | async-start | bytes 6291456 | tf_op jit(solution)/shard_map/all_to_all | solution.py:462
  282.7 3.4 fusion.14
  286.1 75.6 %send_rows_3.1.u_ref = bf16[3,1024,512]{2,1,0:T(8,128)(2,1)S(1)} custom-call(bf16[96,512]{1,0:T(8,128)(2,1)S(1)} %copy-done.23, f32[2,4,4,4,4,8,128]{6,5,4,3,2,1,0:T(8,128)S(1)} %copy-done.31), custom_call_target="tpu_custom_call" | custom-call | flops 30000001024 | bytes 12582912 | tf_op jit(solution)/shard_map/send_rows_3/pallas_call | solution.py:227
  361.7 4.1 combine.4
  365.8 3.0 combine.5.refs_0_.x_ref
  368.9 38.9 %send_rows_4.1 = (bf16[3,1024,512]{2,1,0:T(8,128)(2,1)S(1)}, bf16[3,1024,512]{2,1,0:T(8,128)(2,1)S(1)}) custom-call(bf16[96,512]{1,0:T(8,128)(2,1)S(1)} %combine.5.refs_0_.x_ref, f32[2,4,4,4,4,8,128]{6,5,4,3,2,1,0:T(8,128)S(1)} %copy-done.32), custom_call_target="tpu_custom_call" | custom-call | flops 30000001024 | bytes 12582912 | tf_op jit(solution)/shard_map/send_rows_4/pallas_call | solution.py:227
  407.9 10.1 %expert_backward.3 = (bf16[128,24,512]{2,1,0:T(8,128)(2,1)S(1)}, f32[3,8,128]{2,1,0:T(8,128)S(1)}, bf16[3,1024,128]{2,1,0:T(8,128)(2,1)S(1)}, bf16[3,1024,128]{2,1,0:T(8,128)(2,1)S(1)}, bf16[3,1024,128]{2,1,0:T(8,128)(2,1)S(1)}) custom-call(bf16[3,1024,512]{2,1,0:T(8,128)(2,1)S(1)} %send_rows_3.1.u_ref, bf16[3,1024,512]{2,1,0:T(8,128)(2,1)S(1)} %get-tuple-element.37.dy_ref, ...), custom_call_target="tpu_custom_call" | custom-call | flops 3221225472 | bytes 12582912 | tf_op jit(solution)/shard_map/expert_backward/pallas_call | solution.py:411
  418.0 2.0 fusion.12
  421.2 1.0 copy.121
  422.3 1.9 copy-done.27
  424.2 57.2 %return_home.1 = (bf16[96,512]{1,0:T(8,128)(2,1)S(1)}, f32[128,1,128]{2,1,0:T(1,128)S(1)}) custom-call(bf16[96,512]{1,0:T(8,128)(2,1)S(1)} %combine.5.refs_0_.x_ref, s32[96,8]{1,0:T(8,128)S(1)} %get-tuple-element.93.row_ref, f32[96,8]{1,0:T(8,128)S(1)} %copy.118.gate_ref, bf16[128,24,512]{2,1,0:T(8,128)(2,1)S(1)} %copy-done.27, f32[128,1,128]{2,1,0:T(1,128)S(1)} %bitcast.37), custom_call_target="tpu_custom_call" | custom-call | flops 30000001024 | bytes 6291456 | tf_op jit(solution)/shard_map/return_home/pallas_call | solution.py:314
  482.7 1.7 fusion.7
  486.7 3.3 fusion.10
  490.0 2.1 fusion.11
  (112 shorter events, 16.4 us)
Async XLA Ops:
  6.7 49.8 %copy-start.16 = (bf16[3,512,128]{2,1,0:T(8,128)(2,1)S(1)}, bf16[3,512,128]{2,1,0:T(8,128)(2,1)}, u32[]{:S(2)}) copy-start(bf16[3,512,128]{2,1,0:T(8,128)(2,1)} %w1_ref.7) | copy-start | bytes 1179652
  6.7 49.8 %copy-start.18 = (bf16[3,512,128]{2,1,0:T(8,128)(2,1)S(1)}, bf16[3,512,128]{2,1,0:T(8,128)(2,1)}, u32[]{:S(2)}) copy-start(bf16[3,512,128]{2,1,0:T(8,128)(2,1)} %w3_ref.7) | copy-start | bytes 1179652
  6.7 49.8 %copy-start.20 = (bf16[3,128,512]{2,1,0:T(8,128)(2,1)S(1)}, bf16[3,128,512]{2,1,0:T(8,128)(2,1)}, u32[]{:S(2)}) copy-start(bf16[3,128,512]{2,1,0:T(8,128)(2,1)} %w2_ref.7) | copy-start | bytes 1179652
  63.5 7.4 %copy-start.33 = (f32[96,8]{0,1:T(8,128)S(1)}, f32[96,8]{0,1:T(8,128)}, u32[]{:S(2)}) copy-start(f32[96,8]{0,1:T(8,128)} %param.15) | copy-start | bytes 9220
  63.5 7.5 %copy-start.34 = (f32[96,8]{0,1:T(8,128)S(1)}, f32[96,8]{0,1:T(8,128)}, u32[]{:S(2)}) copy-start(f32[96,8]{0,1:T(8,128)} %param.16) | copy-start | bytes 9220
  63.5 53.0 %copy-start.23 = (bf16[96,512]{1,0:T(8,128)(2,1)S(1)}, bf16[96,512]{1,0:T(8,128)(2,1)}, u32[]{:S(2)}) copy-start(bf16[96,512]{1,0:T(8,128)(2,1)} %refs_0_.4) | copy-start | bytes 294916
  63.5 53.0 %all-to-all-start = ((bf16[128,24,512]{2,1,0:T(8,128)(2,1)}), bf16[128,24,512]{2,1,0:T(8,128)(2,1)S(1)}, u32[]{:S(2)}, u32[]{:S(2)}) async-start(bf16[128,24,512]{2,1,0:T(8,128)(2,1)} %expert_forward.2), calls=%async_computation | async-start | bytes 6291456 | tf_op jit(solution)/shard_map/all_to_all | solution.py:462
  118.1 38.8 %copy-start.10 = (bf16[3,512,128]{2,1,0:T(8,128)(2,1)S(1)}, bf16[3,512,128]{2,1,0:T(8,128)(2,1)}, u32[]{:S(2)}) copy-start(bf16[3,512,128]{2,1,0:T(8,128)(2,1)} %w1_ref.6) | copy-start | bytes 1179652
  118.1 38.8 %copy-start.12 = (bf16[3,512,128]{2,1,0:T(8,128)(2,1)S(1)}, bf16[3,512,128]{2,1,0:T(8,128)(2,1)}, u32[]{:S(2)}) copy-start(bf16[3,512,128]{2,1,0:T(8,128)(2,1)} %w3_ref.6) | copy-start | bytes 1179652
  118.1 38.8 %copy-start.14 = (bf16[3,128,512]{2,1,0:T(8,128)(2,1)S(1)}, bf16[3,128,512]{2,1,0:T(8,128)(2,1)}, u32[]{:S(2)}) copy-start(bf16[3,128,512]{2,1,0:T(8,128)(2,1)} %w2_ref.6) | copy-start | bytes 1179652
  164.8 109.2 %all-to-all-start.1 = ((bf16[128,24,512]{2,1,0:T(8,128)(2,1)}), bf16[128,24,512]{2,1,0:T(8,128)(2,1)}, u32[]{:S(2)}, u32[]{:S(2)}) async-start(bf16[128,24,512]{2,1,0:T(8,128)(2,1)} %copy-done), calls=%async_computation.1 | async-start | bytes 6291456 | tf_op jit(solution)/shard_map/all_to_all | solution.py:462
  174.9 77.0 %copy-start.11 = (bf16[3,512,128]{2,1,0:T(8,128)(2,1)S(1)}, bf16[3,512,128]{2,1,0:T(8,128)(2,1)}, u32[]{:S(2)}) copy-start(bf16[3,512,128]{2,1,0:T(8,128)(2,1)} %w1_ref.6) | copy-start | bytes 1179652
  174.9 77.0 %copy-start.13 = (bf16[3,512,128]{2,1,0:T(8,128)(2,1)S(1)}, bf16[3,512,128]{2,1,0:T(8,128)(2,1)}, u32[]{:S(2)}) copy-start(bf16[3,512,128]{2,1,0:T(8,128)(2,1)} %w3_ref.6) | copy-start | bytes 1179652
  174.9 77.0 %copy-start.15 = (bf16[3,128,512]{2,1,0:T(8,128)(2,1)S(1)}, bf16[3,128,512]{2,1,0:T(8,128)(2,1)}, u32[]{:S(2)}) copy-start(bf16[3,128,512]{2,1,0:T(8,128)(2,1)} %w2_ref.6) | copy-start | bytes 1179652
  251.9 10.1 %copy-start.1 = (bf16[3,1024,512]{2,1,0:T(8,128)(2,1)}, bf16[3,1024,512]{2,1,0:T(8,128)(2,1)S(1)}, u32[]{:S(2)}) copy-start(bf16[3,1024,512]{2,1,0:T(8,128)(2,1)S(1)} %get-tuple-element.33.q_ref) | copy-start | bytes 9437188
  268.1 3.8 copy-start.9
  274.0 91.8 %all-to-all-start.2 = ((bf16[128,24,512]{2,1,0:T(8,128)(2,1)}), bf16[128,24,512]{2,1,0:T(8,128)(2,1)}, u32[]{:S(2)}, u32[]{:S(2)}) async-start(bf16[128,24,512]{2,1,0:T(8,128)(2,1)} %copy-done.2), calls=%async_computation.2 | async-start | bytes 6291456 | tf_op jit(solution)/shard_map/all_to_all | solution.py:462
  282.7 3.4 copy-start.31
  361.7 4.1 copy-start.25
  365.8 3.1 copy-start.32
  368.9 39.0 %copy-start.17 = (bf16[3,512,128]{2,1,0:T(8,128)(2,1)S(1)}, bf16[3,512,128]{2,1,0:T(8,128)(2,1)}, u32[]{:S(2)}) copy-start(bf16[3,512,128]{2,1,0:T(8,128)(2,1)} %w1_ref.7) | copy-start | bytes 1179652
  368.9 39.0 %copy-start.19 = (bf16[3,512,128]{2,1,0:T(8,128)(2,1)S(1)}, bf16[3,512,128]{2,1,0:T(8,128)(2,1)}, u32[]{:S(2)}) copy-start(bf16[3,512,128]{2,1,0:T(8,128)(2,1)} %w3_ref.7) | copy-start | bytes 1179652
  368.9 39.0 %copy-start.21 = (bf16[3,128,512]{2,1,0:T(8,128)(2,1)S(1)}, bf16[3,128,512]{2,1,0:T(8,128)(2,1)}, u32[]{:S(2)}) copy-start(bf16[3,128,512]{2,1,0:T(8,128)(2,1)} %w2_ref.7) | copy-start | bytes 1179652
  418.0 2.0 copy-start.4
  418.0 2.0 copy-start.6
  418.0 2.4 copy-start.26
  422.3 1.9 copy-start.27
  424.2 58.5 %copy-start.37 = (s32[768]{0:T(1024)S(1)}, s32[768]{0:T(1024)}, u32[]{:S(2)}) copy-start(s32[768]{0:T(1024)} %get-tuple-element.96) | copy-start | bytes 9220
  424.2 58.5 %copy-start.38 = (s32[768]{0:T(1024)S(1)}, s32[768]{0:T(1024)}, u32[]{:S(2)}) copy-start(s32[768]{0:T(1024)} %get-tuple-element.97) | copy-start | bytes 9220
  424.2 61.0 %copy-start.35 = (s32[768]{0:T(1024)S(1)}, s32[768]{0:T(1024)}, u32[]{:S(2)}) copy-start(s32[768]{0:T(1024)} %get-tuple-element.98) | copy-start | bytes 9220
  424.2 61.0 %copy-start.36 = (s32[768]{0:T(1024)S(1)}, s32[768]{0:T(1024)}, u32[]{:S(2)}) copy-start(s32[768]{0:T(1024)} %get-tuple-element.99) | copy-start | bytes 9220
  486.7 3.3 copy-start.5
  (10 other events, 12.3 us)

commit v7 on v6

--- a/solution.py
+++ b/solution.py
@@ -23,30 +23,122 @@
 SIDE = 4
 
 
-def send_kernel(own, capacity, layer, plus, first, scaled, *refs):
-    if first:
-        x_ref, tile_ref, u_ref, table_ref, held, local_sem, send_sem, recv_sem, tiles = refs
-    elif scaled:
-        x_ref, tiles, u_ref, q_ref, held, local_sem, send_sem, recv_sem = refs
-    else:
-        x_ref, tiles, u_ref, held, local_sem, send_sem, recv_sem = refs
+def my_place():
     me = lax.axis_index("ep")
-    core = lax.rem(me, 2)
     chip = lax.div(me, 2)
     at = (lax.rem(chip, SIDE), lax.rem(lax.div(chip, SIDE), SIDE), lax.div(chip, SIDE * SIDE))
+    return me, lax.rem(me, 2), at
+
+
+def device_at(at, core, delta, flip):
+    c = [a if d == 0 else lax.rem(a + d + SIDE, SIDE) for a, d in zip(at, delta)]
+    return ((c[2] * SIDE + c[1]) * SIDE + c[0]) * 2 + (1 - core if flip else core)
+
+
+def return_offsets():
+    direct, relayed = [], []
+    devices = 2 * SIDE ** 3
+    for step in range(1, devices):
+        d = step * 37 % devices
+        flip, delta = d % 2, (d // 2 % SIDE, d // (2 * SIDE) % SIDE, d // (2 * SIDE * SIDE))
+        delta = tuple(v if v <= 2 else v - SIDE for v in delta)
+        if 2 in delta:
+            way = 1 if flip == 0 else -1
+            delta = tuple(2 * way if v == 2 else v for v in delta)
+            relayed.append((delta, flip, tuple(way if abs(v) == 2 else 0 for v in delta)))
+        else:
+            direct.append((delta, flip))
+    return direct, relayed
+
+
+RELAYS = len(return_offsets()[1])
+
+
+def greet_all(me, core, at):
+    barrier = pltpu.get_barrier_semaphore()
+    devices = 2 * SIDE ** 3
+
+    def hello(step, carry):
+        pl.semaphore_signal(barrier, inc=1, device_id={"ep": lax.rem(me + step, devices)}, device_id_type=pl.DeviceIdType.MESH)
+        return carry
+
+    lax.fori_loop(1, devices, hello, 0)
+    pl.semaphore_wait(barrier, devices - 1)
+
+
+def return_steps(me, core, at, rows_ref, back, relay, sems, relay_sems):
+    direct, relayed = return_offsets()
+    devices = rows_ref.shape[0]
+
+    def copy(src, dst, send_sem, recv_sem, to):
+        return pltpu.make_async_remote_copy(src_ref=src, dst_ref=dst, send_sem=send_sem, recv_sem=recv_sem, device_id={"ep": to}, device_id_type=pl.DeviceIdType.MESH)
+
+    def to_relay(k):
+        delta, flip, via = relayed[k]
+        return copy(rows_ref.at[device_at(at, core, delta, flip)], relay.at[k], sems.at[0], relay_sems.at[k], device_at(at, core, via, 0))
+
+    def send_direct(k):
+        to = device_at(at, core, *direct[k])
+        copy(rows_ref.at[to], back.at[me], sems.at[1], sems.at[2], to).start()
+
+    def forward(k):
+        delta, flip, via = relayed[k]
+        to_relay(k).wait_recv()
+        origin = device_at(at, core, tuple(-v for v in via), 0)
+        to = device_at(at, core, tuple(d - v for d, v in zip(delta, via)), flip)
+        copy(relay.at[k], back.at[origin], sems.at[1], sems.at[2], to).start()
+
+    def finish():
+        back[me] = rows_ref[me]
+        others = pl.ds(0, devices - 1)
+        pltpu.make_async_copy(rows_ref.at[others], back.at[others], sems.at[2]).wait()
+        pltpu.make_async_copy(rows_ref.at[others], back.at[others], sems.at[1]).wait()
+        relays = pl.ds(0, len(relayed))
+        pltpu.make_async_copy(rows_ref.at[relays], relay.at[relays], sems.at[0]).wait()
+
+    def pieces(count, action, parts):
+        cut = [count * i // parts for i in range(parts + 1)]
+        return [lambda lo=lo, hi=hi: [action(k) for k in range(lo, hi)] for lo, hi in zip(cut, cut[1:])]
+
+    vias = pieces(len(relayed), lambda k: to_relay(k).start(), 4)
+    directs = pieces(len(direct), send_direct, 4)
+    forwards = pieces(len(relayed), forward, 8)
+    return vias, directs, forwards, finish
+
+
+def home_blocks(back):
+    group = 16
+    count, width = back.shape[1], back.shape[2]
+    return ((g * count, back[pl.ds(g, group)].reshape(group * count, width)) for g in range(0, back.shape[0], group))
+
+
+def send_kernel(own, capacity, layer, first, scaled, returning, *refs):
+    refs = list(refs)
+    x_ref, tile_ref = refs.pop(0), refs.pop(0)
+    if returning:
+        base_ref, row_ref, gate_ref, rows_ref = (refs.pop(0) for _ in range(4))
+    u_ref = refs.pop(0)
+    if scaled:
+        q_ref = refs.pop(0)
+    if first:
+        table_ref = refs.pop(0)
+    if returning:
+        home_ref = refs.pop(0)
+    held, local_sem, send_sem, recv_sem = (refs.pop(0) for _ in range(4))
+    tiles = refs.pop(0) if first else tile_ref
+    if returning:
+        back, relay, return_sems, relay_sems = refs
+    me, core, at = my_place()
+    plus = x_ref.shape[0] // 6
     third = x_ref.shape[0] // 3
     spans = {1: (0, plus), -1: (plus, third - plus)}
 
     def device(dim, step):
-        c = list(at)
-        c[dim] = lax.rem(c[dim] + step + SIDE, SIDE)
-        return ((c[2] * SIDE + c[1]) * SIDE + c[0]) * 2 + core
-
-    partner = chip * 2 + (1 - core)
+        return device_at(at, core, [step if d == dim else 0 for d in range(3)], 0)
+
+    partner = device_at(at, core, (0, 0, 0), 1)
 
     def region(part, pos, span):
-        if span[1] == 0:
-            return None
         idx = [pos[d] if d in pos else at[d] for d in range(3)]
         idx = [pl.ds(0, SIDE) if i is None else i for i in idx]
         where = (core, idx[2], idx[1], idx[0])
@@ -55,8 +147,6 @@
     copies = {}
 
     def start(key, refs, to, with_tile):
-        if refs is None:
-            return
         for kind, ref in (("x", refs[0]), ("t", tiles.at[refs[1]])):
             if kind == "t" and not (first and with_tile):
                 continue
@@ -76,13 +166,17 @@
         own_tile = pltpu.make_async_copy(tile_ref, tiles.at[core, at[2], at[1], at[0]], send_sem.at[0])
         own_tile.start()
         own_tile.wait()
-    barrier = pltpu.get_barrier_semaphore()
-    for dim in range(3):
-        for step in (1, -1, 2):
-            pl.semaphore_signal(barrier, inc=1, device_id={"ep": device(dim, step)}, device_id_type=pl.DeviceIdType.MESH)
-    pl.semaphore_signal(barrier, inc=1, device_id={"ep": partner}, device_id_type=pl.DeviceIdType.MESH)
-    mine.wait()
-    pl.semaphore_wait(barrier, 10)
+    if returning:
+        greet_all(me, core, at)
+        mine.wait()
+    else:
+        barrier = pltpu.get_barrier_semaphore()
+        for dim in range(3):
+            for step in (1, -1, 2):
+                pl.semaphore_signal(barrier, inc=1, device_id={"ep": device(dim, step)}, device_id_type=pl.DeviceIdType.MESH)
+        pl.semaphore_signal(barrier, inc=1, device_id={"ep": partner}, device_id_type=pl.DeviceIdType.MESH)
+        mine.wait()
+        pl.semaphore_wait(barrier, 10)
 
     def dims(part):
         return part, (part + 1) % 3, (part + 2) % 3
@@ -166,79 +260,104 @@
                     if (b == 2) + (c == 2) == wanted:
                         arrive("d2d", part, b, c)
 
-    for part in range(3):
-        d1 = dims(part)[0]
-        for way in (2, 1, -1):
-            start(("m1", part, way), region(part, {}, whole), device(d1, way), True)
-    for part in range(3):
-        d2 = dims(part)[1]
-        for way in (1, -1, 2):
-            arrive("m1", part, way)
-        for way in (2, 1, -1):
-            start(("m2", part, way), row_of(part, 0, 0), device(d2, way), True)
-    for part in range(3):
-        whole_row(part, 0)
-    for part in range(3):
-        for way in (1, -1):
-            arrive("m2", part, way)
-            whole_row(part, -way)
-    for part in range(3):
-        for way in (1, -1):
-            pass_on(part, 0, way)
-    for part in range(3):
-        arrive("m2", part, 2)
-        whole_row(part, 2)
-    for b in (-1, 1):
+    def first_sends():
+        for part in range(3):
+            for way in (2, 1, -1):
+                start(("m1", part, way), region(part, {}, whole), device(dims(part)[0], way), True)
+
+    def second_sends():
+        for part in range(3):
+            for way in (1, -1, 2):
+                arrive("m1", part, way)
+            for way in (2, 1, -1):
+                start(("m2", part, way), row_of(part, 0, 0), device(dims(part)[1], way), True)
+
+    def own_rows():
+        for part in range(3):
+            whole_row(part, 0)
+
+    def near_sends():
+        for part in range(3):
+            for way in (1, -1):
+                arrive("m2", part, way)
+                whole_row(part, -way)
+
+    def pass_rows(b):
         for part in range(3):
             for way in (1, -1):
                 pass_on(part, b, way)
-    arrive_across(0)
-    lax.fori_loop(0, 9, near_rows, 0)
-    for part in range(3):
-        last_row(part, 0)
-    for part in range(3):
-        for way in (1, -1):
-            pass_on(part, 2, way)
-    for b in (-1, 1):
+
+    def opposite_rows():
+        for part in range(3):
+            arrive("m2", part, 2)
+            whole_row(part, 2)
+
+    def last_rows(b):
         for part in range(3):
             last_row(part, b)
-    arrive_across(1)
-    lax.fori_loop(0, 9, far_rows, 0)
-    for part in range(3):
-        last_row(part, 2)
+
+    def pick_near():
+        arrive_across(0)
+        lax.fori_loop(0, 9, near_rows, 0)
+
+    def pick_far():
+        arrive_across(1)
+        lax.fori_loop(0, 9, far_rows, 0)
+
+    gathering = [first_sends, second_sends, own_rows, near_sends, lambda: pass_rows(0), opposite_rows, lambda: pass_rows(-1), lambda: pass_rows(1), pick_near, lambda: last_rows(0), lambda: pass_rows(2), lambda: last_rows(-1), lambda: last_rows(1), pick_far]
+    between = {}
+    if returning:
+        vias, directs, forwards, finish = return_steps(me, core, at, rows_ref, back, relay, return_sems, relay_sems)
+        between = {0: vias[:1], 1: vias[1:2], 2: vias[2:3], 3: vias[3:] + directs[:1], 4: forwards[:1] + directs[1:2], 5: forwards[1:2] + directs[2:3], 6: forwards[2:4] + directs[3:], 7: forwards[4:5], 8: forwards[5:7], 9: forwards[7:]}
+    for n, step in enumerate(gathering):
+        step()
+        for extra in between.get(n, []):
+            extra()
+    last_rows(2)
     arrive_across(2)
     lax.fori_loop(0, 3, farthest_rows, 0)
     pick((2, 2, 2))
+    if returning:
+        finish()
+        total = pair_sum(returning == "gated", row_ref, gate_ref, home_blocks(back))
+        home_ref[...] = (base_ref[...].astype(F32) + total).astype(home_ref.dtype)
     if first:
         table_ref[...] = tiles[...]
     for copy in copies.values():
         copy.wait_send()
 
 
-def send_rows(x, table, layer, own, capacity, call_id, plus, first=False, scaled=False):
+def return_scratch(sent):
+    return [pltpu.VMEM(sent.shape, sent.dtype), pltpu.VMEM((RELAYS,) + sent.shape[1:], sent.dtype), pltpu.SemaphoreType.DMA((5,)), pltpu.SemaphoreType.DMA((RELAYS,))]
+
+
+def send_rows(x, table, layer, own, capacity, call_id, first=False, scaled=False, home=None, gated=False):
     tok_dev, width = x.shape
     devices = 2 * SIDE ** 3
     count = 228 if first else 114
     u_shape = jax.ShapeDtypeStruct((own, devices * capacity, width), x.dtype)
     table_shape = jax.ShapeDtypeStruct((2, SIDE, SIDE, SIDE, 4, 8, 128), F32)
-    outs = (u_shape, table_shape) if first else (u_shape, u_shape) if scaled else (u_shape,)
+    outs = (u_shape,) + (u_shape,) * scaled + (table_shape,) * first
+    if home:
+        outs += (jax.ShapeDtypeStruct(home[0].shape, home[0].dtype),)
     vmem = pl.BlockSpec(memory_space=pltpu.VMEM)
     hbm = pl.BlockSpec(memory_space=pl.ANY)
+    returning = None if home is None else "gated" if gated else "plain"
     return pl.pallas_call(
-        functools.partial(send_kernel, own, capacity, layer, plus, first, scaled),
+        functools.partial(send_kernel, own, capacity, layer, first, scaled, returning),
         out_shape=outs,
-        in_specs=[hbm, hbm if first else vmem],
+        in_specs=[hbm, hbm if first else vmem] + [vmem] * (4 if home else 0),
         out_specs=(vmem,) * len(outs),
         scratch_shapes=[
             pltpu.VMEM((2, SIDE, SIDE, SIDE, tok_dev, width), x.dtype),
             pltpu.SemaphoreType.DMA,
             pltpu.SemaphoreType.DMA((count,)),
             pltpu.SemaphoreType.DMA((count,)),
-        ] + ([pltpu.VMEM(table_shape.shape, F32)] if first else []),
-        compiler_params=pltpu.CompilerParams(collective_id=call_id, has_side_effects=True, vmem_limit_bytes=40 * 1024 * 1024),
+        ] + ([pltpu.VMEM(table_shape.shape, F32)] if first else []) + (return_scratch(home[3]) if home else []),
+        compiler_params=pltpu.CompilerParams(collective_id=call_id, has_side_effects=True, vmem_limit_bytes=46 * 1024 * 1024),
         cost_estimate=pl.CostEstimate(flops=3 * 10**10, bytes_accessed=devices * tok_dev * width * 2, transcendentals=0),
         name=f"send_rows_{call_id}",
-    )(x, table)
+    )(x, table, *(home or ()))
 
 
 def pair_sum(gated, row_ref, gate_ref, back):
@@ -262,51 +381,26 @@
     return total
 
 
-def combine_kernel(gated, x_ref, row_ref, gate_ref, back_ref, out_ref):
-    chunk = 512
-    back = ((base, back_ref[pl.ds(base, chunk), :]) for base in range(0, back_ref.shape[0], chunk))
-    out_ref[...] = (x_ref[...].astype(F32) + pair_sum(gated, row_ref, gate_ref, back)).astype(out_ref.dtype)
-
-
-def return_kernel(x_ref, row_ref, gate_ref, rows_ref, line_ref, out_ref, line_out, back, sems):
-    me = lax.axis_index("ep")
+def return_kernel(x_ref, row_ref, gate_ref, rows_ref, line_ref, out_ref, line_out, back, relay, sems, relay_sems):
+    me, core, at = my_place()
     devices = rows_ref.shape[0]
-    chip, core = lax.div(me, 2), lax.rem(me, 2)
-    x, y, z = lax.rem(chip, SIDE), lax.rem(lax.div(chip, SIDE), SIDE), lax.div(chip, SIDE * SIDE)
-
-    def target(step):
-        d = lax.rem(step * 37, devices)
-        tx = lax.rem(x + lax.rem(lax.div(d, 2), SIDE), SIDE)
-        ty = lax.rem(y + lax.rem(lax.div(d, 2 * SIDE), SIDE), SIDE)
-        tz = lax.rem(z + lax.div(d, 2 * SIDE * SIDE), SIDE)
-        return ((tz * SIDE + ty) * SIDE + tx) * 2 + lax.rem(core + lax.rem(d, 2), 2)
-
-    barrier = pltpu.get_barrier_semaphore()
-
-    def hello(step, carry):
-        pl.semaphore_signal(barrier, inc=1, device_id={"ep": target(step)}, device_id_type=pl.DeviceIdType.MESH)
-        return carry
-
-    lax.fori_loop(1, devices, hello, 0)
-    pl.semaphore_wait(barrier, devices - 1)
-
-    def send(step, carry):
-        to = target(step)
-        for src, dst, k in ((rows_ref, back, 0), (line_ref, line_out, 2)):
-            pltpu.make_async_remote_copy(src_ref=src.at[to], dst_ref=dst.at[me], send_sem=sems.at[k], recv_sem=sems.at[k + 1], device_id={"ep": to}, device_id_type=pl.DeviceIdType.MESH).start()
-        return carry
-
-    lax.fori_loop(1, devices, send, 0)
-    back[me] = rows_ref[me]
+    greet_all(me, core, at)
+    vias, directs, forwards, finish = return_steps(me, core, at, rows_ref, back, relay, sems, relay_sems)
+
+    def send_line(step, carry):
+        to = lax.rem(me + step, devices)
+        pltpu.make_async_remote_copy(src_ref=line_ref.at[to], dst_ref=line_out.at[me], send_sem=sems.at[3], recv_sem=sems.at[4], device_id={"ep": to}, device_id_type=pl.DeviceIdType.MESH).start()
+        return carry
+
+    for step in vias + directs[:2] + forwards[:2] + directs[2:] + forwards[2:]:
+        step()
+    lax.fori_loop(1, devices, send_line, 0)
     line_out[me] = line_ref[me]
+    finish()
     others = pl.ds(0, devices - 1)
-    for src, dst, k in ((rows_ref, back, 0), (line_ref, line_out, 2)):
-        for sem in (sems.at[k], sems.at[k + 1]):
-            pltpu.make_async_copy(src.at[others], dst.at[others], sem).wait()
-    group = 16
-    count, width = rows_ref.shape[1], rows_ref.shape[2]
-    blocks = ((g * count, back[pl.ds(g, group)].reshape(group * count, width)) for g in range(0, devices, group))
-    out_ref[...] = (x_ref[...].astype(F32) + pair_sum(False, row_ref, gate_ref, blocks)).astype(out_ref.dtype)
+    for k in (3, 4):
+        pltpu.make_async_copy(line_ref.at[others], line_out.at[others], sems.at[k]).wait()
+    out_ref[...] = (x_ref[...].astype(F32) + pair_sum(False, row_ref, gate_ref, home_blocks(back))).astype(out_ref.dtype)
 
 
 def return_home(x, rows, gates, sent, lines, call_id):
@@ -316,7 +410,7 @@
         out_shape=(jax.ShapeDtypeStruct(x.shape, x.dtype), jax.ShapeDtypeStruct(lines.shape, lines.dtype)),
         in_specs=[vmem] * 5,
         out_specs=(vmem, vmem),
-        scratch_shapes=[pltpu.VMEM(sent.shape, sent.dtype), pltpu.SemaphoreType.DMA((4,))],
+        scratch_shapes=return_scratch(sent),
         compiler_params=pltpu.CompilerParams(collective_id=call_id, has_side_effects=True, vmem_limit_bytes=32 * 1024 * 1024),
         cost_estimate=pl.CostEstimate(flops=3 * 10**10, bytes_accessed=sent.size * 4, transcendentals=0),
         name="return_home",
@@ -454,12 +548,7 @@
         rows_b = pair_rows(idx_b, capacity)
         pad = ((0, 0), (0, 128 - tok_dev))
         tile = jnp.stack([jnp.pad(rows_a.T.astype(F32), pad, constant_values=-1.0), jnp.pad(rows_b.T.astype(F32), pad, constant_values=-1.0), jnp.pad(gate_a.T, pad), jnp.pad(gate_b.T, pad)])
-        third = tok_dev // 3
-        even = third // 2
-        u_a, table = send_rows(x_in, tile, 0, own, capacity, 0, even, first=True)
-
-        def send_back(rows):
-            return lax.all_to_all(rows, "ep", 0, 0, tiled=True).reshape(total, width)
+        u_a, table = send_rows(x_in, tile, 0, own, capacity, 0, first=True)
 
         def by_home(dgate_rows):
             return dgate_rows.reshape(own, n_group, capacity).transpose(1, 0, 2).reshape(n_group, block)
@@ -472,17 +561,13 @@
             return jnp.sum(jnp.where(slot, picked, 0.0), axis=1).reshape(rows.shape)
 
         weights_a, weights_b = (w1_a, w3_a, w2_a), (w1_b, w3_b, w2_b)
-        back_a = send_back(expert_forward(u_a, weights_a, n_group))
-        dy_b, q_b = send_rows(dy_out, table, 1, own, capacity, 1, even, scaled=True)
-        x_mid = combine(x_in, rows_a, gate_a, back_a, True)
-        u_b, = send_rows(x_mid, table, 1, own, capacity, 2, even)
+        out_a = expert_forward(u_a, weights_a, n_group)
+        dy_b, q_b, x_mid = send_rows(dy_out, table, 1, own, capacity, 1, scaled=True, home=(x_in, rows_a, gate_a, out_a), gated=True)
+        u_b, = send_rows(x_mid, table, 1, own, capacity, 2)
         out_b = expert_forward(u_b, weights_b, n_group)
         du_b, dgate_rows_b, grads_b = expert_backward(u_b, dy_b, q_b, weights_b, n_group)
-        x_again, du_b = lax.optimization_barrier((x_in, du_b))
-        u_again, = send_rows(x_again, table, 0, own, capacity, 3, even)
-        dx_mid = combine(dy_out, rows_b, gate_b, send_back(du_b), False)
-        dy_a, q_a = send_rows(dx_mid, table, 0, own, capacity, 4, even, scaled=True)
-        x_out = combine(x_mid, rows_b, gate_b, send_back(out_b), True)
+        u_again, dx_mid = send_rows(x_in, table, 0, own, capacity, 3, home=(dy_out, rows_b, gate_b, du_b))
+        dy_a, q_a, x_out = send_rows(dx_mid, table, 0, own, capacity, 4, scaled=True, home=(x_mid, rows_b, gate_b, out_b), gated=True)
         du_a, dgate_rows_a, grads_a = expert_backward(u_again, dy_a, q_a, weights_a, n_group)
         lines = jnp.concatenate([by_home(dgate_rows_a), by_home(dgate_rows_b)], axis=1)
         lines = jnp.pad(lines, ((0, 0), (0, 128 - 2 * block)))[:, None, :]

time: 497 us -> 451 us (0.907)
  waiting for transfers between devices: 44.3 us -> 0 us
  starting transfers between devices: 23.6 us -> 0 us
  Pallas kernels: 378 us -> 398 us
    all_to_all x3 -> x0, waiting for transfers between devices: 44.3 us -> none  [send_back(): return lax.all_to_all(rows, 'ep', 0, 0, tiled=True).reshape(total, width)]
    pallas_call x8 -> x5, Pallas kernels: 287 us -> 314 us  [send_rows(): pl.pallas_call(functools.partial(send_kernel, own, capacity, layer, first...]
    all_to_all x3 -> x0, starting transfers between devices: 23.6 us -> none  [send_back(): return lax.all_to_all(rows, 'ep', 0, 0, tiled=True).reshape(total, width)]
    pallas_call x1, Pallas kernels: 57.2 us -> 51.7 us  [return_home(): pl.pallas_call(return_kernel, out_shape=(jax.ShapeDtypeStruct(x.shape, x....]
    unnamed x85 -> x108, local copies, waits for them, and re-layouts: 16.8 us -> 21 us
  transfers between devices with their start and end apart: 3 -> 0, of which waited for: 1 -> 0; matrix products, arithmetic and copies ran while one was open for 3% -> 0% of each run, Pallas kernels for 34% -> 0%
where the time goes in v7:
time: 451 us; the launch traced here: 450 us
  Pallas kernels  398 us (88%)
  local copies, waits for them, and re-layouts  28.2 us (6%)
  matrix products  18.2 us (4%)
    pallas_call x5, Pallas kernels, send_rows(): pl.pallas_call(functools.partial(send_kernel, own, capacity, layer, first...  314 us
    pallas_call x1, Pallas kernels, return_home(): pl.pallas_call(return_kernel, out_shape=(jax.ShapeDtypeStruct(x.shape, x....  51.7 us
    pallas_call x4, Pallas kernels, expert_call(): pl.pallas_call(functools.partial(kernel, 256), out_shape=tuple((kinds[k][...  32.4 us
    unnamed x108, local copies, waits for them, and re-layouts  21 us

profile of v7, /device:TPU:1, one launch (start us, length us, event | category | flops | bytes accessed | tf_op | source)
XLA Modules:
  0.0 450.0 jit_solution(8107363794344498580)
XLA Ops:
  3.7 1.4 copy.119.refs_4_
  7.1 0.8 copy.114
  9.8 0.9 copy-done.31
  10.7 48.5 %send_rows_0.1 = (bf16[3,1024,512]{2,1,0:T(8,128)(2,1)S(1)}, f32[2,4,4,4,4,8,128]{6,5,4,3,2,1,0:T(8,128)S(1)}) custom-call(bf16[96,512]{1,0:T(8,128)(2,1)S(1)} %copy-done.31, f32[4,8,128]{2,1,0:T(8,128)S(1)} %pad_maximum_fusion.1.refs_1_), custom_call_target="tpu_custom_call" | custom-call | flops 30000001024 | bytes 12582912 | tf_op jit(solution)/shard_map/send_rows_0/pallas_call | solution.py:346
  59.2 6.2 %expert_forward.2.refs_5_ = bf16[128,24,512]{2,1,0:T(8,128)(2,1)S(1)} custom-call(bf16[3,1024,512]{2,1,0:T(8,128)(2,1)S(1)} %get-tuple-element.33.u_ref, bf16[3,512,128]{2,1,0:T(8,128)(2,1)S(1)} %copy-done.17, bf16[3,512,128]{2,1,0:T(8,128)(2,1)S(1)} %copy-done.19, bf16[3,128,512]{2,1,0:T(8,128)(2,1)S(1)} %copy-done.21), custom_call_target="tpu_custom_call" | custom-call | flops 1207959552 | bytes 6291456 | tf_op jit(solution)/shard_map/expert_forward/pallas_call | solution.py:505
  65.4 1.7 copy-done.5
  67.1 78.8 %send_rows_1.1 = (bf16[3,1024,512]{2,1,0:T(8,128)(2,1)S(1)}, bf16[3,1024,512]{2,1,0:T(8,128)(2,1)}, bf16[96,512]{1,0:T(8,128)(2,1)S(1)}) custom-call(bf16[96,512]{1,0:T(8,128)(2,1)S(1)} %copy-done.33, f32[2,4,4,4,4,8,128]{6,5,4,3,2,1,0:T(8,128)S(1)} %get-tuple-element.32.refs_1_, bf16[96,512]{1,0:T(8,128)(2,1)S(1)} %copy-done.31, ...), custom_call_target="tpu_custom_call" | custom-call | flops 30000001024 | bytes 12582912 | tf_op jit(solution)/shard_map/send_rows_1/pallas_call | solution.py:346
  145.9 1.7 copy-done.36
  147.7 36.7 %send_rows_2.1.u_ref = bf16[3,1024,512]{2,1,0:T(8,128)(2,1)S(1)} custom-call(bf16[96,512]{1,0:T(8,128)(2,1)S(1)} %get-tuple-element.34.refs_0_.refs_2_, f32[2,4,4,4,4,8,128]{6,5,4,3,2,1,0:T(8,128)S(1)} %get-tuple-element.32.refs_1_), custom_call_target="tpu_custom_call" | custom-call | flops 30000001024 | bytes 12582912 | tf_op jit(solution)/shard_map/send_rows_2/pallas_call | solution.py:346
  184.4 1.9 copy-done.37
  186.3 10.0 %expert_backward.2 = (bf16[128,24,512]{2,1,0:T(8,128)(2,1)S(1)}, f32[3,8,128]{2,1,0:T(8,128)S(1)}, bf16[3,1024,128]{2,1,0:T(8,128)(2,1)S(1)}, bf16[3,1024,128]{2,1,0:T(8,128)(2,1)S(1)}, bf16[3,1024,128]{2,1,0:T(8,128)(2,1)S(1)}) custom-call(bf16[3,1024,512]{2,1,0:T(8,128)(2,1)S(1)} %send_rows_2.1.u_ref, bf16[3,1024,512]{2,1,0:T(8,128)(2,1)S(1)} %copy-done.37, ...), custom_call_target="tpu_custom_call" | custom-call | flops 3221225472 | bytes 12582912 | tf_op jit(solution)/shard_map/expert_backward/pallas_call | solution.py:505
  196.5 2.1 fusion.15
  198.8 73.8 %send_rows_3.1 = (bf16[3,1024,512]{2,1,0:T(8,128)(2,1)S(1)}, bf16[96,512]{1,0:T(8,128)(2,1)S(1)}) custom-call(bf16[96,512]{1,0:T(8,128)(2,1)S(1)} %copy-done.32, f32[2,4,4,4,4,8,128]{6,5,4,3,2,1,0:T(8,128)S(1)} %get-tuple-element.32.refs_1_, bf16[96,512]{1,0:T(8,128)(2,1)S(1)} %copy-done.33, s32[96,8]{1,0:T(8,128)S(1)} %copy-done.29, ...), custom_call_target="tpu_custom_call" | custom-call | flops 30000001024 | bytes 12582912 | tf_op jit(solution)/shard_map/send_rows_3/pallas_call | solution.py:346
  272.6 1.6 copy-done
  274.9 0.8 reshape.94
  275.7 1.0 copy.122
  276.7 3.3 fusion.13
  280.0 2.1 fusion.14
  282.2 6.2 %expert_forward.3.refs_5_ = bf16[128,24,512]{2,1,0:T(8,128)(2,1)S(1)} custom-call(bf16[3,1024,512]{2,1,0:T(8,128)(2,1)S(1)} %send_rows_2.1.u_ref, bf16[3,512,128]{2,1,0:T(8,128)(2,1)S(1)} %copy-done.12, bf16[3,512,128]{2,1,0:T(8,128)(2,1)S(1)} %copy-done.14, bf16[3,128,512]{2,1,0:T(8,128)(2,1)S(1)} %copy-done.16), custom_call_target="tpu_custom_call" | custom-call | flops 1207959552 | bytes 6291456 | tf_op jit(solution)/shard_map/expert_forward/pallas_call | solution.py:505
  288.4 1.7 copy-done.4
  290.1 76.4 %send_rows_4.1 = (bf16[3,1024,512]{2,1,0:T(8,128)(2,1)S(1)}, bf16[3,1024,512]{2,1,0:T(8,128)(2,1)}, bf16[96,512]{1,0:T(8,128)(2,1)S(1)}) custom-call(bf16[96,512]{1,0:T(8,128)(2,1)S(1)} %copy-done.42, f32[2,4,4,4,4,8,128]{6,5,4,3,2,1,0:T(8,128)S(1)} %copy-done.40, bf16[96,512]{1,0:T(8,128)(2,1)S(1)} %copy-done.45, s32[96,8]{1,0:T(8,128)S(1)} %copy-done.30, ...), custom_call_target="tpu_custom_call" | custom-call | flops 30000001024 | bytes 12582912 | tf_op jit(solution)/shard_map/send_rows_4/pallas_call | solution.py:346
  366.6 1.9 copy-done.2
  368.4 10.0 %expert_backward.3 = (bf16[128,24,512]{2,1,0:T(8,128)(2,1)S(1)}, f32[3,8,128]{2,1,0:T(8,128)S(1)}, bf16[3,1024,128]{2,1,0:T(8,128)(2,1)S(1)}, bf16[3,1024,128]{2,1,0:T(8,128)(2,1)S(1)}, bf16[3,1024,128]{2,1,0:T(8,128)(2,1)S(1)}) custom-call(bf16[3,1024,512]{2,1,0:T(8,128)(2,1)S(1)} %copy-done.1, bf16[3,1024,512]{2,1,0:T(8,128)(2,1)S(1)} %get-tuple-element.41.dy_ref, ...), custom_call_target="tpu_custom_call" | custom-call | flops 3221225472 | bytes 12582912 | tf_op jit(solution)/shard_map/expert_backward/pallas_call | solution.py:505
  378.6 2.0 fusion.12
  380.9 0.8 reshape.92
  381.7 1.0 copy.121
  382.9 1.9 copy-done.35
  384.8 51.7 %return_home.1 = (bf16[96,512]{1,0:T(8,128)(2,1)S(1)}, f32[128,1,128]{2,1,0:T(1,128)S(1)}) custom-call(bf16[96,512]{1,0:T(8,128)(2,1)S(1)} %copy-done.43, s32[96,8]{1,0:T(8,128)S(1)} %copy-done.28, f32[96,8]{1,0:T(8,128)S(1)} %copy-done.24, bf16[128,24,512]{2,1,0:T(8,128)(2,1)S(1)} %copy-done.35, f32[128,1,128]{2,1,0:T(1,128)S(1)} %bitcast.33), custom_call_target="tpu_custom_call" | custom-call | flops 30000001024 | bytes 6291456 | tf_op jit(solution)/shard_map/return_home/pallas_call | solution.py:408
  437.7 1.7 fusion.7
  440.9 1.7 fusion.6
  443.3 3.3 fusion.10
  446.6 2.1 fusion.11
  (126 shorter events, 13.1 us)
Async XLA Ops:
  3.7 61.7 %copy-start.23 = (f32[96,8]{1,0:T(8,128)}, f32[96,8]{1,0:T(8,128)S(1)}, u32[]{:S(2)}) copy-start(f32[96,8]{1,0:T(8,128)S(1)} %copy.118.refs_4_.gate_ref) | copy-start | bytes 9220
  7.1 58.4 %copy-start.27 = (s32[96,8]{1,0:T(8,128)}, s32[96,8]{1,0:T(8,128)S(1)}, u32[]{:S(2)}) copy-start(s32[96,8]{1,0:T(8,128)S(1)} %get-tuple-element.97.refs_3_.row_ref) | copy-start | bytes 9220
  10.7 48.5 %copy-start.17 = (bf16[3,512,128]{2,1,0:T(8,128)(2,1)S(1)}, bf16[3,512,128]{2,1,0:T(8,128)(2,1)}, u32[]{:S(2)}) copy-start(bf16[3,512,128]{2,1,0:T(8,128)(2,1)} %w1_ref.7) | copy-start | bytes 1179652
  10.7 48.5 %copy-start.19 = (bf16[3,512,128]{2,1,0:T(8,128)(2,1)S(1)}, bf16[3,512,128]{2,1,0:T(8,128)(2,1)}, u32[]{:S(2)}) copy-start(bf16[3,512,128]{2,1,0:T(8,128)(2,1)} %w3_ref.7) | copy-start | bytes 1179652
  10.7 48.5 %copy-start.21 = (bf16[3,128,512]{2,1,0:T(8,128)(2,1)S(1)}, bf16[3,128,512]{2,1,0:T(8,128)(2,1)}, u32[]{:S(2)}) copy-start(bf16[3,128,512]{2,1,0:T(8,128)(2,1)} %w2_ref.7) | copy-start | bytes 1179652
  59.2 139.6 %copy-start.39 = (f32[2,4,4,4,4,8,128]{6,5,4,3,2,1,0:T(8,128)}, f32[2,4,4,4,4,8,128]{6,5,4,3,2,1,0:T(8,128)S(1)}, u32[]{:S(2)}) copy-start(f32[2,4,4,4,4,8,128]{6,5,4,3,2,1,0:T(8,128)S(1)} %get-tuple-element.32.refs_1_) | copy-start | bytes 6291460
  59.2 7.9 %copy-start.33 = (bf16[96,512]{1,0:T(8,128)(2,1)S(1)}, bf16[96,512]{1,0:T(8,128)(2,1)}, u32[]{:S(2)}) copy-start(bf16[96,512]{1,0:T(8,128)(2,1)} %refs_2_.3) | copy-start | bytes 294916
  147.6 36.8 %copy-start.44 = (bf16[96,512]{1,0:T(8,128)(2,1)}, bf16[96,512]{1,0:T(8,128)(2,1)S(1)}, u32[]{:S(2)}) copy-start(bf16[96,512]{1,0:T(8,128)(2,1)S(1)} %get-tuple-element.34.refs_0_.refs_2_) | copy-start | bytes 294916
  147.6 36.8 %copy-start.3 = (bf16[3,1024,512]{2,1,0:T(8,128)(2,1)S(1)}, bf16[3,1024,512]{2,1,0:T(8,128)(2,1)}, u32[]{:S(2)}) copy-start(bf16[3,1024,512]{2,1,0:T(8,128)(2,1)} %get-tuple-element.36.q_ref) | copy-start | bytes 9437188
  147.6 36.8 %copy-start.12 = (bf16[3,512,128]{2,1,0:T(8,128)(2,1)S(1)}, bf16[3,512,128]{2,1,0:T(8,128)(2,1)}, u32[]{:S(2)}) copy-start(bf16[3,512,128]{2,1,0:T(8,128)(2,1)} %w1_ref.6) | copy-start | bytes 1179652
  147.6 36.8 %copy-start.13 = (bf16[3,512,128]{2,1,0:T(8,128)(2,1)S(1)}, bf16[3,512,128]{2,1,0:T(8,128)(2,1)}, u32[]{:S(2)}) copy-start(bf16[3,512,128]{2,1,0:T(8,128)(2,1)} %w3_ref.6) | copy-start | bytes 1179652
  147.6 36.8 %copy-start.15 = (bf16[3,128,512]{2,1,0:T(8,128)(2,1)S(1)}, bf16[3,128,512]{2,1,0:T(8,128)(2,1)}, u32[]{:S(2)}) copy-start(bf16[3,128,512]{2,1,0:T(8,128)(2,1)} %w2_ref.6) | copy-start | bytes 1179652
  196.4 2.4 copy-start.38
  276.7 3.3 copy-start.10
  282.1 7.9 %copy-start.26 = (f32[96,8]{1,0:T(8,128)S(1)}, f32[96,8]{1,0:T(8,128)}, u32[]{:S(2)}) copy-start(f32[96,8]{1,0:T(8,128)} %copy.119.refs_4_) | copy-start | bytes 9220
  282.1 7.9 %copy-start.30 = (s32[96,8]{1,0:T(8,128)S(1)}, s32[96,8]{1,0:T(8,128)}, u32[]{:S(2)}) copy-start(s32[96,8]{1,0:T(8,128)} %get-tuple-element.99.refs_3_) | copy-start | bytes 9220
  282.1 7.9 %copy-start.40 = (f32[2,4,4,4,4,8,128]{6,5,4,3,2,1,0:T(8,128)S(1)}, f32[2,4,4,4,4,8,128]{6,5,4,3,2,1,0:T(8,128)}, u32[]{:S(2)}) copy-start(f32[2,4,4,4,4,8,128]{6,5,4,3,2,1,0:T(8,128)} %copy-done.39) | copy-start | bytes 6291460
  282.2 7.9 %copy-start.42 = (bf16[96,512]{1,0:T(8,128)(2,1)S(1)}, bf16[96,512]{1,0:T(8,128)(2,1)}, u32[]{:S(2)}) copy-start(bf16[96,512]{1,0:T(8,128)(2,1)} %copy-done.41) | copy-start | bytes 294916
  282.2 7.9 %copy-start.45 = (bf16[96,512]{1,0:T(8,128)(2,1)S(1)}, bf16[96,512]{1,0:T(8,128)(2,1)}, u32[]{:S(2)}) copy-start(bf16[96,512]{1,0:T(8,128)(2,1)} %copy-done.44) | copy-start | bytes 294916
  290.1 76.4 %copy-start.1 = (bf16[3,1024,512]{2,1,0:T(8,128)(2,1)S(1)}, bf16[3,1024,512]{2,1,0:T(8,128)(2,1)}, u32[]{:S(2)}) copy-start(bf16[3,1024,512]{2,1,0:T(8,128)(2,1)} %copy-done) | copy-start | bytes 9437188
  290.1 76.4 %copy-start.18 = (bf16[3,512,128]{2,1,0:T(8,128)(2,1)S(1)}, bf16[3,512,128]{2,1,0:T(8,128)(2,1)}, u32[]{:S(2)}) copy-start(bf16[3,512,128]{2,1,0:T(8,128)(2,1)} %w1_ref.7) | copy-start | bytes 1179652
  290.1 76.4 %copy-start.20 = (bf16[3,512,128]{2,1,0:T(8,128)(2,1)S(1)}, bf16[3,512,128]{2,1,0:T(8,128)(2,1)}, u32[]{:S(2)}) copy-start(bf16[3,512,128]{2,1,0:T(8,128)(2,1)} %w3_ref.7) | copy-start | bytes 1179652
  290.1 76.4 %copy-start.22 = (bf16[3,128,512]{2,1,0:T(8,128)(2,1)S(1)}, bf16[3,128,512]{2,1,0:T(8,128)(2,1)}, u32[]{:S(2)}) copy-start(bf16[3,128,512]{2,1,0:T(8,128)(2,1)} %w2_ref.7) | copy-start | bytes 1179652
  378.5 2.4 copy-start.34
  378.5 4.3 copy-start.24
  378.5 4.3 copy-start.28
  378.6 4.3 copy-start.43
  384.8 52.9 %copy-start.48 = (s32[768]{0:T(1024)S(1)}, s32[768]{0:T(1024)}, u32[]{:S(2)}) copy-start(s32[768]{0:T(1024)} %get-tuple-element.100) | copy-start | bytes 9220
  384.8 52.9 %copy-start.49 = (s32[768]{0:T(1024)S(1)}, s32[768]{0:T(1024)}, u32[]{:S(2)}) copy-start(s32[768]{0:T(1024)} %get-tuple-element.101) | copy-start | bytes 9220
  384.8 56.1 %copy-start.46 = (s32[768]{0:T(1024)S(1)}, s32[768]{0:T(1024)}, u32[]{:S(2)}) copy-start(s32[768]{0:T(1024)} %get-tuple-element.102) | copy-start | bytes 9220
  384.8 56.1 %copy-start.47 = (s32[768]{0:T(1024)S(1)}, s32[768]{0:T(1024)}, u32[]{:S(2)}) copy-start(s32[768]{0:T(1024)} %get-tuple-element.103) | copy-start | bytes 9220
  443.3 3.3 copy-start.7
  (18 other events, 33.8 us)

commit v8 on v7

--- a/solution.py
+++ b/solution.py
@@ -12,12 +12,50 @@
 BF16 = jnp.bfloat16
 
 
-def pair_rows(ids, capacity):
-    flat = ids.reshape(-1)
-    pair = jnp.arange(flat.shape[0], dtype=jnp.int32)
-    earlier = (flat[None, :] == flat[:, None]) & (pair[None, :] < pair[:, None])
-    slot = jnp.sum(earlier.astype(jnp.int32), axis=1)
-    return (flat * capacity + slot).reshape(ids.shape)
+def table_kernel(experts, capacity, ids_a_ref, ids_b_ref, gate_a_ref, gate_b_ref, tile_ref, code_a_ref, code_b_ref, gates_a_ref, gates_b_ref):
+    top_k, tok_dev = ids_a_ref.shape
+    full = 128
+    expert = lax.broadcasted_iota(jnp.int32, (full, experts), 1)
+    row = lax.broadcasted_iota(jnp.int32, (full, full), 0)
+    lane = lax.broadcasted_iota(jnp.int32, (full, full), 1)
+    earlier = jnp.where(lane < row, 1.0, 0.0).astype(BF16)
+
+    def turned(value, fill):
+        value = jnp.concatenate([value.astype(F32), jnp.full((top_k, full - tok_dev), fill, F32)], axis=1)
+        return value, jnp.concatenate([value, jnp.full((full - top_k, full), fill, F32)], axis=0).T
+
+    for layer, (ids_ref, code_ref) in enumerate(((ids_a_ref, code_a_ref), (ids_b_ref, code_b_ref))):
+        ids = turned(ids_ref[...], -1.0)[1].astype(jnp.int32)
+        hits = [ids[:, j:j + 1] == expert for j in range(top_k)]
+        chosen = jnp.zeros((full, experts), F32)
+        for hit in hits:
+            chosen = jnp.where(hit, 1.0, chosen)
+        before = jnp.dot(earlier, chosen.astype(BF16), preferred_element_type=F32)
+        code = jnp.full((full, full), -1.0, F32)
+        for j, hit in enumerate(hits):
+            slot = jnp.sum(jnp.where(hit, before, 0.0), axis=1, keepdims=True)
+            code = jnp.where(lane == j, ids[:, j:j + 1].astype(F32) * capacity + slot, code)
+        code = jnp.where(row < tok_dev, code, -1.0)
+        code_ref[...] = code[:tok_dev, :top_k].astype(jnp.int32)
+        tile_ref[layer] = code.T[:top_k]
+    for layer, (gate_ref, out_ref) in enumerate(((gate_a_ref, gates_a_ref), (gate_b_ref, gates_b_ref))):
+        tile, by_token = turned(gate_ref[...], 0.0)
+        tile_ref[2 + layer] = tile
+        out_ref[...] = by_token[:tok_dev, :top_k]
+
+
+def make_tables(idx_a, idx_b, gate_a, gate_b, experts, capacity):
+    tok_dev, top_k = idx_a.shape
+    codes = jax.ShapeDtypeStruct((tok_dev, top_k), jnp.int32)
+    gates = jax.ShapeDtypeStruct((tok_dev, top_k), F32)
+    vmem = pl.BlockSpec(memory_space=pltpu.VMEM)
+    return pl.pallas_call(
+        functools.partial(table_kernel, experts, capacity),
+        out_shape=(jax.ShapeDtypeStruct((4, top_k, 128), F32), codes, codes, gates, gates),
+        in_specs=[vmem] * 4,
+        out_specs=(vmem,) * 5,
+        name="make_tables",
+    )(idx_a.T, idx_b.T, gate_a.T, gate_b.T)
 
 
 SIDE = 4
@@ -112,11 +150,12 @@
     return ((g * count, back[pl.ds(g, group)].reshape(group * count, width)) for g in range(0, back.shape[0], group))
 
 
-def send_kernel(own, capacity, layer, first, scaled, returning, *refs):
+def send_kernel(own, capacity, layer, first, scaled, returning, work, *refs):
     refs = list(refs)
     x_ref, tile_ref = refs.pop(0), refs.pop(0)
     if returning:
         base_ref, row_ref, gate_ref, rows_ref = (refs.pop(0) for _ in range(4))
+    work_in = [refs.pop(0) for _ in range(work[1])] if work else []
     u_ref = refs.pop(0)
     if scaled:
         q_ref = refs.pop(0)
@@ -124,6 +163,7 @@
         table_ref = refs.pop(0)
     if returning:
         home_ref = refs.pop(0)
+    work_out = [refs.pop(0) for _ in range(work[2])] if work else []
     held, local_sem, send_sem, recv_sem = (refs.pop(0) for _ in range(4))
     tiles = refs.pop(0) if first else tile_ref
     if returning:
@@ -309,10 +349,15 @@
     if returning:
         vias, directs, forwards, finish = return_steps(me, core, at, rows_ref, back, relay, return_sems, relay_sems)
         between = {0: vias[:1], 1: vias[1:2], 2: vias[2:3], 3: vias[3:] + directs[:1], 4: forwards[:1] + directs[1:2], 5: forwards[1:2] + directs[2:3], 6: forwards[2:4] + directs[3:], 7: forwards[4:5], 8: forwards[5:7], 9: forwards[7:]}
+    jobs = work[0](work_in, work_out) if work else []
     for n, step in enumerate(gathering):
         step()
         for extra in between.get(n, []):
             extra()
+        if 3 <= n and jobs:
+            jobs.pop(0)()
+    for job in jobs:
+        job()
     last_rows(2)
     arrive_across(2)
     lax.fori_loop(0, 3, farthest_rows, 0)
@@ -331,7 +376,7 @@
     return [pltpu.VMEM(sent.shape, sent.dtype), pltpu.VMEM((RELAYS,) + sent.shape[1:], sent.dtype), pltpu.SemaphoreType.DMA((5,)), pltpu.SemaphoreType.DMA((RELAYS,))]
 
 
-def send_rows(x, table, layer, own, capacity, call_id, first=False, scaled=False, home=None, gated=False):
+def send_rows(x, table, layer, own, capacity, call_id, first=False, scaled=False, home=None, gated=False, work=None):
     tok_dev, width = x.shape
     devices = 2 * SIDE ** 3
     count = 228 if first else 114
@@ -340,13 +385,15 @@
     outs = (u_shape,) + (u_shape,) * scaled + (table_shape,) * first
     if home:
         outs += (jax.ShapeDtypeStruct(home[0].shape, home[0].dtype),)
+    jobs, job_in, job_out = work or (None, (), ())
+    outs += tuple(job_out)
     vmem = pl.BlockSpec(memory_space=pltpu.VMEM)
     hbm = pl.BlockSpec(memory_space=pl.ANY)
     returning = None if home is None else "gated" if gated else "plain"
     return pl.pallas_call(
-        functools.partial(send_kernel, own, capacity, layer, first, scaled, returning),
+        functools.partial(send_kernel, own, capacity, layer, first, scaled, returning, work and (jobs, len(job_in), len(job_out))),
         out_shape=outs,
-        in_specs=[hbm, hbm if first else vmem] + [vmem] * (4 if home else 0),
+        in_specs=[hbm, hbm if first else vmem] + [vmem] * ((4 if home else 0) + len(job_in)),
         out_specs=(vmem,) * len(outs),
         scratch_shapes=[
             pltpu.VMEM((2, SIDE, SIDE, SIDE, tok_dev, width), x.dtype),
@@ -354,10 +401,10 @@
             pltpu.SemaphoreType.DMA((count,)),
             pltpu.SemaphoreType.DMA((count,)),
         ] + ([pltpu.VMEM(table_shape.shape, F32)] if first else []) + (return_scratch(home[3]) if home else []),
-        compiler_params=pltpu.CompilerParams(collective_id=call_id, has_side_effects=True, vmem_limit_bytes=46 * 1024 * 1024),
+        compiler_params=pltpu.CompilerParams(collective_id=call_id, has_side_effects=True, vmem_limit_bytes=54 * 1024 * 1024),
         cost_estimate=pl.CostEstimate(flops=3 * 10**10, bytes_accessed=devices * tok_dev * width * 2, transcendentals=0),
         name=f"send_rows_{call_id}",
-    )(x, table, *(home or ()))
+    )(x, table, *(home or ()), *job_in)
 
 
 def pair_sum(gated, row_ref, gate_ref, back):
@@ -381,54 +428,70 @@
     return total
 
 
-def return_kernel(x_ref, row_ref, gate_ref, rows_ref, line_ref, out_ref, line_out, back, relay, sems, relay_sems):
+def look_up(lines, codes, per_device, first_lane):
+    device = jnp.floor((codes.astype(F32) + 0.5) * (1.0 / per_device))
+    place = codes.astype(F32) - device * per_device + first_lane
+    hi = lines.astype(BF16)
+    rest = lines - hi.astype(F32)
+    mid = rest.astype(BF16)
+    terms = jnp.concatenate([hi, mid, (rest - mid.astype(F32)).astype(BF16)], axis=1)
+    tok_dev, top_k = codes.shape
+    lane = lax.broadcasted_iota(jnp.int32, (tok_dev, 128), 1).astype(F32)
+    out = jnp.zeros((tok_dev, 128), F32)
+    for j in range(top_k):
+        onehot = jnp.where(device[:, j:j + 1] == lane, 1.0, 0.0).astype(BF16)
+        picked = jnp.dot(onehot, terms, preferred_element_type=F32)
+        picked = picked[:, :128] + (picked[:, 128:256] + picked[:, 256:])
+        value = jnp.sum(jnp.where(place[:, j:j + 1] == lane, picked, 0.0), axis=1, keepdims=True)
+        out = jnp.where(lane == j, value, out)
+    return out[:, :top_k]
+
+
+def return_kernel(per_device, x_ref, row_ref, gate_ref, rows_ref, line_a_ref, line_b_ref, row_b_ref, u_ref, q_ref, hidden_ref, da_ref, db_ref, out_ref, dgate_a_ref, dgate_b_ref, dw1_ref, dw3_ref, dw2_ref, back, relay, sems, relay_sems, line_ref, line_back):
     me, core, at = my_place()
     devices = rows_ref.shape[0]
+    line_ref[...] = line_a_ref[...] + line_b_ref[...]
     greet_all(me, core, at)
     vias, directs, forwards, finish = return_steps(me, core, at, rows_ref, back, relay, sems, relay_sems)
 
     def send_line(step, carry):
         to = lax.rem(me + step, devices)
-        pltpu.make_async_remote_copy(src_ref=line_ref.at[to], dst_ref=line_out.at[me], send_sem=sems.at[3], recv_sem=sems.at[4], device_id={"ep": to}, device_id_type=pl.DeviceIdType.MESH).start()
+        pltpu.make_async_remote_copy(src_ref=line_ref.at[to], dst_ref=line_back.at[me], send_sem=sems.at[3], recv_sem=sems.at[4], device_id={"ep": to}, device_id_type=pl.DeviceIdType.MESH).start()
         return carry
 
-    for step in vias + directs[:2] + forwards[:2] + directs[2:] + forwards[2:]:
+    jobs = grad_jobs([u_ref, q_ref, hidden_ref, da_ref, db_ref], [dw1_ref, dw3_ref, dw2_ref])
+    for step in vias + directs[:2] + forwards[:2] + directs[2:] + forwards[2:4]:
         step()
     lax.fori_loop(1, devices, send_line, 0)
-    line_out[me] = line_ref[me]
-    finish()
+    for n, step in enumerate(forwards[4:]):
+        step()
+        if jobs:
+            jobs.pop(0)()
+    line_back[me] = line_ref[me]
     others = pl.ds(0, devices - 1)
     for k in (3, 4):
-        pltpu.make_async_copy(line_ref.at[others], line_out.at[others], sems.at[k]).wait()
+        pltpu.make_async_copy(line_ref.at[others], line_back.at[others], sems.at[k]).wait()
+    lines = line_back[...].reshape(devices, 128)
+    dgate_a_ref[...] = look_up(lines, row_ref[...], per_device, 0)
+    dgate_b_ref[...] = look_up(lines, row_b_ref[...], per_device, per_device)
+    finish()
     out_ref[...] = (x_ref[...].astype(F32) + pair_sum(False, row_ref, gate_ref, home_blocks(back))).astype(out_ref.dtype)
 
 
-def return_home(x, rows, gates, sent, lines, call_id):
+def return_home(x, rows, gates, sent, line_a, line_b, rows_b, saved, grad_shapes, per_device, call_id):
     vmem = pl.BlockSpec(memory_space=pltpu.VMEM)
+    dgate = jax.ShapeDtypeStruct(rows.shape, F32)
+    outs = (jax.ShapeDtypeStruct(x.shape, x.dtype), dgate, dgate) + tuple(grad_shapes)
     return pl.pallas_call(
-        return_kernel,
-        out_shape=(jax.ShapeDtypeStruct(x.shape, x.dtype), jax.ShapeDtypeStruct(lines.shape, lines.dtype)),
-        in_specs=[vmem] * 5,
-        out_specs=(vmem, vmem),
-        scratch_shapes=return_scratch(sent),
-        compiler_params=pltpu.CompilerParams(collective_id=call_id, has_side_effects=True, vmem_limit_bytes=32 * 1024 * 1024),
+        functools.partial(return_kernel, per_device),
+        out_shape=outs,
+        in_specs=[vmem] * (7 + len(saved)),
+        out_specs=(vmem,) * len(outs),
+        scratch_shapes=return_scratch(sent) + [pltpu.VMEM(line_a.shape, F32)] * 2,
+        compiler_params=pltpu.CompilerParams(collective_id=call_id, has_side_effects=True, vmem_limit_bytes=40 * 1024 * 1024),
         cost_estimate=pl.CostEstimate(flops=3 * 10**10, bytes_accessed=sent.size * 4, transcendentals=0),
         name="return_home",
-    )(x, rows, gates, sent, lines)
-
-
-def combine(x, rows, gates, back, gated):
-    tok_dev, width = x.shape
-    flops = 2 * tok_dev * back.shape[0] * width
-    return pl.pallas_call(
-        functools.partial(combine_kernel, gated),
-        out_shape=jax.ShapeDtypeStruct(x.shape, x.dtype),
-        in_specs=[pl.BlockSpec(memory_space=pltpu.VMEM)] * 4,
-        out_specs=pl.BlockSpec(memory_space=pltpu.VMEM),
-        compiler_params=pltpu.CompilerParams(vmem_limit_bytes=24 * 1024 * 1024),
-        cost_estimate=pl.CostEstimate(flops=flops * (3 if gated else 1), bytes_accessed=back.size * 2, transcendentals=0),
-        name="combine",
-    )(x, rows, gates, back)
+    )(x, rows, gates, sent, line_a, line_b, rows_b, *saved)
 
 
 def forward_rows(u, w_both, w_down):
@@ -461,7 +524,45 @@
     lax.fori_loop(0, u_ref.shape[1] // chunk, body, 0)
 
 
-def backward_kernel(chunk, u_ref, dy_ref, q_ref, w1_ref, w3_ref, w2_ref, du_ref, dgate_ref, hidden_ref, da_ref, db_ref):
+def forward_jobs(ins, outs):
+    u_ref, w1_ref, w3_ref, w2_ref = ins
+    out_ref, = outs
+    chunk = 256
+    own, count, width = u_ref.shape
+    sources = out_ref.shape[0] * chunk // count
+    slots = out_ref.shape[1] // own
+
+    def job(e):
+        w_both = jnp.concatenate([w1_ref[e], w3_ref[e]], axis=1)
+
+        def body(step, carry):
+            rows = pl.ds(pl.multiple_of(step * chunk, chunk), chunk)
+            out = forward_rows(u_ref[e, rows, :], w_both, w2_ref[e])[-1]
+            out_ref[pl.ds(step * sources, sources), e * slots:(e + 1) * slots, :] = out.reshape(sources, slots, width).astype(BF16)
+            return carry
+
+        lax.fori_loop(0, count // chunk, body, 0)
+
+    return [functools.partial(job, e) for e in range(own)]
+
+
+def grad_jobs(ins, outs):
+    u_ref, q_ref, hidden_ref, da_ref, db_ref = ins
+    dw1_ref, dw3_ref, dw2_ref = outs
+    ff = da_ref.shape[2]
+    rows = (((0,), (0,)), ((), ()))
+
+    def job(e):
+        both = jnp.concatenate([da_ref[e], db_ref[e]], axis=1)
+        dw = lax.dot_general(u_ref[e], both, rows, preferred_element_type=F32)
+        dw1_ref[e] = dw[:, :ff]
+        dw3_ref[e] = dw[:, ff:]
+        dw2_ref[e] = lax.dot_general(hidden_ref[e], q_ref[e], rows, preferred_element_type=F32)
+
+    return [functools.partial(job, e) for e in range(u_ref.shape[0])]
+
+
+def backward_kernel(first_lane, chunk, u_ref, dy_ref, q_ref, w1_ref, w3_ref, w2_ref, du_ref, dgate_ref, hidden_ref, da_ref, db_ref):
     ff = w2_ref.shape[1]
     w_both = jnp.concatenate([w1_ref[0], w3_ref[0]], axis=1)
     last = (((1,), (1,)), ((), ()))
@@ -470,10 +571,13 @@
         rows = pl.ds(pl.multiple_of(step * chunk, chunk), chunk)
         pre_gate, pre_up, sig, silu, hidden, out = forward_rows(u_ref[0, rows, :], w_both, w2_ref[0])
         dgate = jnp.sum(dy_ref[0, rows, :].astype(F32) * out.astype(BF16).astype(F32), axis=1, keepdims=True)
-        diagonal = lax.broadcasted_iota(jnp.int32, (128, 128), 0) == lax.broadcasted_iota(jnp.int32, (128, 128), 1)
-        for k in range(chunk // 128):
-            line = jnp.sum(jnp.where(diagonal, dgate[k * 128:(k + 1) * 128], 0.0), axis=0, keepdims=True)
-            dgate_ref[0, pl.ds(step * (chunk // 128) + k, 1), :] = line
+        slots = du_ref.shape[1]
+        lane = lax.broadcasted_iota(jnp.int32, (chunk, 128), 1)
+        wanted = lax.rem(lax.broadcasted_iota(jnp.int32, (chunk, 128), 0), slots) + first_lane + pl.program_id(0) * slots
+        line = jnp.where(lane == wanted, dgate, 0.0).reshape(chunk // slots, slots, 128)
+        line = jnp.sum(line, axis=1, keepdims=True)
+        at = pl.ds(step * (chunk // slots), chunk // slots)
+        dgate_ref[at] = jnp.where(pl.program_id(0) == 0, 0.0, dgate_ref[at]) + line
         d_hidden = lax.dot_general(q_ref[0, rows, :], w2_ref[0], last, preferred_element_type=F32)
         da = (d_hidden * pre_up * sig * (1.0 + pre_gate * (1.0 - sig))).astype(BF16)
         db = (d_hidden * silu).astype(BF16)
@@ -498,7 +602,7 @@
     home = (jax.ShapeDtypeStruct((n_group, own * slots, width), BF16), pl.BlockSpec((n_group, slots, width), lambda e: (0, e, 0)))
     kinds = {
         "home": home,
-        "gate": (jax.ShapeDtypeStruct((own, count // 128, 128), F32), each((count // 128, 128))),
+        "gate": (jax.ShapeDtypeStruct((n_group, 1, 128), F32), pl.BlockSpec((n_group, 1, 128), lambda e: (0, 0, 0))),
         "ff": (jax.ShapeDtypeStruct((own, count, ff), BF16), each((count, ff))),
     }
     steps = 3 if len(outs) == 1 else 8
@@ -518,17 +622,11 @@
     return expert_call(forward_kernel, (u_rows,), ("home",), weights, n_group, "expert_forward")[0]
 
 
-def expert_backward(u_rows, dy_rows, q_rows, weights, n_group):
+def expert_backward(u_rows, dy_rows, q_rows, weights, n_group, first_lane):
     outs = ("home", "gate", "ff", "ff", "ff")
-    du, dgate, hidden, da, db = expert_call(backward_kernel, (u_rows, dy_rows, q_rows), outs, weights, n_group, "expert_backward")
-
-    def grads(u_rows, q_rows, hidden, da, db):
-        dw_gate = jnp.einsum("erd,erf->edf", u_rows, da, preferred_element_type=F32)
-        dw_up = jnp.einsum("erd,erf->edf", u_rows, db, preferred_element_type=F32)
-        dw_down = jnp.einsum("erf,erd->efd", hidden, q_rows, preferred_element_type=F32)
-        return dw_gate, dw_up, dw_down
-
-    return du, dgate, grads(u_rows, q_rows, hidden, da, db)
+    kernel = functools.partial(backward_kernel, first_lane)
+    du, lines, *saved = expert_call(kernel, (u_rows, dy_rows, q_rows), outs, weights, n_group, "expert_backward")
+    return du, lines, (u_rows, q_rows, *saved)
 
 
 def solution(mesh):
@@ -544,36 +642,20 @@
         total = own * n_group * capacity
         block = own * capacity
 
-        rows_a = pair_rows(idx_a, capacity)
-        rows_b = pair_rows(idx_b, capacity)
-        pad = ((0, 0), (0, 128 - tok_dev))
-        tile = jnp.stack([jnp.pad(rows_a.T.astype(F32), pad, constant_values=-1.0), jnp.pad(rows_b.T.astype(F32), pad, constant_values=-1.0), jnp.pad(gate_a.T, pad), jnp.pad(gate_b.T, pad)])
+        tile, rows_a, rows_b, gates_a, gates_b = make_tables(idx_a, idx_b, gate_a, gate_b, own * n_group, capacity)
         u_a, table = send_rows(x_in, tile, 0, own, capacity, 0, first=True)
-
-        def by_home(dgate_rows):
-            return dgate_rows.reshape(own, n_group, capacity).transpose(1, 0, 2).reshape(n_group, block)
-
-        def look_up(back, rows):
-            flat = rows.reshape(-1)
-            expert = lax.div(flat, capacity)[:, None] == jnp.arange(own * n_group, dtype=jnp.int32)[None, :]
-            picked = jnp.dot(expert.astype(F32), back.reshape(own * n_group, capacity), precision=lax.Precision.HIGHEST)
-            slot = lax.rem(flat, capacity)[:, None] == jnp.arange(capacity, dtype=jnp.int32)[None, :]
-            return jnp.sum(jnp.where(slot, picked, 0.0), axis=1).reshape(rows.shape)
 
         weights_a, weights_b = (w1_a, w3_a, w2_a), (w1_b, w3_b, w2_b)
         out_a = expert_forward(u_a, weights_a, n_group)
-        dy_b, q_b, x_mid = send_rows(dy_out, table, 1, own, capacity, 1, scaled=True, home=(x_in, rows_a, gate_a, out_a), gated=True)
+        dy_b, q_b, x_mid = send_rows(dy_out, table, 1, own, capacity, 1, scaled=True, home=(x_in, rows_a, gates_a, out_a), gated=True)
         u_b, = send_rows(x_mid, table, 1, own, capacity, 2)
-        out_b = expert_forward(u_b, weights_b, n_group)
-        du_b, dgate_rows_b, grads_b = expert_backward(u_b, dy_b, q_b, weights_b, n_group)
-        u_again, dx_mid = send_rows(x_in, table, 0, own, capacity, 3, home=(dy_out, rows_b, gate_b, du_b))
-        dy_a, q_a, x_out = send_rows(dx_mid, table, 0, own, capacity, 4, scaled=True, home=(x_mid, rows_b, gate_b, out_b), gated=True)
-        du_a, dgate_rows_a, grads_a = expert_backward(u_again, dy_a, q_a, weights_a, n_group)
-        lines = jnp.concatenate([by_home(dgate_rows_a), by_home(dgate_rows_b)], axis=1)
-        lines = jnp.pad(lines, ((0, 0), (0, 128 - 2 * block)))[:, None, :]
-        dx_in, lines = return_home(dx_mid, rows_a, gate_a, du_a, lines, 5)
-        dgate_a = look_up(lines[:, 0, :block], rows_a)
-        dgate_b = look_up(lines[:, 0, block:2 * block], rows_b)
+        du_b, line_b, saved_b = expert_backward(u_b, dy_b, q_b, weights_b, n_group, block)
+        forward_b = (forward_jobs, (u_b,) + weights_b, (jax.ShapeDtypeStruct((n_group, block, width), BF16),))
+        u_again, dx_mid, out_b = send_rows(x_in, table, 0, own, capacity, 3, home=(dy_out, rows_b, gates_b, du_b), work=forward_b)
+        grad_shapes = tuple(jax.ShapeDtypeStruct(w.shape, F32) for w in weights_b)
+        dy_a, q_a, x_out, *grads_b = send_rows(dx_mid, table, 0, own, capacity, 4, scaled=True, home=(x_mid, rows_b, gates_b, out_b), gated=True, work=(grad_jobs, saved_b, grad_shapes))
+        du_a, line_a, saved_a = expert_backward(u_again, dy_a, q_a, weights_a, n_group, 0)
+        dx_in, dgate_a, dgate_b, *grads_a = return_home(dx_mid, rows_a, gates_a, du_a, line_a, line_b, rows_b, saved_a, grad_shapes, block, 5)
         return (x_out, dx_in) + tuple(grads_a) + tuple(grads_b) + (dgate_a, dgate_b)
 
     return jax.shard_map(device_program, mesh=mesh, in_specs=(tok_spec,) * 6 + (w_spec,) * 6, out_specs=(tok_spec,) * 10, check_vma=False)

time: 451 us -> 443 us (0.982)
  matrix products: 18.2 us -> 0 us
  Pallas kernels: 398 us -> 415 us
    pallas_call x5, Pallas kernels: 314 us -> 333 us  [send_rows(): pl.pallas_call(functools.partial(send_kernel, own, capacity, layer, first...]
    dot_general x8 -> x0, matrix products: 18.2 us -> none  [the longest x2 6.61 us: grads(): dw_gate = jnp.einsum('erd,erf->edf', u_rows, da, preferred_element_type=F32)]
    pallas_call x4 -> x3, Pallas kernels: 32.4 us -> 26.3 us  [expert_call(): pl.pallas_call(functools.partial(kernel, 256), out_shape=tuple((kinds[k][...]
    unnamed x108 -> x66, local copies, waits for them, and re-layouts: 21 us -> 26.9 us
    pallas_call x1 -> x2, Pallas kernels: 51.7 us -> 55.3 us  [the longest x1 51.1 us: return_home(): pl.pallas_call(functools.partial(return_kernel, per_device), out_shape=ou...]
where the time goes in v8:
time: 443 us; the launch traced here: 442 us
  Pallas kernels  415 us (94%)
  local copies, waits for them, and re-layouts  26.9 us (6%)
    pallas_call x5, Pallas kernels, send_rows(): pl.pallas_call(functools.partial(send_kernel, own, capacity, layer, first...  333 us
    pallas_call x1, Pallas kernels, return_home(): pl.pallas_call(functools.partial(return_kernel, per_device), out_shape=ou...  51.1 us
    unnamed x66, local copies, waits for them, and re-layouts  26.9 us
    pallas_call x3, Pallas kernels, expert_call(): pl.pallas_call(functools.partial(kernel, 256), out_shape=tuple((kinds[k][...  26.3 us

profile of v8, /device:TPU:1, one launch (start us, length us, event | category | flops | bytes accessed | tf_op | source)
XLA Modules:
  0.0 442.4 jit_solution(9673221337682604916)
XLA Ops:
  0.6 4.3 make_tables.1
  4.9 51.5 %send_rows_0.1 = (bf16[3,1024,512]{2,1,0:T(8,128)(2,1)}, f32[2,4,4,4,4,8,128]{6,5,4,3,2,1,0:T(8,128)}) custom-call(bf16[96,512]{1,0:T(8,128)(2,1)} %refs_0_.5, f32[4,8,128]{2,1,0:T(8,128)} %get-tuple-element.45.refs_1_), custom_call_target="tpu_custom_call" | custom-call | flops 30000001024 | bytes 12582912 | tf_op jit(solution)/shard_map/send_rows_0/pallas_call | solution.py:393
  56.4 1.9 copy-done.1
  58.3 6.1 %expert_forward.1.refs_5_ = bf16[128,24,512]{2,1,0:T(8,128)(2,1)S(1)} custom-call(bf16[3,1024,512]{2,1,0:T(8,128)(2,1)S(1)} %copy-done.1, bf16[3,512,128]{2,1,0:T(8,128)(2,1)S(1)} %copy-done.2, bf16[3,512,128]{2,1,0:T(8,128)(2,1)S(1)} %copy-done.3, bf16[3,128,512]{2,1,0:T(8,128)(2,1)S(1)} %copy-done.4), custom_call_target="tpu_custom_call" | custom-call | flops 1207959552 | bytes 6291456 | tf_op jit(solution)/shard_map/expert_forward/pallas_call | solution.py:609
  64.5 1.7 copy-done
  66.1 79.4 %send_rows_1.1 = (bf16[3,1024,512]{2,1,0:T(8,128)(2,1)}, bf16[3,1024,512]{2,1,0:T(8,128)(2,1)}, bf16[96,512]{1,0:T(8,128)(2,1)}) custom-call(bf16[96,512]{1,0:T(8,128)(2,1)} %refs_2_.3, f32[2,4,4,4,4,8,128]{6,5,4,3,2,1,0:T(8,128)} %get-tuple-element.46.refs_1_, bf16[96,512]{1,0:T(8,128)(2,1)} %refs_0_.5, s32[96,8]{1,0:T(8,128)} %get-tuple-element.49.refs_3_.row_ref, ...), custom_call_target="tpu_custom_call" | custom-call | flops 30000001024 | bytes 12582912 | tf_op jit(solution)/shard_map/send_rows_1/pallas_call | solution.py:393
  145.6 41.5 %send_rows_2.1.u_ref.refs_6_ = bf16[3,1024,512]{2,1,0:T(8,128)(2,1)} custom-call(bf16[96,512]{1,0:T(8,128)(2,1)} %get-tuple-element.52.refs_0_.refs_2_, f32[2,4,4,4,4,8,128]{6,5,4,3,2,1,0:T(8,128)} %get-tuple-element.46.refs_1_), custom_call_target="tpu_custom_call" | custom-call | flops 30000001024 | bytes 12582912 | tf_op jit(solution)/shard_map/send_rows_2/pallas_call | solution.py:393
  187.2 1.9 copy-done.14
  189.1 1.9 copy-done.18
  190.9 10.1 %expert_backward.2 = (bf16[128,24,512]{2,1,0:T(8,128)(2,1)S(1)}, f32[128,1,128]{2,1,0:T(1,128)S(1)}, bf16[3,1024,128]{2,1,0:T(8,128)(2,1)S(1)}, bf16[3,1024,128]...) custom-call(bf16[3,1024,512]{2,1,0:T(8,128)(2,1)S(1)} %copy-done.14, bf16[3,1024,512]{2,1,0:T(8,128)(2,1)S(1)} %copy-done.18, ...), custom_call_target="tpu_custom_call" | custom-call | flops 3221225472 | bytes 12582912 | tf_op jit(solution)/shard_map/expert_backward/pallas_call | solution.py:609
  201.0 1.7 copy-done.19
  202.7 0.9 copy-done.20
  203.6 0.9 copy-done.21
  204.5 0.9 copy-done.22
  205.4 80.5 %send_rows_3.1 = (bf16[3,1024,512]{2,1,0:T(8,128)(2,1)}, bf16[96,512]{1,0:T(8,128)(2,1)}, bf16[128,24,512]{2,1,0:T(8,128)(2,1)}) custom-call(bf16[96,512]{1,0:T(8,128)(2,1)} %refs_0_.5, f32[2,4,4,4,4,8,128]{6,5,4,3,2,1,0:T(8,128)} %get-tuple-element.46.refs_1_, bf16[96,512]{1,0:T(8,128)(2,1)} %refs_2_.3, s32[96,8]{1,0:T(8,128)} %get-tuple-element.47.refs_3_.row_b_ref, ...), custom_call_target="tpu_custom_call" | custom-call | flops 30000001024 | bytes 12582912 | tf_op jit(solution)/shard_map/send_rows_3/pallas_call | solution.py:393
  285.9 80.1 %send_rows_4.1 = (bf16[3,1024,512]{2,1,0:T(8,128)(2,1)}, bf16[3,1024,512]{2,1,0:T(8,128)(2,1)}, bf16[96,512]{1,0:T(8,128)(2,1)}, f32[3,512,128]{2,1,0:T(8,128)},...) custom-call(bf16[96,512]{1,0:T(8,128)(2,1)} %get-tuple-element.56.refs_0_.x_ref, ...), custom_call_target="tpu_custom_call" | custom-call | flops 30000001024 | bytes 12582912 | tf_op jit(solution)/shard_map/send_rows_4/pallas_call | solution.py:393
  366.0 1.9 copy-done.12
  367.9 1.9 copy-done.15
  369.8 10.1 %expert_backward.3 = (bf16[128,24,512]{2,1,0:T(8,128)(2,1)S(1)}, f32[128,1,128]{2,1,0:T(1,128)S(1)}, bf16[3,1024,128]{2,1,0:T(8,128)(2,1)S(1)}, bf16[3,1024,128]...) custom-call(bf16[3,1024,512]{2,1,0:T(8,128)(2,1)S(1)} %copy-done.11, bf16[3,1024,512]{2,1,0:T(8,128)(2,1)S(1)} %copy-done.15, ...), custom_call_target="tpu_custom_call" | custom-call | flops 3221225472 | bytes 12582912 | tf_op jit(solution)/shard_map/expert_backward/pallas_call | solution.py:609
  379.9 1.6 copy-done.16
  381.5 1.9 copy-done.17
  383.4 51.1 %return_home.1 = (bf16[96,512]{1,0:T(8,128)(2,1)S(1)}, f32[96,8]{1,0:T(8,128)S(1)}, f32[96,8]{1,0:T(8,128)S(1)}, f32[3,512,128]{2,1,0:T(8,128)S(1)}, f32[3,512,1...) custom-call(bf16[96,512]{1,0:T(8,128)(2,1)S(1)} %copy-done.23, s32[96,8]{1,0:T(8,128)S(1)} %copy-done.8, ...), custom_call_target="tpu_custom_call" | custom-call | flops 30000001024 | bytes 6291456 | tf_op jit(solution)/shard_map/return_home/pallas_call | solution.py:485
  434.5 0.7 copy.22
  435.2 0.7 copy.23
  435.8 0.6 copy.32
  436.5 0.6 copy.33
  437.1 0.9 copy.34
  438.0 0.9 copy.35
  438.9 0.9 copy.36
  439.8 0.9 copy.37
  440.6 0.9 copy.38
  441.5 0.9 copy.39
  (44 shorter events, 0.1 us)
Async XLA Ops:
  4.9 51.5 %copy-start.2 = (bf16[3,512,128]{2,1,0:T(8,128)(2,1)S(1)}, bf16[3,512,128]{2,1,0:T(8,128)(2,1)}, u32[]{:S(2)}) copy-start(bf16[3,512,128]{2,1,0:T(8,128)(2,1)} %w1_ref.5) | copy-start | bytes 1179652
  4.9 51.5 %copy-start.3 = (bf16[3,512,128]{2,1,0:T(8,128)(2,1)S(1)}, bf16[3,512,128]{2,1,0:T(8,128)(2,1)}, u32[]{:S(2)}) copy-start(bf16[3,512,128]{2,1,0:T(8,128)(2,1)} %w3_ref.5) | copy-start | bytes 1179652
  4.9 51.5 %copy-start.4 = (bf16[3,128,512]{2,1,0:T(8,128)(2,1)S(1)}, bf16[3,128,512]{2,1,0:T(8,128)(2,1)}, u32[]{:S(2)}) copy-start(bf16[3,128,512]{2,1,0:T(8,128)(2,1)} %w2_ref.5) | copy-start | bytes 1179652
  56.4 1.9 copy-start.1
  64.4 1.7 copy-start
  145.5 41.6 %copy-start.5 = (bf16[3,512,128]{2,1,0:T(8,128)(2,1)S(1)}, bf16[3,512,128]{2,1,0:T(8,128)(2,1)}, u32[]{:S(2)}) copy-start(bf16[3,512,128]{2,1,0:T(8,128)(2,1)} %refs_7_.1) | copy-start | bytes 1179652
  145.5 41.6 %copy-start.6 = (bf16[3,512,128]{2,1,0:T(8,128)(2,1)S(1)}, bf16[3,512,128]{2,1,0:T(8,128)(2,1)}, u32[]{:S(2)}) copy-start(bf16[3,512,128]{2,1,0:T(8,128)(2,1)} %refs_8_.1) | copy-start | bytes 1179652
  145.5 41.6 %copy-start.7 = (bf16[3,128,512]{2,1,0:T(8,128)(2,1)S(1)}, bf16[3,128,512]{2,1,0:T(8,128)(2,1)}, u32[]{:S(2)}) copy-start(bf16[3,128,512]{2,1,0:T(8,128)(2,1)} %refs_9_.1) | copy-start | bytes 1179652
  145.6 41.6 %copy-start.13 = (bf16[3,1024,512]{2,1,0:T(8,128)(2,1)S(1)}, bf16[3,1024,512]{2,1,0:T(8,128)(2,1)}, u32[]{:S(2)}) copy-start(bf16[3,1024,512]{2,1,0:T(8,128)(2,1)} %get-tuple-element.54.q_ref.refs_7_) | copy-start | bytes 9437188
  187.2 1.9 copy-start.14
  189.1 1.9 copy-start.18
  201.0 1.7 copy-start.19
  202.7 0.9 copy-start.20
  203.6 0.9 copy-start.21
  204.5 0.9 copy-start.22
  285.8 80.1 %copy-start.11 = (bf16[3,1024,512]{2,1,0:T(8,128)(2,1)S(1)}, bf16[3,1024,512]{2,1,0:T(8,128)(2,1)}, u32[]{:S(2)}) copy-start(bf16[3,1024,512]{2,1,0:T(8,128)(2,1)} %get-tuple-element.62.u_ref) | copy-start | bytes 9437188
  366.0 1.9 copy-start.12
  367.9 1.9 copy-start.15
  369.8 11.7 %copy-start.8 = (s32[96,8]{1,0:T(8,128)S(1)}, s32[96,8]{1,0:T(8,128)}, u32[]{:S(2)}) copy-start(s32[96,8]{1,0:T(8,128)} %get-tuple-element.49.refs_3_.row_ref) | copy-start | bytes 9220
  369.8 11.7 %copy-start.9 = (s32[96,8]{1,0:T(8,128)S(1)}, s32[96,8]{1,0:T(8,128)}, u32[]{:S(2)}) copy-start(s32[96,8]{1,0:T(8,128)} %get-tuple-element.47.refs_3_.row_b_ref) | copy-start | bytes 9220
  369.8 11.7 %copy-start.10 = (f32[96,8]{1,0:T(8,128)S(1)}, f32[96,8]{1,0:T(8,128)}, u32[]{:S(2)}) copy-start(f32[96,8]{1,0:T(8,128)} %get-tuple-element.50.refs_4_.gate_ref) | copy-start | bytes 9220
  369.8 11.7 %copy-start.23 = (bf16[96,512]{1,0:T(8,128)(2,1)S(1)}, bf16[96,512]{1,0:T(8,128)(2,1)}, u32[]{:S(2)}) copy-start(bf16[96,512]{1,0:T(8,128)(2,1)} %get-tuple-element.56.refs_0_.x_ref) | copy-start | bytes 294916
  379.9 1.6 copy-start.16
  381.5 1.9 copy-start.17
  383.4 52.4 %copy-start.27 = (bf16[96,512]{1,0:T(8,128)(2,1)S(1)}, bf16[96,512]{1,0:T(8,128)(2,1)}, u32[]{:S(2)}) copy-start(bf16[96,512]{1,0:T(8,128)(2,1)} %get-tuple-element.100) | copy-start | bytes 294916
  434.5 5.3 %copy-start.26 = (f32[3,512,128]{2,1,0:T(8,128)S(1)}, f32[3,512,128]{2,1,0:T(8,128)}, u32[]{:S(2)}) copy-start(f32[3,512,128]{2,1,0:T(8,128)} %get-tuple-element.105) | copy-start | bytes 2359300
  437.1 3.5 copy-start.25
  438.0 3.5 copy-start.24

commit v9 on v8

--- a/solution.py
+++ b/solution.py
@@ -401,7 +401,7 @@
             pltpu.SemaphoreType.DMA((count,)),
             pltpu.SemaphoreType.DMA((count,)),
         ] + ([pltpu.VMEM(table_shape.shape, F32)] if first else []) + (return_scratch(home[3]) if home else []),
-        compiler_params=pltpu.CompilerParams(collective_id=call_id, has_side_effects=True, vmem_limit_bytes=54 * 1024 * 1024),
+        compiler_params=pltpu.CompilerParams(collective_id=call_id, has_side_effects=True, vmem_limit_bytes=(34 if home else 24) * 1024 * 1024),
         cost_estimate=pl.CostEstimate(flops=3 * 10**10, bytes_accessed=devices * tok_dev * width * 2, transcendentals=0),
         name=f"send_rows_{call_id}",
     )(x, table, *(home or ()), *job_in)
@@ -447,7 +447,7 @@
     return out[:, :top_k]
 
 
-def return_kernel(per_device, x_ref, row_ref, gate_ref, rows_ref, line_a_ref, line_b_ref, row_b_ref, u_ref, q_ref, hidden_ref, da_ref, db_ref, out_ref, dgate_a_ref, dgate_b_ref, dw1_ref, dw3_ref, dw2_ref, back, relay, sems, relay_sems, line_ref, line_back):
+def return_kernel(per_device, x_ref, row_ref, gate_ref, rows_ref, line_a_ref, line_b_ref, row_b_ref, out_ref, dgate_a_ref, dgate_b_ref, back, relay, sems, relay_sems, line_ref, line_back):
     me, core, at = my_place()
     devices = rows_ref.shape[0]
     line_ref[...] = line_a_ref[...] + line_b_ref[...]
@@ -459,14 +459,11 @@
         pltpu.make_async_remote_copy(src_ref=line_ref.at[to], dst_ref=line_back.at[me], send_sem=sems.at[3], recv_sem=sems.at[4], device_id={"ep": to}, device_id_type=pl.DeviceIdType.MESH).start()
         return carry
 
-    jobs = grad_jobs([u_ref, q_ref, hidden_ref, da_ref, db_ref], [dw1_ref, dw3_ref, dw2_ref])
     for step in vias + directs[:2] + forwards[:2] + directs[2:] + forwards[2:4]:
         step()
     lax.fori_loop(1, devices, send_line, 0)
-    for n, step in enumerate(forwards[4:]):
+    for step in forwards[4:]:
         step()
-        if jobs:
-            jobs.pop(0)()
     line_back[me] = line_ref[me]
     others = pl.ds(0, devices - 1)
     for k in (3, 4):
@@ -478,20 +475,20 @@
     out_ref[...] = (x_ref[...].astype(F32) + pair_sum(False, row_ref, gate_ref, home_blocks(back))).astype(out_ref.dtype)
 
 
-def return_home(x, rows, gates, sent, line_a, line_b, rows_b, saved, grad_shapes, per_device, call_id):
+def return_home(x, rows, gates, sent, line_a, line_b, rows_b, per_device, call_id):
     vmem = pl.BlockSpec(memory_space=pltpu.VMEM)
     dgate = jax.ShapeDtypeStruct(rows.shape, F32)
-    outs = (jax.ShapeDtypeStruct(x.shape, x.dtype), dgate, dgate) + tuple(grad_shapes)
+    outs = (jax.ShapeDtypeStruct(x.shape, x.dtype), dgate, dgate)
     return pl.pallas_call(
         functools.partial(return_kernel, per_device),
         out_shape=outs,
-        in_specs=[vmem] * (7 + len(saved)),
+        in_specs=[vmem] * 7,
         out_specs=(vmem,) * len(outs),
         scratch_shapes=return_scratch(sent) + [pltpu.VMEM(line_a.shape, F32)] * 2,
-        compiler_params=pltpu.CompilerParams(collective_id=call_id, has_side_effects=True, vmem_limit_bytes=40 * 1024 * 1024),
+        compiler_params=pltpu.CompilerParams(collective_id=call_id, has_side_effects=True, vmem_limit_bytes=20 * 1024 * 1024),
         cost_estimate=pl.CostEstimate(flops=3 * 10**10, bytes_accessed=sent.size * 4, transcendentals=0),
         name="return_home",
-    )(x, rows, gates, sent, line_a, line_b, rows_b, *saved)
+    )(x, rows, gates, sent, line_a, line_b, rows_b)
 
 
 def forward_rows(u, w_both, w_down):
@@ -546,23 +543,7 @@
     return [functools.partial(job, e) for e in range(own)]
 
 
-def grad_jobs(ins, outs):
-    u_ref, q_ref, hidden_ref, da_ref, db_ref = ins
-    dw1_ref, dw3_ref, dw2_ref = outs
-    ff = da_ref.shape[2]
-    rows = (((0,), (0,)), ((), ()))
-
-    def job(e):
-        both = jnp.concatenate([da_ref[e], db_ref[e]], axis=1)
-        dw = lax.dot_general(u_ref[e], both, rows, preferred_element_type=F32)
-        dw1_ref[e] = dw[:, :ff]
-        dw3_ref[e] = dw[:, ff:]
-        dw2_ref[e] = lax.dot_general(hidden_ref[e], q_ref[e], rows, preferred_element_type=F32)
-
-    return [functools.partial(job, e) for e in range(u_ref.shape[0])]
-
-
-def backward_kernel(first_lane, chunk, u_ref, dy_ref, q_ref, w1_ref, w3_ref, w2_ref, du_ref, dgate_ref, hidden_ref, da_ref, db_ref):
+def backward_kernel(first_lane, chunk, u_ref, dy_ref, q_ref, w1_ref, w3_ref, w2_ref, du_ref, dgate_ref, dw1_ref, dw3_ref, dw2_ref, hidden_ref, both_ref):
     ff = w2_ref.shape[1]
     w_both = jnp.concatenate([w1_ref[0], w3_ref[0]], axis=1)
     last = (((1,), (1,)), ((), ()))
@@ -581,14 +562,18 @@
         d_hidden = lax.dot_general(q_ref[0, rows, :], w2_ref[0], last, preferred_element_type=F32)
         da = (d_hidden * pre_up * sig * (1.0 + pre_gate * (1.0 - sig))).astype(BF16)
         db = (d_hidden * silu).astype(BF16)
-        hidden_ref[0, rows, :] = hidden
-        da_ref[0, rows, :] = da
-        db_ref[0, rows, :] = db
         both = jnp.concatenate([da, db], axis=1)
+        hidden_ref[rows, :] = hidden
+        both_ref[rows, :] = both
         store_home(du_ref, step, lax.dot_general(both, w_both, last, preferred_element_type=F32))
         return carry
 
     lax.fori_loop(0, u_ref.shape[1] // chunk, body, 0)
+    over_rows = (((0,), (0,)), ((), ()))
+    dw = lax.dot_general(u_ref[0], both_ref[...], over_rows, preferred_element_type=F32)
+    dw1_ref[0] = dw[:, :ff]
+    dw3_ref[0] = dw[:, ff:]
+    dw2_ref[0] = lax.dot_general(hidden_ref[...], q_ref[0], over_rows, preferred_element_type=F32)
 
 
 def expert_call(kernel, inputs, outs, weights, n_group, name):
@@ -603,16 +588,19 @@
     kinds = {
         "home": home,
         "gate": (jax.ShapeDtypeStruct((n_group, 1, 128), F32), pl.BlockSpec((n_group, 1, 128), lambda e: (0, 0, 0))),
-        "ff": (jax.ShapeDtypeStruct((own, count, ff), BF16), each((count, ff))),
+        "up": (jax.ShapeDtypeStruct((own, width, ff), F32), each((width, ff))),
+        "down": (jax.ShapeDtypeStruct((own, ff, width), F32), each((ff, width))),
     }
-    steps = 3 if len(outs) == 1 else 8
+    steps = 3 if len(outs) == 1 else 11
+    scratch = [] if len(outs) == 1 else [pltpu.VMEM((count, ff), BF16), pltpu.VMEM((count, 2 * ff), BF16)]
     return pl.pallas_call(
         functools.partial(kernel, 256),
         out_shape=tuple(kinds[k][0] for k in outs),
         grid=(own,),
         in_specs=[each((count, width))] * len(inputs) + [each((width, ff)), each((width, ff)), each((ff, width))],
         out_specs=tuple(kinds[k][1] for k in outs),
-        compiler_params=pltpu.CompilerParams(vmem_limit_bytes=32 * 1024 * 1024),
+        scratch_shapes=scratch,
+        compiler_params=pltpu.CompilerParams(vmem_limit_bytes=24 * 1024 * 1024),
         cost_estimate=pl.CostEstimate(flops=2 * steps * own * count * width * ff, bytes_accessed=own * count * width * 2 * (len(inputs) + 1), transcendentals=own * count * ff),
         name=name,
     )(*inputs, *weights)
@@ -623,10 +611,10 @@
 
 
 def expert_backward(u_rows, dy_rows, q_rows, weights, n_group, first_lane):
-    outs = ("home", "gate", "ff", "ff", "ff")
+    outs = ("home", "gate", "up", "up", "down")
     kernel = functools.partial(backward_kernel, first_lane)
-    du, lines, *saved = expert_call(kernel, (u_rows, dy_rows, q_rows), outs, weights, n_group, "expert_backward")
-    return du, lines, (u_rows, q_rows, *saved)
+    du, lines, *grads = expert_call(kernel, (u_rows, dy_rows, q_rows), outs, weights, n_group, "expert_backward")
+    return du, lines, grads
 
 
 def solution(mesh):
@@ -649,13 +637,12 @@
         out_a = expert_forward(u_a, weights_a, n_group)
         dy_b, q_b, x_mid = send_rows(dy_out, table, 1, own, capacity, 1, scaled=True, home=(x_in, rows_a, gates_a, out_a), gated=True)
         u_b, = send_rows(x_mid, table, 1, own, capacity, 2)
-        du_b, line_b, saved_b = expert_backward(u_b, dy_b, q_b, weights_b, n_group, block)
+        du_b, line_b, grads_b = expert_backward(u_b, dy_b, q_b, weights_b, n_group, block)
         forward_b = (forward_jobs, (u_b,) + weights_b, (jax.ShapeDtypeStruct((n_group, block, width), BF16),))
         u_again, dx_mid, out_b = send_rows(x_in, table, 0, own, capacity, 3, home=(dy_out, rows_b, gates_b, du_b), work=forward_b)
-        grad_shapes = tuple(jax.ShapeDtypeStruct(w.shape, F32) for w in weights_b)
-        dy_a, q_a, x_out, *grads_b = send_rows(dx_mid, table, 0, own, capacity, 4, scaled=True, home=(x_mid, rows_b, gates_b, out_b), gated=True, work=(grad_jobs, saved_b, grad_shapes))
-        du_a, line_a, saved_a = expert_backward(u_again, dy_a, q_a, weights_a, n_group, 0)
-        dx_in, dgate_a, dgate_b, *grads_a = return_home(dx_mid, rows_a, gates_a, du_a, line_a, line_b, rows_b, saved_a, grad_shapes, block, 5)
+        dy_a, q_a, x_out = send_rows(dx_mid, table, 0, own, capacity, 4, scaled=True, home=(x_mid, rows_b, gates_b, out_b), gated=True)
+        du_a, line_a, grads_a = expert_backward(u_again, dy_a, q_a, weights_a, n_group, 0)
+        dx_in, dgate_a, dgate_b = return_home(dx_mid, rows_a, gates_a, du_a, line_a, line_b, rows_b, block, 5)
         return (x_out, dx_in) + tuple(grads_a) + tuple(grads_b) + (dgate_a, dgate_b)
 
     return jax.shard_map(device_program, mesh=mesh, in_specs=(tok_spec,) * 6 + (w_spec,) * 6, out_specs=(tok_spec,) * 10, check_vma=False)

time: 443 us -> 396 us (0.89)
  Pallas kernels: 415 us -> 390 us
  local copies, waits for them, and re-layouts: 26.9 us -> 4.28 us
    pallas_call x5, Pallas kernels: 333 us -> 305 us  [send_rows(): pl.pallas_call(functools.partial(send_kernel, own, capacity, layer, first...]
    unnamed x66 -> x32, local copies, waits for them, and re-layouts: 26.9 us -> 4.28 us
    pallas_call x3, Pallas kernels: 26.3 us -> 31.4 us  [expert_call(): pl.pallas_call(functools.partial(kernel, 256), out_shape=tuple((kinds[k][...]
where the time goes in v9:
time: 396 us
  Pallas kernels  390 us (98%)
  local copies, waits for them, and re-layouts  4.28 us (1%)
    pallas_call x5, Pallas kernels, send_rows(): pl.pallas_call(functools.partial(send_kernel, own, capacity, layer, first...  305 us
    pallas_call x1, Pallas kernels, return_home(): pl.pallas_call(functools.partial(return_kernel, per_device), out_shape=ou...  49.2 us
    pallas_call x3, Pallas kernels, expert_call(): pl.pallas_call(functools.partial(kernel, 256), out_shape=tuple((kinds[k][...  31.4 us

profile of v9, /device:TPU:1, one launch (start us, length us, event | category | flops | bytes accessed | tf_op | source)
XLA Modules:
  0.0 395.5 jit_solution(9393717404843029191)
XLA Ops:
  0.6 4.3 %make_tables.1 = (f32[4,8,128]{2,1,0:T(8,128)}, s32[96,8]{1,0:T(8,128)}, s32[96,8]{1,0:T(8,128)}, f32[96,8]{1,0:T(8,128)}, f32[96,8]{1,0:T(8,128)}) custom-call(s32[8,96]{1,0:T(8,128)} %bitcast.4, s32[8,96]{1,0:T(8,128)} %bitcast.5, f32[8,96]{1,0:T(8,128)} %bitcast.6, f32[8,96]{1,0:T(8,128)} %bitcast.7), custom_call_target="tpu_custom_call" | custom-call | tf_op jit(solution)/shard_map/make_tables/pallas_call | solution.py:52
  4.9 0.9 copy-done.6
  5.8 0.7 copy-done.13
  6.5 48.5 %send_rows_0.1 = (bf16[3,1024,512]{2,1,0:T(8,128)(2,1)S(1)}, f32[2,4,4,4,4,8,128]{6,5,4,3,2,1,0:T(8,128)S(1)}) custom-call(bf16[96,512]{1,0:T(8,128)(2,1)S(1)} %copy-done.6, f32[4,8,128]{2,1,0:T(8,128)S(1)} %copy-done.13), custom_call_target="tpu_custom_call" | custom-call | flops 30000001024 | bytes 12582912 | tf_op jit(solution)/shard_map/send_rows_0/pallas_call | solution.py:393
  55.0 0.0 copy-done
  55.0 0.0 copy-done.1
  55.0 0.0 copy-done.2
  55.0 0.0 copy-start.7
  55.0 0.0 copy-start.8
  55.0 0.0 copy-start.9
  55.1 0.0 copy-start.11
  55.1 6.2 %expert_forward.1.refs_5_ = bf16[128,24,512]{2,1,0:T(8,128)(2,1)S(1)} custom-call(bf16[3,1024,512]{2,1,0:T(8,128)(2,1)S(1)} %get-tuple-element.45.u_ref, bf16[3,512,128]{2,1,0:T(8,128)(2,1)S(1)} %copy-done, bf16[3,512,128]{2,1,0:T(8,128)(2,1)S(1)} %copy-done.1, bf16[3,128,512]{2,1,0:T(8,128)(2,1)S(1)} %copy-done.2), custom_call_target="tpu_custom_call" | custom-call | flops 1207959552 | bytes 6291456 | tf_op jit(solution)/shard_map/expert_forward/pallas_call | solution.py:596
  61.2 0.0 copy-done.7
  61.3 0.0 copy-done.8
  61.3 0.0 copy-done.9
  61.3 74.5 %send_rows_1.1 = (bf16[3,1024,512]{2,1,0:T(8,128)(2,1)S(1)}, bf16[3,1024,512]{2,1,0:T(8,128)(2,1)S(1)}, bf16[96,512]{1,0:T(8,128)(2,1)S(1)}) custom-call(bf16[96,512]{1,0:T(8,128)(2,1)S(1)} %copy-done.8, f32[2,4,4,4,4,8,128]{6,5,4,3,2,1,0:T(8,128)S(1)} %get-tuple-element.40.refs_1_, bf16[96,512]{1,0:T(8,128)(2,1)S(1)} %copy-done.7, s32[96,8]{1,0:T(8,128)S(1)} %copy-done.9, ...), custom_call_target="tpu_custom_call" | custom-call | flops 30000001024 | bytes 12582912 | tf_op jit(solution)/shard_map/send_rows_1/pallas_call | solution.py:393
  135.8 0.0 copy-start.3
  135.8 0.0 copy-start.4
  135.8 0.0 copy-start.5
  135.8 37.4 %send_rows_2.1.u_ref.refs_6_ = bf16[3,1024,512]{2,1,0:T(8,128)(2,1)S(1)} custom-call(bf16[96,512]{1,0:T(8,128)(2,1)S(1)} %get-tuple-element.46.refs_0_.refs_2_, f32[2,4,4,4,4,8,128]{6,5,4,3,2,1,0:T(8,128)S(1)} %get-tuple-element.40.refs_1_), custom_call_target="tpu_custom_call" | custom-call | flops 30000001024 | bytes 12582912 | tf_op jit(solution)/shard_map/send_rows_2/pallas_call | solution.py:393
  173.3 0.0 copy-start.10
  173.3 0.0 copy-start.12
  173.3 12.6 %expert_backward.2 = (bf16[128,24,512]{2,1,0:T(8,128)(2,1)S(1)}, f32[128,1,128]{2,1,0:T(1,128)S(1)}, f32[3,512,128]{2,1,0:T(8,128)}, f32[3,512,128]{2,1,0:T(8,128)}, f32[3,128,512]{2,1,0:T(8,128)}) custom-call(bf16[3,1024,512]{2,1,0:T(8,128)(2,1)S(1)} %send_rows_2.1.u_ref.refs_6_, bf16[3,1024,512]{2,1,0:T(8,128)(2,1)S(1)} %get-tuple-element.47.dy_ref, ...), custom_call_target="tpu_custom_call" | custom-call | flops 4429185024 | bytes 12582912 | tf_op jit(solution)/shard_map/expert_backward/pallas_call | solution.py:596
  185.9 0.0 copy-done.12
  185.9 71.2 %send_rows_3.1 = (bf16[3,1024,512]{2,1,0:T(8,128)(2,1)S(1)}, bf16[96,512]{1,0:T(8,128)(2,1)S(1)}, bf16[128,24,512]{2,1,0:T(8,128)(2,1)S(1)}) custom-call(bf16[96,512]{1,0:T(8,128)(2,1)S(1)} %copy-done.7, f32[2,4,4,4,4,8,128]{6,5,4,3,2,1,0:T(8,128)S(1)} %get-tuple-element.40.refs_1_, bf16[96,512]{1,0:T(8,128)(2,1)S(1)} %copy-done.8, s32[96,8]{1,0:T(8,128)S(1)} %copy-done.10, ...), custom_call_target="tpu_custom_call" | custom-call | flops 30000001024 | bytes 12582912 | tf_op jit(solution)/shard_map/send_rows_3/pallas_call | solution.py:393
  257.1 73.9 %send_rows_4.1 = (bf16[3,1024,512]{2,1,0:T(8,128)(2,1)S(1)}, bf16[3,1024,512]{2,1,0:T(8,128)(2,1)S(1)}, bf16[96,512]{1,0:T(8,128)(2,1)S(1)}) custom-call(bf16[96,512]{1,0:T(8,128)(2,1)S(1)} %get-tuple-element.50.refs_0_.x_ref, f32[2,4,4,4,4,8,128]{6,5,4,3,2,1,0:T(8,128)S(1)} %get-tuple-element.40.refs_1_, ...), custom_call_target="tpu_custom_call" | custom-call | flops 30000001024 | bytes 12582912 | tf_op jit(solution)/shard_map/send_rows_4/pallas_call | solution.py:393
  331.1 12.6 %expert_backward.3 = (bf16[128,24,512]{2,1,0:T(8,128)(2,1)S(1)}, f32[128,1,128]{2,1,0:T(1,128)S(1)}, f32[3,512,128]{2,1,0:T(8,128)}, f32[3,512,128]{2,1,0:T(8,128)}, f32[3,128,512]{2,1,0:T(8,128)}) custom-call(bf16[3,1024,512]{2,1,0:T(8,128)(2,1)S(1)} %get-tuple-element.53.u_ref, bf16[3,1024,512]{2,1,0:T(8,128)(2,1)S(1)} %get-tuple-element.54.dy_ref, ...), custom_call_target="tpu_custom_call" | custom-call | flops 4429185024 | bytes 12582912 | tf_op jit(solution)/shard_map/expert_backward/pallas_call | solution.py:596
  343.7 49.2 %return_home.1 = (bf16[96,512]{1,0:T(8,128)(2,1)S(1)}, f32[96,8]{1,0:T(8,128)S(1)}, f32[96,8]{1,0:T(8,128)S(1)}) custom-call(bf16[96,512]{1,0:T(8,128)(2,1)S(1)} %get-tuple-element.50.refs_0_.x_ref, s32[96,8]{1,0:T(8,128)S(1)} %copy-done.9, f32[96,8]{1,0:T(8,128)S(1)} %copy-done.11, bf16[128,24,512]{2,1,0:T(8,128)(2,1)S(1)} %get-tuple-element.56.rows_ref, ...), custom_call_target="tpu_custom_call" | custom-call | flops 30000001024 | bytes 6291456 | tf_op jit(solution)/shard_map/return_home/pallas_call | solution.py:482
  392.9 0.7 copy.22
  393.6 0.7 copy.23
  394.2 0.6 copy.26
  394.9 0.6 copy.27
  (10 shorter events, 0.0 us)
Async XLA Ops:
  4.9 0.9 copy-start.6
  5.8 0.7 copy-start.13
  6.5 48.5 %copy-start = (bf16[3,512,128]{2,1,0:T(8,128)(2,1)S(1)}, bf16[3,512,128]{2,1,0:T(8,128)(2,1)}, u32[]{:S(2)}) copy-start(bf16[3,512,128]{2,1,0:T(8,128)(2,1)} %w1_ref.5) | copy-start | bytes 1179652
  6.5 48.5 %copy-start.1 = (bf16[3,512,128]{2,1,0:T(8,128)(2,1)S(1)}, bf16[3,512,128]{2,1,0:T(8,128)(2,1)}, u32[]{:S(2)}) copy-start(bf16[3,512,128]{2,1,0:T(8,128)(2,1)} %w3_ref.5) | copy-start | bytes 1179652
  6.5 48.5 %copy-start.2 = (bf16[3,128,512]{2,1,0:T(8,128)(2,1)S(1)}, bf16[3,128,512]{2,1,0:T(8,128)(2,1)}, u32[]{:S(2)}) copy-start(bf16[3,128,512]{2,1,0:T(8,128)(2,1)} %w2_ref.5) | copy-start | bytes 1179652
  55.0 6.2 %copy-start.7 = (bf16[96,512]{1,0:T(8,128)(2,1)S(1)}, bf16[96,512]{1,0:T(8,128)(2,1)}, u32[]{:S(2)}) copy-start(bf16[96,512]{1,0:T(8,128)(2,1)} %refs_0_.5) | copy-start | bytes 294916
  55.0 6.2 %copy-start.8 = (bf16[96,512]{1,0:T(8,128)(2,1)S(1)}, bf16[96,512]{1,0:T(8,128)(2,1)}, u32[]{:S(2)}) copy-start(bf16[96,512]{1,0:T(8,128)(2,1)} %refs_2_.3) | copy-start | bytes 294916
  55.0 6.2 %copy-start.9 = (s32[96,8]{1,0:T(8,128)S(1)}, s32[96,8]{1,0:T(8,128)}, u32[]{:S(2)}) copy-start(s32[96,8]{1,0:T(8,128)} %get-tuple-element.43.refs_3_.row_ref) | copy-start | bytes 9220
  55.1 6.2 %copy-start.11 = (f32[96,8]{1,0:T(8,128)S(1)}, f32[96,8]{1,0:T(8,128)}, u32[]{:S(2)}) copy-start(f32[96,8]{1,0:T(8,128)} %get-tuple-element.44.refs_4_.gate_ref) | copy-start | bytes 9220
  135.8 37.5 %copy-start.3 = (bf16[3,512,128]{2,1,0:T(8,128)(2,1)S(1)}, bf16[3,512,128]{2,1,0:T(8,128)(2,1)}, u32[]{:S(2)}) copy-start(bf16[3,512,128]{2,1,0:T(8,128)(2,1)} %refs_7_.1) | copy-start | bytes 1179652
  135.8 37.5 %copy-start.4 = (bf16[3,512,128]{2,1,0:T(8,128)(2,1)S(1)}, bf16[3,512,128]{2,1,0:T(8,128)(2,1)}, u32[]{:S(2)}) copy-start(bf16[3,512,128]{2,1,0:T(8,128)(2,1)} %refs_8_.1) | copy-start | bytes 1179652
  135.8 37.5 %copy-start.5 = (bf16[3,128,512]{2,1,0:T(8,128)(2,1)S(1)}, bf16[3,128,512]{2,1,0:T(8,128)(2,1)}, u32[]{:S(2)}) copy-start(bf16[3,128,512]{2,1,0:T(8,128)(2,1)} %refs_9_.1) | copy-start | bytes 1179652
  173.3 12.7 %copy-start.10 = (s32[96,8]{1,0:T(8,128)S(1)}, s32[96,8]{1,0:T(8,128)}, u32[]{:S(2)}) copy-start(s32[96,8]{1,0:T(8,128)} %get-tuple-element.41.refs_3_.row_b_ref) | copy-start | bytes 9220
  173.3 12.7 %copy-start.12 = (f32[96,8]{1,0:T(8,128)S(1)}, f32[96,8]{1,0:T(8,128)}, u32[]{:S(2)}) copy-start(f32[96,8]{1,0:T(8,128)} %get-tuple-element.42.refs_4_) | copy-start | bytes 9220

commit v10 on v9

--- a/solution.py
+++ b/solution.py
@@ -524,7 +524,7 @@
 def forward_jobs(ins, outs):
     u_ref, w1_ref, w3_ref, w2_ref = ins
     out_ref, = outs
-    chunk = 256
+    chunk = 512
     own, count, width = u_ref.shape
     sources = out_ref.shape[0] * chunk // count
     slots = out_ref.shape[1] // own
@@ -594,7 +594,7 @@
     steps = 3 if len(outs) == 1 else 11
     scratch = [] if len(outs) == 1 else [pltpu.VMEM((count, ff), BF16), pltpu.VMEM((count, 2 * ff), BF16)]
     return pl.pallas_call(
-        functools.partial(kernel, 256),
+        functools.partial(kernel, 512),
         out_shape=tuple(kinds[k][0] for k in outs),
         grid=(own,),
         in_specs=[each((count, width))] * len(inputs) + [each((width, ff)), each((width, ff)), each((ff, width))],

time: 396 us -> 389 us (0.982)
  Pallas kernels: 390 us -> 384 us
    pallas_call x3, Pallas kernels: 31.4 us -> 24.9 us  [expert_call(): pl.pallas_call(functools.partial(kernel, 512), out_shape=tuple((kinds[k][...]
where the time goes in v10:
time: 389 us
  Pallas kernels  384 us (99%)
  local copies, waits for them, and re-layouts  4.28 us (1%)
    pallas_call x5, Pallas kernels, send_rows(): pl.pallas_call(functools.partial(send_kernel, own, capacity, layer, first...  305 us
    pallas_call x1, Pallas kernels, return_home(): pl.pallas_call(functools.partial(return_kernel, per_device), out_shape=ou...  49.9 us
    pallas_call x3, Pallas kernels, expert_call(): pl.pallas_call(functools.partial(kernel, 512), out_shape=tuple((kinds[k][...  24.9 us

profile of v10, /device:TPU:1, one launch (start us, length us, event | category | flops | bytes accessed | tf_op | source)
XLA Modules:
  0.0 388.8 jit_solution(16534392904226305942)
XLA Ops:
  0.6 4.3 %make_tables.1 = (f32[4,8,128]{2,1,0:T(8,128)}, s32[96,8]{1,0:T(8,128)}, s32[96,8]{1,0:T(8,128)}, f32[96,8]{1,0:T(8,128)}, f32[96,8]{1,0:T(8,128)}) custom-call(s32[8,96]{1,0:T(8,128)} %bitcast.4, s32[8,96]{1,0:T(8,128)} %bitcast.5, f32[8,96]{1,0:T(8,128)} %bitcast.6, f32[8,96]{1,0:T(8,128)} %bitcast.7), custom_call_target="tpu_custom_call" | custom-call | tf_op jit(solution)/shard_map/make_tables/pallas_call | solution.py:52
  4.9 0.9 copy-done.6
  5.8 0.7 copy-done.13
  6.5 48.5 %send_rows_0.1 = (bf16[3,1024,512]{2,1,0:T(8,128)(2,1)S(1)}, f32[2,4,4,4,4,8,128]{6,5,4,3,2,1,0:T(8,128)S(1)}) custom-call(bf16[96,512]{1,0:T(8,128)(2,1)S(1)} %copy-done.6, f32[4,8,128]{2,1,0:T(8,128)S(1)} %copy-done.13), custom_call_target="tpu_custom_call" | custom-call | flops 30000001024 | bytes 12582912 | tf_op jit(solution)/shard_map/send_rows_0/pallas_call | solution.py:393
  55.0 0.0 copy-done
  55.0 0.0 copy-done.1
  55.0 0.0 copy-done.2
  55.0 0.0 copy-start.7
  55.0 0.0 copy-start.8
  55.0 0.0 copy-start.9
  55.1 0.0 copy-start.11
  55.1 4.4 %expert_forward.1.refs_5_ = bf16[128,24,512]{2,1,0:T(8,128)(2,1)S(1)} custom-call(bf16[3,1024,512]{2,1,0:T(8,128)(2,1)S(1)} %get-tuple-element.45.u_ref, bf16[3,512,128]{2,1,0:T(8,128)(2,1)S(1)} %copy-done, bf16[3,512,128]{2,1,0:T(8,128)(2,1)S(1)} %copy-done.1, bf16[3,128,512]{2,1,0:T(8,128)(2,1)S(1)} %copy-done.2), custom_call_target="tpu_custom_call" | custom-call | flops 1207959552 | bytes 6291456 | tf_op jit(solution)/shard_map/expert_forward/pallas_call | solution.py:596
  59.5 0.0 copy-done.7
  59.5 0.0 copy-done.8
  59.5 0.0 copy-done.9
  59.6 74.5 %send_rows_1.1 = (bf16[3,1024,512]{2,1,0:T(8,128)(2,1)S(1)}, bf16[3,1024,512]{2,1,0:T(8,128)(2,1)S(1)}, bf16[96,512]{1,0:T(8,128)(2,1)S(1)}) custom-call(bf16[96,512]{1,0:T(8,128)(2,1)S(1)} %copy-done.8, f32[2,4,4,4,4,8,128]{6,5,4,3,2,1,0:T(8,128)S(1)} %get-tuple-element.40.refs_1_, bf16[96,512]{1,0:T(8,128)(2,1)S(1)} %copy-done.7, s32[96,8]{1,0:T(8,128)S(1)} %copy-done.9, ...), custom_call_target="tpu_custom_call" | custom-call | flops 30000001024 | bytes 12582912 | tf_op jit(solution)/shard_map/send_rows_1/pallas_call | solution.py:393
  134.0 0.0 copy-start.3
  134.0 0.0 copy-start.4
  134.0 0.0 copy-start.5
  134.1 37.4 %send_rows_2.1.u_ref.refs_6_ = bf16[3,1024,512]{2,1,0:T(8,128)(2,1)S(1)} custom-call(bf16[96,512]{1,0:T(8,128)(2,1)S(1)} %get-tuple-element.46.refs_0_.refs_2_, f32[2,4,4,4,4,8,128]{6,5,4,3,2,1,0:T(8,128)S(1)} %get-tuple-element.40.refs_1_), custom_call_target="tpu_custom_call" | custom-call | flops 30000001024 | bytes 12582912 | tf_op jit(solution)/shard_map/send_rows_2/pallas_call | solution.py:393
  171.5 0.0 copy-start.10
  171.5 0.0 copy-start.12
  171.5 10.2 %expert_backward.2 = (bf16[128,24,512]{2,1,0:T(8,128)(2,1)S(1)}, f32[128,1,128]{2,1,0:T(1,128)S(1)}, f32[3,512,128]{2,1,0:T(8,128)}, f32[3,512,128]{2,1,0:T(8,128)}, f32[3,128,512]{2,1,0:T(8,128)}) custom-call(bf16[3,1024,512]{2,1,0:T(8,128)(2,1)S(1)} %send_rows_2.1.u_ref.refs_6_, bf16[3,1024,512]{2,1,0:T(8,128)(2,1)S(1)} %get-tuple-element.47.dy_ref, ...), custom_call_target="tpu_custom_call" | custom-call | flops 4429185024 | bytes 12582912 | tf_op jit(solution)/shard_map/expert_backward/pallas_call | solution.py:596
  181.7 0.0 copy-done.12
  181.7 72.4 %send_rows_3.1 = (bf16[3,1024,512]{2,1,0:T(8,128)(2,1)S(1)}, bf16[96,512]{1,0:T(8,128)(2,1)S(1)}, bf16[128,24,512]{2,1,0:T(8,128)(2,1)S(1)}) custom-call(bf16[96,512]{1,0:T(8,128)(2,1)S(1)} %copy-done.7, f32[2,4,4,4,4,8,128]{6,5,4,3,2,1,0:T(8,128)S(1)} %get-tuple-element.40.refs_1_, bf16[96,512]{1,0:T(8,128)(2,1)S(1)} %copy-done.8, s32[96,8]{1,0:T(8,128)S(1)} %copy-done.10, ...), custom_call_target="tpu_custom_call" | custom-call | flops 30000001024 | bytes 12582912 | tf_op jit(solution)/shard_map/send_rows_3/pallas_call | solution.py:393
  254.1 72.0 %send_rows_4.1 = (bf16[3,1024,512]{2,1,0:T(8,128)(2,1)S(1)}, bf16[3,1024,512]{2,1,0:T(8,128)(2,1)S(1)}, bf16[96,512]{1,0:T(8,128)(2,1)S(1)}) custom-call(bf16[96,512]{1,0:T(8,128)(2,1)S(1)} %get-tuple-element.50.refs_0_.x_ref, f32[2,4,4,4,4,8,128]{6,5,4,3,2,1,0:T(8,128)S(1)} %get-tuple-element.40.refs_1_, ...), custom_call_target="tpu_custom_call" | custom-call | flops 30000001024 | bytes 12582912 | tf_op jit(solution)/shard_map/send_rows_4/pallas_call | solution.py:393
  326.1 10.2 %expert_backward.3 = (bf16[128,24,512]{2,1,0:T(8,128)(2,1)S(1)}, f32[128,1,128]{2,1,0:T(1,128)S(1)}, f32[3,512,128]{2,1,0:T(8,128)}, f32[3,512,128]{2,1,0:T(8,128)}, f32[3,128,512]{2,1,0:T(8,128)}) custom-call(bf16[3,1024,512]{2,1,0:T(8,128)(2,1)S(1)} %get-tuple-element.53.u_ref, bf16[3,1024,512]{2,1,0:T(8,128)(2,1)S(1)} %get-tuple-element.54.dy_ref, ...), custom_call_target="tpu_custom_call" | custom-call | flops 4429185024 | bytes 12582912 | tf_op jit(solution)/shard_map/expert_backward/pallas_call | solution.py:596
  336.3 49.9 %return_home.1 = (bf16[96,512]{1,0:T(8,128)(2,1)S(1)}, f32[96,8]{1,0:T(8,128)S(1)}, f32[96,8]{1,0:T(8,128)S(1)}) custom-call(bf16[96,512]{1,0:T(8,128)(2,1)S(1)} %get-tuple-element.50.refs_0_.x_ref, s32[96,8]{1,0:T(8,128)S(1)} %copy-done.9, f32[96,8]{1,0:T(8,128)S(1)} %copy-done.11, bf16[128,24,512]{2,1,0:T(8,128)(2,1)S(1)} %get-tuple-element.56.rows_ref, ...), custom_call_target="tpu_custom_call" | custom-call | flops 30000001024 | bytes 6291456 | tf_op jit(solution)/shard_map/return_home/pallas_call | solution.py:482
  386.2 0.7 copy.22
  386.9 0.7 copy.23
  387.5 0.6 copy.26
  388.2 0.6 copy.27
  (10 shorter events, 0.0 us)
Async XLA Ops:
  4.9 0.9 copy-start.6
  5.8 0.7 copy-start.13
  6.5 48.5 %copy-start = (bf16[3,512,128]{2,1,0:T(8,128)(2,1)S(1)}, bf16[3,512,128]{2,1,0:T(8,128)(2,1)}, u32[]{:S(2)}) copy-start(bf16[3,512,128]{2,1,0:T(8,128)(2,1)} %w1_ref.5) | copy-start | bytes 1179652
  6.5 48.5 %copy-start.1 = (bf16[3,512,128]{2,1,0:T(8,128)(2,1)S(1)}, bf16[3,512,128]{2,1,0:T(8,128)(2,1)}, u32[]{:S(2)}) copy-start(bf16[3,512,128]{2,1,0:T(8,128)(2,1)} %w3_ref.5) | copy-start | bytes 1179652
  6.5 48.5 %copy-start.2 = (bf16[3,128,512]{2,1,0:T(8,128)(2,1)S(1)}, bf16[3,128,512]{2,1,0:T(8,128)(2,1)}, u32[]{:S(2)}) copy-start(bf16[3,128,512]{2,1,0:T(8,128)(2,1)} %w2_ref.5) | copy-start | bytes 1179652
  55.0 4.5 %copy-start.7 = (bf16[96,512]{1,0:T(8,128)(2,1)S(1)}, bf16[96,512]{1,0:T(8,128)(2,1)}, u32[]{:S(2)}) copy-start(bf16[96,512]{1,0:T(8,128)(2,1)} %refs_0_.5) | copy-start | bytes 294916
  55.0 4.5 %copy-start.8 = (bf16[96,512]{1,0:T(8,128)(2,1)S(1)}, bf16[96,512]{1,0:T(8,128)(2,1)}, u32[]{:S(2)}) copy-start(bf16[96,512]{1,0:T(8,128)(2,1)} %refs_2_.3) | copy-start | bytes 294916
  55.0 4.5 %copy-start.9 = (s32[96,8]{1,0:T(8,128)S(1)}, s32[96,8]{1,0:T(8,128)}, u32[]{:S(2)}) copy-start(s32[96,8]{1,0:T(8,128)} %get-tuple-element.43.refs_3_.row_ref) | copy-start | bytes 9220
  55.1 4.5 %copy-start.11 = (f32[96,8]{1,0:T(8,128)S(1)}, f32[96,8]{1,0:T(8,128)}, u32[]{:S(2)}) copy-start(f32[96,8]{1,0:T(8,128)} %get-tuple-element.44.refs_4_.gate_ref) | copy-start | bytes 9220
  134.0 37.4 %copy-start.3 = (bf16[3,512,128]{2,1,0:T(8,128)(2,1)S(1)}, bf16[3,512,128]{2,1,0:T(8,128)(2,1)}, u32[]{:S(2)}) copy-start(bf16[3,512,128]{2,1,0:T(8,128)(2,1)} %refs_7_.1) | copy-start | bytes 1179652
  134.0 37.4 %copy-start.4 = (bf16[3,512,128]{2,1,0:T(8,128)(2,1)S(1)}, bf16[3,512,128]{2,1,0:T(8,128)(2,1)}, u32[]{:S(2)}) copy-start(bf16[3,512,128]{2,1,0:T(8,128)(2,1)} %refs_8_.1) | copy-start | bytes 1179652
  134.0 37.4 %copy-start.5 = (bf16[3,128,512]{2,1,0:T(8,128)(2,1)S(1)}, bf16[3,128,512]{2,1,0:T(8,128)(2,1)}, u32[]{:S(2)}) copy-start(bf16[3,128,512]{2,1,0:T(8,128)(2,1)} %refs_9_.1) | copy-start | bytes 1179652
  171.5 10.3 %copy-start.10 = (s32[96,8]{1,0:T(8,128)S(1)}, s32[96,8]{1,0:T(8,128)}, u32[]{:S(2)}) copy-start(s32[96,8]{1,0:T(8,128)} %get-tuple-element.41.refs_3_.row_b_ref) | copy-start | bytes 9220
  171.5 10.3 %copy-start.12 = (f32[96,8]{1,0:T(8,128)S(1)}, f32[96,8]{1,0:T(8,128)}, u32[]{:S(2)}) copy-start(f32[96,8]{1,0:T(8,128)} %get-tuple-element.42.refs_4_) | copy-start | bytes 9220
